TPU v7x, 32 devices: a whole 2x2x4 slice. The times are simulated.
32 devices in a mesh: seq: 8 (over z, y), head: 4 (over x, core).
Axes of the slice: x: 2, y: 2, z: 4, core: 2. Of those that a mesh axis runs over, the one named last changes fastest.
Arguments:
- layer_in: bfloat16 [4096, 2048], P('seq', 'head'), may hold values from -6 to 6
- query_weight: bfloat16 [2048, 1024], P(None, 'head'), may hold values from -0.125 to 0.125
- key_weight: bfloat16 [2048, 1024], P(None, 'head'), may hold values from -0.125 to 0.125
- value_weight: bfloat16 [2048, 1024], P(None, 'head'), may hold values from -0.125 to 0.125
- gate_weight: bfloat16 [2048, 1024], P(None, 'head'), may hold values from -0.125 to 0.125
- beta_weight: bfloat16 [2048, 8], P(None, 'head'), may hold values from -0.125 to 0.125
- decay_weight: bfloat16 [2048, 8], P(None, 'head'), may hold values from -0.125 to 0.125
- conv_weight: float32 [4, 3, 1024], P(None, None, 'head'), may hold values from -3 to 3
- decay_log: float32 [8], P('head'), as said below
- beta_bias: float32 [8], P('head'), as said below
- decay_bias: float32 [8], P('head'), may hold values from -1 to 1
- norm_gain: float32 [128], replicated, may hold values from 0.1 to 1.9
- out_weight: bfloat16 [1024, 2048], P('head'), may hold values from -0.1875 to 0.1875
Outputs:
- layer_out: bfloat16 [4096, 2048], P('seq', 'head')
Inputs may be any that keep to these rules, and one draw needn't show every extreme that they name: decay_log lies between log(0.1 / 4096) and log(0.05). beta_bias lies between log(0.5 * 128 / 4096) and 1.
All inputs are finite; a program needn't handle non-finite values.
Results may differ from a plain program's by a relative error of at most 0.0049.
Values may be sent and summed in bfloat16 or wider, within the bound.
No kernel may reach another device: no remote copies, remote signals or barrier semaphores. Data moves between devices by JAX's collectives and lax.ppermute only.
A program may use at most 128 MiB of HBM per device.

v0:
```python
import jax
import jax.numpy as jnp
from jax import lax
from jax.sharding import PartitionSpec as P

BLOCK = 128


exact_mode = lax.Precision.HIGHEST
norm_floor = 0.0001


def passed_along(value, axis, steps):
    count = lax.axis_size(axis)
    leading, last = (max(0, -steps), min(count, count - steps))
    return lax.ppermute(value, axis, [(source, source + steps) for source in range(leading, last)])


def causal_conv(values, earlier, kernel):
    reach_back = kernel.shape[0] - 1
    tokens = values.shape[0]
    extended = jnp.concatenate([earlier, values], axis=0)
    summed = kernel[0] * values
    for offset in range(1, reach_back + 1):
        summed = (
            summed + kernel[offset] * extended[reach_back - offset : reach_back - offset + tokens]
        )
    return jax.nn.silu(summed)


def unit_rows(values):
    return values * lax.rsqrt(jnp.sum(values * values, axis=-1, keepdims=True) + 1.0)


def unit_lower_inverse(system):
    length = system.shape[-1]
    row_index = lax.broadcasted_iota(jnp.int32, (length, length), 0)
    col_index = lax.broadcasted_iota(jnp.int32, (length, length), 1)
    inverse = jnp.broadcast_to(jnp.eye(length, dtype=jnp.float32), system.shape)
    width = 1
    while width < length:
        same_pair = row_index // (2 * width) == col_index // (2 * width)
        lower_half = row_index // width > col_index // width
        linking = jnp.where(same_pair & lower_half, system, 0.0)
        middle = lax.optimization_barrier(
            jnp.einsum("...rs,...st->...rt", linking, inverse, precision=exact_mode)
        )
        update = lax.optimization_barrier(
            jnp.einsum("...rs,...st->...rt", inverse, middle, precision=exact_mode)
        )
        inverse = inverse - update
        width = width * 2
    return inverse


def block_terms(queries, key_rows, values, beta_gate, log_decay):
    length = log_decay.shape[-1]
    running = jnp.cumsum(log_decay, axis=-1)
    row_index = lax.broadcasted_iota(jnp.int32, (length, length), 0)
    col_index = lax.broadcasted_iota(jnp.int32, (length, length), 1)
    within = row_index >= col_index
    before = row_index > col_index
    spread = running[..., :, None] - running[..., None, :]
    decay_matrix = jnp.where(within, jnp.exp(jnp.minimum(spread, 0.0)), 0.0)
    key_gram = jnp.einsum("...rd,...sd->...rs", key_rows, key_rows, precision=exact_mode)
    lower_part = jnp.where(before, beta_gate[..., :, None] * decay_matrix * key_gram, 0.0)
    system = lower_part + jnp.eye(length, dtype=jnp.float32)
    growth = jnp.exp(running)
    right_side = jnp.concatenate(
        [beta_gate[..., None] * values, (beta_gate * growth)[..., None] * key_rows], axis=-1
    )
    solved = jnp.einsum(
        "...rs,...se->...re", unit_lower_inverse(system), right_side, precision=exact_mode
    )
    value_dim = values.shape[-1]
    fixed_rows = solved[..., :value_dim]
    erased = solved[..., value_dim:]
    query_key = jnp.einsum("...rd,...sd->...rs", queries, key_rows, precision=exact_mode)
    mixing = jnp.where(within, decay_matrix * query_key, 0.0)
    local_out = jnp.einsum("...rs,...se->...re", mixing, fixed_rows, precision=exact_mode)
    removed = lax.optimization_barrier(
        jnp.einsum("...rs,...sd->...rd", mixing, erased, precision=exact_mode)
    )
    reader = growth[..., None] * queries - removed
    tail_decay = jnp.exp(running[..., -1:] - running)
    weighted = tail_decay[..., None] * key_rows
    key_dim = key_rows.shape[-1]
    lost_part = lax.optimization_barrier(
        jnp.einsum("...bd,...be->...de", weighted, erased, precision=exact_mode)
    )
    transit = (
        jnp.exp(running[..., -1])[..., None, None] * jnp.eye(key_dim, dtype=jnp.float32) - lost_part
    )
    carried = jnp.einsum("...bd,...be->...de", weighted, fixed_rows, precision=exact_mode)
    return (local_out, reader, transit, carried)


def compose(earlier, later_map):
    joined = jnp.einsum("...de,...ef->...df", later_map[0], earlier[0], precision=exact_mode)
    moved = (
        jnp.einsum("...de,...ef->...df", later_map[0], earlier[1], precision=exact_mode)
        + later_map[1]
    )
    return (joined, moved)


def on_device(
    layer_in,
    query_weight,
    key_weight,
    value_weight,
    gate_weight,
    beta_weight,
    decay_weight,
    conv_weight,
    decay_log,
    beta_bias,
    decay_bias,
    norm_gain,
    out_weight,
):
    tokens = layer_in.shape[0]
    head_count = beta_weight.shape[1]
    head_dim = query_weight.shape[1] // head_count
    weights = (query_weight, key_weight, value_weight, gate_weight, beta_weight, decay_weight)
    shard_piece = lax.all_gather(layer_in, "head", axis=1, tiled=True)
    query_raw, key_raw, value_raw, gate_raw, beta_raw, decay_raw = tuple(
        (jnp.dot(shard_piece, weight, preferred_element_type=jnp.float32) for weight in weights)
    )
    reach_back = conv_weight.shape[0] - 1
    channels = query_raw.shape[1]
    last_rows = jnp.concatenate(
        [
            query_raw[tokens - reach_back :],
            key_raw[tokens - reach_back :],
            value_raw[tokens - reach_back :],
        ],
        axis=1,
    )
    prior_rows = passed_along(last_rows, "seq", 1)
    mixed_query = causal_conv(query_raw, prior_rows[:, :channels], conv_weight[:, 0])
    mixed_key = causal_conv(key_raw, prior_rows[:, channels : 2 * channels], conv_weight[:, 1])
    mixed_value = causal_conv(value_raw, prior_rows[:, 2 * channels :], conv_weight[:, 2])
    queries = unit_rows(mixed_query.reshape(tokens, head_count, head_dim))
    key_rows = unit_rows(mixed_key.reshape(tokens, head_count, head_dim))
    values = mixed_value.reshape(tokens, head_count, head_dim)
    beta_gate = jax.nn.sigmoid(beta_raw + beta_bias)
    log_decay = -jnp.exp(decay_log) * jax.nn.softplus(decay_raw + decay_bias)
    blocks = tokens // BLOCK

    def arrange(array):
        return array.reshape(blocks, BLOCK, head_count, head_dim).transpose(0, 2, 1, 3)

    def arrange_gate(array):
        return array.reshape(blocks, BLOCK, head_count).transpose(0, 2, 1)

    local_out, reader, transit, carried = block_terms(
        arrange(queries),
        arrange(key_rows),
        arrange(values),
        arrange_gate(beta_gate),
        arrange_gate(log_decay),
    )
    identity = jnp.broadcast_to(
        jnp.eye(head_dim, dtype=jnp.float32), (head_count, head_dim, head_dim)
    )
    nothing = jnp.zeros((head_count, head_dim, head_dim), jnp.float32)

    def through(running_pair, block_maps):
        return (compose(running_pair, block_maps), None)

    slab_pair, unused_rest = lax.scan(through, (identity, nothing), (transit, carried))
    slab_transit, slab_state = slab_pair
    stacked = jnp.stack([slab_transit, slab_state], axis=0)[None]
    every_map = lax.all_gather(stacked, "seq", axis=0, tiled=True)
    every_transit = every_map[:, 0]
    every_state = every_map[:, 1]
    position = lax.axis_index("seq")
    order = lax.broadcasted_iota(jnp.int32, (every_transit.shape[0], 1, 1, 1), 0)
    earlier_ones = order < position
    affine = (
        jnp.where(earlier_ones, every_transit, identity[None]),
        jnp.where(earlier_ones, every_state, 0.0),
    )
    while affine[0].shape[0] > 1:
        affine = compose((affine[0][0::2], affine[1][0::2]), (affine[0][1::2], affine[1][1::2]))
    incoming = affine[1][0]

    def advance(carry_state, block_maps):
        following = (
            jnp.einsum("hde,hef->hdf", block_maps[0], carry_state, precision=exact_mode)
            + block_maps[1]
        )
        return (following, carry_state)

    unused_last, starts = lax.scan(advance, incoming, (transit, carried))
    outputs = local_out + jnp.einsum("nhrd,nhde->nhre", reader, starts, precision=exact_mode)
    head_out = outputs.transpose(0, 2, 1, 3).reshape(tokens, head_count, head_dim)
    gate_rows = gate_raw.reshape(tokens, head_count, head_dim)
    scaled = head_out * lax.rsqrt(
        jnp.mean(head_out * head_out, axis=-1, keepdims=True) + norm_floor
    )
    hidden = (
        (scaled * norm_gain * jax.nn.silu(gate_rows))
        .reshape(tokens, head_count * head_dim)
        .astype(jnp.bfloat16)
    )
    column_weight = lax.all_to_all(out_weight, "head", split_axis=1, concat_axis=0, tiled=True)
    summed = jnp.dot(
        lax.all_gather(hidden, "head", axis=1, tiled=True),
        column_weight,
        preferred_element_type=jnp.float32,
    )
    return summed.astype(jnp.bfloat16)


def solution(mesh):
    return jax.shard_map(
        on_device,
        mesh=mesh,
        in_specs=(
            P("seq", "head"),
            P(None, "head"),
            P(None, "head"),
            P(None, "head"),
            P(None, "head"),
            P(None, "head"),
            P(None, "head"),
            P(None, None, "head"),
            P("head"),
            P("head"),
            P("head"),
            P(),
            P("head", None),
        ),
        out_specs=P("seq", "head"),
        check_vma=False,
    )
```

profile of v0, /device:TPU:0, one launch (start us, length us, event | category | flops | bytes accessed | tf_op | source)
XLA Modules:
  0.0 182.9 jit_solution(447879425216133817)
XLA Ops:
  8.7 1.5 fusion.147
  10.7 23.5 %all-gather.5.cloned.1.call-done = bf16[512,2048]{1,0:T(8,128)(2,1)} async-done(((bf16[512,512]{1,0:T(8,128)(2,1)}), bf16[512,2048]{1,0:T(8,128)(2,1)}) %all-gather.5.cloned.1.call-update) | async-done | bytes 2097168 | tf_op jit(solution)/shard_map/all_gather | solution.py:126
  34.2 2.4 %fusion.135 = f32[4,2,128]{2,1,0:T(2,128)S(1)} fusion(bf16[512,2048]{1,0:T(8,128)(2,1)} %all-gather.5.cloned.1.call-done, bf16[2048,2]{0,1:T(2,128)(2,1)} %param.23, f32[2]{0:T(128)} %param.27, f32[2]{0:T(128)} %exponential_negate_fusion), kind=kOutput, calls=%fused_computation.194 | convolution fusion | flops 4202496 | bytes 2109456 | tf_op jit(solution)/shard_map/dot_general | solution.py:128
  41.7 3.6 %collective-permute-start = (f32[3,768]{1,0:T(4,128)S(1)}, f32[3,768]{1,0:T(4,128)S(1)}, u32[]{:S(2)}, u32[]{:S(2)}) collective-permute-start(f32[3,768]{1,0:T(4,128)S(1)} %pad_maximum_fusion.4), channel_id=1, source_target_pairs={{0,4},{4,8},{8,12},{12,16},{16,20},{20,24},{24,28},{1,5},{5,9},{9,... | collective-permute-start | bytes 27656 | tf_op jit(solution)/shard_map/ppermute | solution.py:16
  46.5 2.2 %fusion.146 = (f32[512,256]{1,0:T(8,128)S(1)}, f32[512,256]{1,0:T(8,128)S(1)}) fusion(f32[512,256]{1,0:T(8,128)} %copy-done.7, f32[3,256]{1,0:T(4,128)S(1)} %get-tuple-element.120, f32[256]{0:T(256)} %bitcast.193, f32[256]{0:T(256)} %bitcast.194, f32[256]{0:T(256)} %bitcast.195, f32[256]{0:T(256)} %bitcast.196), kind=kLoop, calls=%fused_computation.241 | loop fusion | flops 1966080 | bytes 1580032 | tf_op jit(solution)/shard_map/mul | solution.py:32
  63.2 1.6 fusion.145
  65.3 2.2 %fusion.27 = f32[4,2,128,256]{3,2,1,0:T(8,128)S(1)} fusion(f32[4,2,128,128]{3,2,1,0:T(8,128)} %bitcast_multiply_fusion.3, f32[4,2,128,128]{3,2,1,0:T(8,128)S(1)} %bitcast_multiply_fusion.1, f32[4,2,128,128]{3,2,1,0:T(8,128)S(1)} %sub.166, f32[4,2,128,128]{3,2,1,0:T(8,128)} %fusion.157), kind=kOutput, calls=%fused_computation.42 | convolution fusion | flops 403046400 | bytes 3145728 | tf_op jit(solution)/shard_map/...rs,...se->...re/dot_general | solution.py:72
  67.5 2.1 %fusion.81 = f32[4,2,128,128]{3,2,1,0:T(8,128)} fusion(f32[4,2,128,256]{3,2,1,0:T(8,128)S(1)} %fusion.27, f32[4,128,2,128]{3,2,1,0:T(2,128)S(1)} %reshape.141, f32[4,2,128]{2,1,0:T(2,128)S(1)} %get-tuple-element.124, f32[4,128,2]{1,2,0:T(2,128)S(1)} %bitcast.179), kind=kOutput, calls=%fused_computation.117 | convolution fusion | flops 201588736 | bytes 1581056 | tf_op jit(solution)/shard_map/...bd,...be->...de/dot_general | solution.py:94
  71.0 6.0 %while.28 = (s32[]{:T(128)}, f32[2,128,128]{2,1,0:T(8,128)S(1)}, f32[2,128,128]{2,1,0:T(8,128)S(1)}, f32[4,2,128,128]{3,2,1,0:T(8,128)S(1)}, f32[4,2,128,128]{3,2,1,0:T(8,128)}) while((s32[]{:T(128)}, f32[2,128,128]{2,1,0:T(8,128)S(1)}, f32[2,128,128]{2,1,0:T(8,128)S(1)}, f32[4,2,128,128]{3,2,1,0:T(8,128)S(1)}, ...), condition=%wide.region_4.5_spmd.clone.clone, body=%wide.region_3.4_spmd.clone.sunk.clone | while | flops 100728832 | bytes 1443410 | solution.py:172
  77.9 2.1 %mul.279 = f32[512,2,128]{2,1,0:T(2,128)} reshape(f32[512,256]{1,0:T(8,128)} %get-tuple-element.101) | data formatting | bytes 1048576 | tf_op jit(solution)/shard_map/mul | solution.py:32
  80.0 2.4 %reduce_sum.27 = f32[512,2]{1,0:T(8,128)} reduce(f32[512,2,128]{2,1,0:T(2,128)} %mul.279, f32[]{:T(128)} %constant.223.clone.1), dimensions={2}, to_apply=%region_1.2 | reduce | flops 130048 | bytes 528388 | tf_op jit(solution)/shard_map/reduce_sum | solution.py:32
  82.4 1.7 add_rsqrt_fusion.1
  85.2 2.1 %reshape.140 = f32[4,128,2,128]{3,2,1,0:T(2,128)} reshape(f32[512,256]{1,0:T(8,128)} %get-tuple-element.102) | data formatting | bytes 1048576 | tf_op jit(solution)/shard_map/reshape | solution.py:144
  87.3 2.4 %fusion.17 = f32[4,2,128,128]{3,2,1,0:T(8,128)S(1)} fusion(f32[4,128,2,128]{3,2,1,0:T(2,128)} %reshape.140, f32[4,128,2,128]{3,2,1,0:T(2,128)S(1)} %reshape.141, f32[4,128,2]{1,2,0:T(2,128)S(1)} %bitcast.181, f32[4,128,2]{1,2,0:T(2,128)S(1)} %bitcast.182, f32[4,2,128]{2,1,0:T(2,128)S(1)} %reduce_window_sum.11, pred[128,128]{1,0:T(8,128)(4,1)S(1)} %get-tuple-element.137), kind=kOutput, calls=%fused_computation.25 | convolution fusion | flops 202244096 | bytes 1601536 | tf_op jit(solution)/shard_map/...rd,...sd->...rs/dot_general | solution.py:78
  91.2 1.8 fusion.87
  92.9 35.0 %all-gather.9.cloned.1.call-done = f32[16,2,128,128]{3,2,1,0:T(8,128)} async-done(((f32[2,2,128,128]{3,2,1,0:T(8,128)}), f32[16,2,128,128]{3,2,1,0:T(8,128)}) %all-gather.9.cloned.1.call-update) | async-done | bytes 2097168 | tf_op jit(solution)/shard_map/all_gather | solution.py:175
  127.9 1.8 %fusion.25 = (f32[8,2,128,128]{3,2,1,0:T(8,128)S(1)}, f32[8,2,128,128]{3,2,1,0:T(8,128)S(1)}) fusion(f32[8,2,2,128,128]{4,3,2,1,0:T(8,128)} %bitcast.173, pred[8]{0:T(512)(128)(4,1)S(1)} %iota_compare_fusion.3, f32[128,128]{1,0:T(8,128)S(1)} %fusion.133), kind=kLoop, calls=%fused_computation.39 | loop fusion | flops 524288 | bytes 4259848 | tf_op jit(solution)/shard_map/jit(_where)/select_n | solution.py:183
  132.0 7.5 %while.27 = (s32[]{:T(128)}, f32[2,128,128]{2,1,0:T(8,128)S(1)}, f32[4,2,128,128]{3,2,1,0:T(8,128)}, f32[4,2,128,128]{3,2,1,0:T(8,128)S(1)}, f32[4,2,128,128]{3,2,1,0:T(8,128)}) while((s32[]{:T(128)}, f32[2,128,128]{2,1,0:T(8,128)S(1)}, f32[4,2,128,128]{3,2,1,0:T(8,128)}, f32[4,2,128,128]{3,2,1,0:T(8,128)S(1)}, ...), condition=%wide.region_6.7_spmd.clone, body=%wide.region_5.6_spmd.sunk.clone | while | flops 50364416 | bytes 1049673 | solution.py:196
  139.6 3.8 %multiply_reduce_fusion = (f32[4,128,2]{1,2,0:T(2,128)S(1)}, f32[4,128,2,128]{1,3,2,0:T(8,128)}) fusion(f32[4,2,128,128]{2,3,1,0:T(8,128)} %fusion.87, f32[4,2,128,128]{3,2,1,0:T(8,128)} %get-tuple-element.62, f32[4,2,128,128]{3,2,1,0:T(8,128)} %fusion.84, f32[4,128,2,128]{3,2,1,0:T(2,128)} %reshape.140, f32[4,2,128]{2,1,0:T(2,128)S(1)} %get-tuple-element.122, ...), kind=kOutput, calls=%fused_computation.93 | convolution fusion | flops 202112000 | bytes 2633728 | tf_op jit(solution)/shard_map/nhrd,nhde->nhre/dot_general | solution.py:197
  143.5 2.0 %copy.104 = f32[4,128,2,128]{3,2,1,0:T(2,128)} copy(f32[4,128,2,128]{1,3,2,0:T(8,128)} %get-tuple-element.134) | data formatting | bytes 1048576 | tf_op jit(solution)/shard_map/add | solution.py:197
  146.2 2.8 %fusion.54 = bf16[512,256]{1,0:T(8,128)(2,1)} fusion(f32[64,8,2,128]{3,2,1,0:T(2,128)S(1)} %bitcast.175, f32[64,8,2,128]{3,2,1,0:T(2,128)} %bitcast.176, f32[256]{0:T(256)S(1)} %broadcast_bitcast_fusion, bf16[512,2048]{1,0:T(8,128)(2,1)S(1)} %copy-done.2, bf16[2048,256]{1,0:T(8,128)(2,1)} %param.21), kind=kOutput, calls=%fused_computation.76 | convolution fusion | flops 537919488 | bytes 4457472 | tf_op jit(solution)/shard_map/dot_general | solution.py:128
  149.0 1.5 copy.106
  150.5 22.6 %all_to_all.19 = bf16[256,4,512]{0,2,1:T(8,128)(2,1)S(1)} all-to-all(bf16[256,4,512]{0,2,1:T(8,128)(2,1)S(1)} %bitcast.172), channel_id=1, replica_groups=mesh['seq'=8,'head'=4] {'head'}, dimensions={1} | all-to-all | bytes 2097152 | tf_op jit(solution)/shard_map/all_to_all | solution.py:208
  173.6 2.7 %convolution_convert_fusion = bf16[512,512]{1,0:T(8,128)(2,1)} fusion(bf16[512,1024]{1,0:T(8,128)(2,1)} %all-gather.7.cloned.1.call-done, bf16[1024,512]{1,0:T(8,128)(2,1)S(1)} %bitcast.174), kind=kOutput, calls=%fused_computation.17 | convolution fusion | flops 537133056 | bytes 2621440 | tf_op jit(solution)/shard_map/dot_general | solution.py:209
  (152 shorter events, 44.9 us)
Async XLA Ops:
  6.5 31.6 %copy-start = (bf16[2048,256]{1,0:T(8,128)(2,1)S(1)}, bf16[2048,256]{1,0:T(8,128)(2,1)}, u32[]{:S(2)}) copy-start(bf16[2048,256]{1,0:T(8,128)(2,1)} %param.20) | copy-start | bytes 3145732
  6.5 27.7 %all-gather.5.cloned.1.call-start = ((), (), s32[]{:S(2)}) async-start(), calls=%async_computation.1 | async-start | bytes 2621440 | tf_op jit(solution)/shard_map/all_gather | solution.py:126
  7.3 120.7 %all-gather.9.cloned.1.call-start = ((), (), s32[]{:S(2)}) async-start(), calls=%async_computation.3 | async-start | bytes 2359296 | tf_op jit(solution)/shard_map/all_gather | solution.py:175
  34.2 3.9 %copy-start.1 = (bf16[512,2048]{1,0:T(8,128)(2,1)S(1)}, bf16[512,2048]{1,0:T(8,128)(2,1)}, u32[]{:S(2)}) copy-start(bf16[512,2048]{1,0:T(8,128)(2,1)} %all-gather.5.cloned.1.call-done) | copy-start | bytes 6291460
  38.2 1.2 copy-start.16
  38.9 2.8 %copy-start.3 = (f32[512,256]{1,0:T(8,128)}, f32[512,256]{1,0:T(8,128)S(1)}, u32[]{:S(2)}) copy-start(f32[512,256]{1,0:T(8,128)S(1)} %fusion.152) | copy-start | bytes 1572868
  38.9 2.0 %copy-start.17 = (bf16[2048,256]{1,0:T(8,128)(2,1)S(1)}, bf16[2048,256]{1,0:T(8,128)(2,1)}, u32[]{:S(2)}) copy-start(bf16[2048,256]{1,0:T(8,128)(2,1)} %param.18) | copy-start | bytes 3145732
  40.1 0.8 copy-start.7
  40.9 4.3 %copy-start.8 = (bf16[2048,2]{0,1:T(2,128)(2,1)S(1)}, bf16[2048,2]{0,1:T(2,128)(2,1)}, u32[]{:S(2)}) copy-start(bf16[2048,2]{0,1:T(2,128)(2,1)} %param.22) | copy-start | bytes 24580
  40.9 4.4 %copy-start.15 = (f32[2]{0:T(128)S(1)}, f32[2]{0:T(128)}, u32[]{:S(2)}) copy-start(f32[2]{0:T(128)} %param.26) | copy-start | bytes 28
  41.7 4.3 %copy-start.5 = (f32[512,256]{1,0:T(8,128)}, f32[512,256]{1,0:T(8,128)S(1)}, u32[]{:S(2)}) copy-start(f32[512,256]{1,0:T(8,128)S(1)} %fusion.150) | copy-start | bytes 1572868
  41.7 4.8 %collective-permute-start = (f32[3,768]{1,0:T(4,128)S(1)}, f32[3,768]{1,0:T(4,128)S(1)}, u32[]{:S(2)}, u32[]{:S(2)}) collective-permute-start(f32[3,768]{1,0:T(4,128)S(1)} %pad_maximum_fusion.4), channel_id=1, source_target_pairs={{0,4},{4,8},{8,12},{12,16},{16,20},{20,24},{24,28},{1,5},{5,9},{9,... | collective-permute-start | bytes 27656 | tf_op jit(solution)/shard_map/ppermute | solution.py:16
  59.6 3.5 %copy-start.4 = (f32[512,256]{1,0:T(8,128)S(1)}, f32[512,256]{1,0:T(8,128)}, u32[]{:S(2)}) copy-start(f32[512,256]{1,0:T(8,128)} %copy-done.3) | copy-start | bytes 1572868
  59.6 3.5 %copy-start.6 = (f32[512,256]{1,0:T(8,128)S(1)}, f32[512,256]{1,0:T(8,128)}, u32[]{:S(2)}) copy-start(f32[512,256]{1,0:T(8,128)} %copy-done.5) | copy-start | bytes 1572868
  59.6 3.5 %copy-start.9 = (f32[1,1,256]{2,0,1:T(1,128)S(1)}, f32[1,1,256]{2,0,1:T(1,128)}, u32[]{:S(2)}) copy-start(f32[1,1,256]{2,0,1:T(1,128)} %get-tuple-element.113) | copy-start | bytes 3076
  59.6 3.5 %copy-start.10 = (f32[1,1,256]{2,0,1:T(1,128)S(1)}, f32[1,1,256]{2,0,1:T(1,128)}, u32[]{:S(2)}) copy-start(f32[1,1,256]{2,0,1:T(1,128)} %get-tuple-element.114) | copy-start | bytes 3076
  59.6 3.5 %copy-start.11 = (f32[1,1,256]{2,0,1:T(1,128)S(1)}, f32[1,1,256]{2,0,1:T(1,128)}, u32[]{:S(2)}) copy-start(f32[1,1,256]{2,0,1:T(1,128)} %get-tuple-element.115) | copy-start | bytes 3076
  59.6 3.5 %copy-start.12 = (f32[1,1,256]{2,0,1:T(1,128)S(1)}, f32[1,1,256]{2,0,1:T(1,128)}, u32[]{:S(2)}) copy-start(f32[1,1,256]{2,0,1:T(1,128)} %get-tuple-element.116) | copy-start | bytes 3076
  59.6 3.5 %copy-start.13 = (f32[1,1,256]{2,0,1:T(1,128)S(1)}, f32[1,1,256]{2,0,1:T(1,128)}, u32[]{:S(2)}) copy-start(f32[1,1,256]{2,0,1:T(1,128)} %get-tuple-element.117) | copy-start | bytes 3076
  59.6 3.5 %copy-start.14 = (f32[1,1,256]{2,0,1:T(1,128)S(1)}, f32[1,1,256]{2,0,1:T(1,128)}, u32[]{:S(2)}) copy-start(f32[1,1,256]{2,0,1:T(1,128)} %get-tuple-element.118) | copy-start | bytes 3076
  71.0 6.9 %copy-start.18 = (f32[128]{0:T(128)S(1)}, f32[128]{0:T(128)}, u32[]{:S(2)}) copy-start(f32[128]{0:T(128)} %param.28) | copy-start | bytes 1540
  77.8 95.8 %all-gather.7.cloned.1.call-start = ((), (), s32[]{:S(2)}) async-start(), calls=%async_computation.2 | async-start | bytes 1310720 | tf_op jit(solution)/shard_map/all_gather | solution.py:210
  139.5 6.6 %copy-start.2 = (bf16[512,2048]{1,0:T(8,128)(2,1)S(1)}, bf16[512,2048]{1,0:T(8,128)(2,1)}, u32[]{:S(2)}) copy-start(bf16[512,2048]{1,0:T(8,128)(2,1)} %all-gather.5.cloned.1.call-done) | copy-start | bytes 6291460
Sparse Core Ops, SparseCore 0:
  8.9 25.2 all-gather.4
  78.0 49.9 all-gather.8
  149.1 21.0 all-gather.6
where the time goes:
time: 184 us; the launch traced here: 183 us
  waiting for transfers between devices  59.6 us (32%)
  matrix products  49.9 us (27%)
  blocking collectives  22.6 us (12%)
  local copies, waits for them, and re-layouts  17.1 us (9%)
  other arithmetic  15.9 us (9%)
  between operations  13.9 us (8%)
  starting transfers between devices  3.64 us (2%)
    all_gather x1, waiting for transfers between devices, on_device(): every_map = lax.all_gather(stacked, 'seq', axis=0, tiled=True)  35 us
    all_gather x1, waiting for transfers between devices, on_device(): shard_piece = lax.all_gather(layer_in, 'head', axis=1, tiled=True)  23.5 us
    all_to_all x1, blocking collectives, on_device(): lax.all_to_all(out_weight, 'head', split_axis=1, concat_axis=0, tiled=True)  22.6 us
    dot_general x6, matrix products, on_device(): jnp.dot(shard_piece, weight, preferred_element_type=jnp.float32)  8.02 us
    dot_general x7, matrix products, compose(): jnp.einsum('...de,...ef->...df', later_map[0], earlier[1], precision=exac...  6.03 us
    dot_general x7, matrix products, unit_lower_inverse(): jnp.einsum('...rs,...st->...rt', inverse, middle, precision=exact_mode)  5.27 us
    dot_general x7, matrix products, unit_lower_inverse(): jnp.einsum('...rs,...st->...rt', linking, inverse, precision=exact_mode)  4.78 us
    dot_general x4, matrix products, advance(): jnp.einsum('hde,hef->hdf', block_maps[0], carry_state, precision=exact_mode)  4.67 us
  transfers between devices with their start and end apart: 4, of which 3 were waited for; matrix products, arithmetic and copies ran while one was open for 12% of the time, Pallas kernels for 0%

commit v1 on v0

v1 whole, which is shorter than its diff:
```python
import functools

import jax
import jax.numpy as jnp
from jax import lax
from jax.experimental import pallas as pl
from jax.experimental.pallas import tpu as pltpu
from jax.sharding import PartitionSpec as P

BLOCK = 128
HALO = 8
norm_floor = 0.0001
f32 = jnp.float32
bf16 = jnp.bfloat16


def split(a):
    hi = a.astype(bf16)
    return hi, (a - hi.astype(f32)).astype(bf16)


def dot(a, b):
    return lax.dot_general(a, b, (((1,), (0,)), ((), ())), preferred_element_type=f32)


def dot_nt(a, b):
    return lax.dot_general(a, b, (((1,), (1,)), ((), ())), preferred_element_type=f32)


def mm_square(a, b):
    n = b[0].shape[1]
    right = jnp.concatenate([b[0], b[1]], axis=1)
    out = dot(jnp.concatenate([a[0], a[1]], axis=1), jnp.concatenate([right, right], axis=0))
    return out[:, :n] + out[:, n:]


def mm_wide(a, b):
    left = jnp.concatenate([a[0], a[1]], axis=1)
    return dot(left, jnp.concatenate([b[0], b[0]], axis=0)) + dot(a[0], b[1])


def mm_nt(a, b):
    left = jnp.concatenate([a[0], a[1]], axis=1)
    return dot_nt(left, jnp.concatenate([b[0], b[0]], axis=1)) + dot_nt(a[0], b[1])


def iotas(n):
    return (
        lax.broadcasted_iota(jnp.int32, (n, n), 0),
        lax.broadcasted_iota(jnp.int32, (n, n), 1),
    )


def project(pieces, weight_ref, index, rows, features):
    total = None
    for mask, piece in enumerate(pieces):
        start = pl.multiple_of((index ^ mask) * features, features)
        part = dot(piece(rows), weight_ref[pl.ds(start, features), :])
        total = part if total is None else total + part
    return total


def conv_rows(ext_ref, conv_ref, channel, taps, tokens):
    summed = None
    for s in range(taps):
        part = conv_ref[pl.ds(s * 3 + channel, 1), :] * ext_ref[pl.ds(HALO - s, tokens), :]
        summed = part if summed is None else summed + part
    return jax.nn.silu(summed)


def unit_heads(values, heads, dim):
    parts = []
    for h in range(heads):
        v = values[:, h * dim : (h + 1) * dim]
        parts.append(v * lax.rsqrt(jnp.sum(v * v, axis=-1, keepdims=True) + 1.0))
    return jnp.concatenate(parts, axis=1)


def decay_of(running, running_t, lane):
    row, col = iotas(BLOCK)
    spread = running[:, lane : lane + 1] - running_t[lane : lane + 1, :]
    return jnp.where(row >= col, jnp.exp(jnp.minimum(spread, 0.0)), 0.0)


def key_kernel(masks, chunks, heads, dim, taps, *refs):
    index = refs[0][0]
    x_refs = refs[1 : 1 + masks * chunks]
    refs = refs[1 + masks * chunks :]
    halo_refs = refs[:masks]
    key_w, value_w, gate_w, conv_ref, bias_ref, rate_ref = refs[masks : masks + 6]
    k_out, run_out, solved_out, prefix_out, slab_out, slab_low_out, ext = refs[masks + 6 :]
    tokens = k_out.shape[0]
    features = x_refs[0].shape[1]
    step = tokens // chunks
    pieces = [
        (lambda c, m=m: x_refs[m * chunks + c][...]) for m in range(masks)
    ]
    halos = [(lambda c, m=m: halo_refs[m][...]) for m in range(masks)]

    def mixed(weight, channel):
        ext[pl.ds(0, HALO), :] = project(halos, weight, index, 0, features)
        for c in range(chunks):
            ext[pl.ds(HALO + c * step, step), :] = project(pieces, weight, index, c, features)
        return conv_rows(ext, conv_ref, channel, taps, tokens)

    gates = jnp.concatenate(
        [project(pieces, gate_w, index, c, features) for c in range(chunks)], axis=0
    )
    z = gates + bias_ref[...]
    beta = jax.nn.sigmoid(z)
    log_decay = -rate_ref[...] * (jnp.maximum(z, 0.0) + jnp.log(1.0 + jnp.exp(-jnp.abs(z))))
    keys = unit_heads(mixed(key_w, 1), heads, dim)
    k_out[...] = keys
    values = mixed(value_w, 2)
    blocks = tokens // BLOCK
    row, col = iotas(BLOCK)
    triangle = jnp.where(row >= col, 1.0, 0.0).astype(f32)
    eye = jnp.where(row == col, 1.0, 0.0).astype(f32)
    units = [(b, h) for b in range(blocks) for h in range(heads)]
    running = []
    for b in range(blocks):
        r = lax.dot_general(
            triangle,
            log_decay[b * BLOCK : (b + 1) * BLOCK],
            (((1,), (0,)), ((), ())),
            preferred_element_type=f32,
            precision=lax.Precision.HIGHEST,
        )
        run_out[pl.ds(b * BLOCK, BLOCK), :] = r
        running.append(r)
    running_t = [jnp.transpose(r) for r in running]
    k_of = {}
    lower = {}
    inverse = {}
    for b, h in units:
        k = keys[b * BLOCK : (b + 1) * BLOCK, h * dim : (h + 1) * dim]
        k_of[b, h] = k
        pair = split(k)
        bcol = beta[b * BLOCK : (b + 1) * BLOCK, h : h + 1]
        gram = mm_nt(pair, pair)
        system = jnp.where(
            row > col, bcol * decay_of(running[b], running_t[b], heads + h) * gram, 0.0
        )
        lower[b, h] = system
        link = (row // 2 == col // 2) & (row > col)
        inverse[b, h] = eye - jnp.where(link, system, 0.0)
    width = 2
    while width < BLOCK:
        link = (row // (2 * width) == col // (2 * width)) & (row // width > col // width)
        middle = {}
        pairs = {}
        for u in units:
            pairs[u] = split(inverse[u])
            middle[u] = mm_square(split(jnp.where(link, lower[u], 0.0)), pairs[u])
        for u in units:
            inverse[u] = inverse[u] - mm_square(pairs[u], split(middle[u]))
        width *= 2
    maps = {}
    solved_pair = {}
    for b, h in units:
        k = k_of[b, h]
        bcol = beta[b * BLOCK : (b + 1) * BLOCK, h : h + 1]
        rcol = running[b][:, heads + h : heads + h + 1]
        v = values[b * BLOCK : (b + 1) * BLOCK, h * dim : (h + 1) * dim]
        right = jnp.concatenate([(bcol * jnp.exp(rcol)) * k, bcol * v], axis=1)
        solved = mm_wide(split(inverse[b, h]), split(right))
        solved_out[b * heads + h] = solved
        solved_pair[b, h] = split(solved)
    for b, h in units:
        rcol = running[b][:, heads + h : heads + h + 1]
        last = rcol[BLOCK - 1 : BLOCK, :]
        weighted = jnp.transpose(jnp.exp(last - rcol) * k_of[b, h])
        moved = mm_wide(split(weighted), solved_pair[b, h])
        transit = jnp.exp(last) * eye - moved[:, :dim]
        maps[b, h] = jnp.concatenate([transit, moved[:, dim:]], axis=1)

    def compose(later, earlier):
        out = mm_wide(split(later[:, :dim]), split(earlier))
        return jnp.concatenate([out[:, :dim], out[:, dim:] + later[:, dim:]], axis=1)

    for h in range(heads):
        prefix = {1: maps[0, h]}
        spans = {(b, 1): maps[b, h] for b in range(blocks)}

        def span(start, count):
            if (start, count) not in spans:
                half = 1
                while half * 2 < count:
                    half *= 2
                spans[start, count] = compose(
                    span(start + half, count - half), span(start, half)
                )
            return spans[start, count]

        for b in range(1, blocks):
            prefix_out[h * (blocks - 1) + b - 1] = span(0, b)
        slab = span(0, blocks)
        slab_out[h] = slab
        slab_low_out[h] = slab.astype(bf16)


def query_kernel(masks, chunks, heads, dim, taps, *refs):
    index = refs[0][0]
    x_refs = refs[1 : 1 + masks * chunks]
    refs = refs[1 + masks * chunks :]
    halo_refs = refs[:masks]
    query_w, gate_w, conv_ref, gain_ref = refs[masks : masks + 4]
    q_out, gate_out, ext = refs[masks + 4 :]
    tokens = q_out.shape[0]
    features = x_refs[0].shape[1]
    step = tokens // chunks
    pieces = [(lambda c, m=m: x_refs[m * chunks + c][...]) for m in range(masks)]
    halos = [(lambda c, m=m: halo_refs[m][...]) for m in range(masks)]
    ext[pl.ds(0, HALO), :] = project(halos, query_w, index, 0, features)
    for c in range(chunks):
        ext[pl.ds(HALO + c * step, step), :] = project(pieces, query_w, index, c, features)
        gate_out[pl.ds(c * step, step), :] = (
            jax.nn.silu(project(pieces, gate_w, index, c, features)) * gain_ref[...]
        )
    q_out[...] = unit_heads(conv_rows(ext, conv_ref, 0, taps, tokens), heads, dim)


def read_kernel(heads, dim, q_ref, k_ref, run_ref, solved_ref, prefix_ref, a_out, r_out):
    tokens = q_ref.shape[0]
    blocks = tokens // BLOCK
    units = [(b, h) for b in range(blocks) for h in range(heads)]
    running = [run_ref[pl.ds(b * BLOCK, BLOCK), :] for b in range(blocks)]
    running_t = [jnp.transpose(r) for r in running]
    mixing = {}
    for b, h in units:
        q = split(q_ref[pl.ds(b * BLOCK, BLOCK), pl.ds(h * dim, dim)])
        k = split(k_ref[pl.ds(b * BLOCK, BLOCK), pl.ds(h * dim, dim)])
        mixing[b, h] = decay_of(running[b], running_t[b], heads + h) * mm_nt(q, k)
    for b, h in units:
        rows, cols = pl.ds(b * BLOCK, BLOCK), pl.ds(h * dim, dim)
        out = mm_wide(split(mixing[b, h]), split(solved_ref[b * heads + h]))
        growth = jnp.exp(running[b][:, heads + h : heads + h + 1])
        reader = growth * q_ref[rows, cols] - out[:, :dim]
        local = out[:, dim:]
        if b > 0:
            moved = mm_wide(split(reader), split(prefix_ref[h * (blocks - 1) + b - 1]))
            reader = moved[:, :dim]
            local = local + moved[:, dim:]
        a_out[rows, cols] = local
        r_out[rows, cols] = reader


def step_kernel(heads, dim, first, distance, pos_ref, got_ref, *refs):
    if first:
        own_ref, before_out, own_out, low_out = refs
    else:
        before_ref, own_ref, before_out, own_out, low_out = refs
    valid = pos_ref[0] >= distance
    row = lax.broadcasted_iota(jnp.int32, (dim, 2 * dim), 0)
    col = lax.broadcasted_iota(jnp.int32, (dim, 2 * dim), 1)
    unchanged = jnp.where(row == col, 1.0, 0.0).astype(f32)
    for h in range(heads):
        got = jnp.where(valid, got_ref[h].astype(f32), unchanged)
        low = got.astype(bf16)
        low = jnp.concatenate([low, low], axis=0)

        def after(later):
            hi, lo = split(later[:, :dim])
            out = dot(jnp.concatenate([hi, lo], axis=1), low)
            return jnp.concatenate([out[:, :dim], out[:, dim:] + later[:, dim:]], axis=1)

        own = after(own_ref[h])
        own_out[h] = own
        low_out[h] = own.astype(bf16)
        before_out[h] = got if first else after(before_ref[h])


def hidden_kernel(heads, dim, a_ref, r_ref, gate_ref, before_ref, got_ref, out_ref):
    for h in range(heads):
        cols = pl.ds(h * dim, dim)
        before = before_ref[h]
        got = got_ref[h]
        hi, lo = split(before[:, :dim])
        state = before[:, dim:] + dot(
            jnp.concatenate([hi, lo], axis=1), jnp.concatenate([got, got], axis=0)
        )
        out = a_ref[:, cols] + mm_square(split(r_ref[:, cols]), split(state))
        scaled = out * lax.rsqrt(jnp.mean(out * out, axis=-1, keepdims=True) + norm_floor)
        out_ref[:, cols] = (scaled * gate_ref[:, cols]).astype(bf16)


def output_kernel(masks, *refs):
    out_ref = refs[2 * masks]
    total = None
    for m in range(masks):
        part = dot(refs[m][...], refs[masks + m][...])
        total = part if total is None else total + part
    out_ref[...] = total.astype(bf16)


def xor_permute(value, mask):
    count = lax.axis_size("head")
    return lax.ppermute(value, "head", [(i, i ^ mask) for i in range(count)])


def gather_chunks(parts, masks):
    pieces = {0: list(parts)}
    top = masks // 2
    order = []
    while top >= 1:
        order.append(top)
        top //= 2
    for bit in order:
        for mask in sorted(pieces):
            pieces[mask | bit] = [xor_permute(c, bit) for c in pieces[mask]]
    return [pieces[m] for m in range(masks)]


def vmem_call(kernel, out_shape, operands, scalars=0, scratch=(), flops=0):
    specs = [
        pl.BlockSpec(memory_space=pltpu.SMEM if i < scalars else pltpu.VMEM)
        for i in range(len(operands))
    ]
    outs = jax.tree.map(lambda _: pl.BlockSpec(memory_space=pltpu.VMEM), out_shape)
    return pl.pallas_call(
        kernel,
        out_shape=out_shape,
        in_specs=specs,
        out_specs=outs,
        scratch_shapes=list(scratch),
        cost_estimate=pl.CostEstimate(flops=flops, transcendentals=0, bytes_accessed=flops // 256),
    )(*operands)


def on_device(
    layer_in,
    query_weight,
    key_weight,
    value_weight,
    gate_weight,
    beta_weight,
    decay_weight,
    conv_weight,
    decay_log,
    beta_bias,
    decay_bias,
    norm_gain,
    out_weight,
):
    tokens, features = layer_in.shape
    heads = beta_weight.shape[1]
    channels = query_weight.shape[1]
    dim = channels // heads
    taps = conv_weight.shape[0]
    masks = lax.axis_size("head")
    slabs = lax.axis_size("seq")
    blocks = tokens // BLOCK
    chunks = 2
    head = lax.axis_index("head")
    position = lax.axis_index("seq")
    head_at = head.reshape(1).astype(jnp.int32)
    pos_at = position.reshape(1).astype(jnp.int32)

    step = tokens // chunks
    x_pieces = gather_chunks([layer_in[c * step : (c + 1) * step] for c in range(chunks)], masks)
    tail = layer_in[tokens - HALO :]
    halos = []
    for mask in range(masks):
        pairs = [
            (s * masks + h, (s + 1) * masks + (h ^ mask))
            for s in range(slabs - 1)
            for h in range(masks)
        ]
        halos.append(lax.ppermute(tail, ("seq", "head"), pairs))

    lanes = 128
    narrow = jnp.concatenate([beta_weight, decay_weight], axis=1)
    narrow = jnp.pad(narrow, ((0, 0), (0, lanes - 2 * heads)))
    bias = jnp.pad(jnp.concatenate([beta_bias, decay_bias]), (0, lanes - 2 * heads))[None]
    rate = jnp.pad(jnp.exp(decay_log), (heads, lanes - 2 * heads))[None]
    conv = conv_weight.reshape(taps * 3, channels)
    gain = jnp.tile(norm_gain, heads)[None]

    x_flat = [c for piece in x_pieces for c in piece]
    shape = jax.ShapeDtypeStruct
    ext = pltpu.VMEM((tokens + HALO, channels), f32)
    keys, running, solved, prefix, slab, slab_low = vmem_call(
        functools.partial(key_kernel, masks, chunks, heads, dim, taps),
        (
            shape((tokens, channels), f32),
            shape((tokens, lanes), f32),
            shape((blocks * heads, BLOCK, 2 * dim), f32),
            shape(((blocks - 1) * heads, dim, 2 * dim), f32),
            shape((heads, dim, 2 * dim), f32),
            shape((heads, dim, 2 * dim), bf16),
        ),
        [head_at, *x_flat, *halos, key_weight, value_weight, narrow, conv, bias, rate],
        scalars=1,
        scratch=(ext,),
        flops=10**10,
    )

    width = out_weight.shape[1] // masks
    sends = [
        lax.dynamic_slice(out_weight, (0, (head ^ m) * width), (channels, width))
        for m in range(masks)
    ]
    sends, _ = lax.optimization_barrier((sends, x_pieces[masks // 2]))
    columns = [sends[0]] + [xor_permute(sends[m], m) for m in range(1, masks)]

    x_late, _ = lax.optimization_barrier((x_flat, slab_low))
    queries, gates = vmem_call(
        functools.partial(query_kernel, masks, chunks, heads, dim, taps),
        (shape((tokens, channels), f32), shape((tokens, channels), f32)),
        [head_at, *x_late, *halos, query_weight, gate_weight, conv, gain],
        scalars=1,
        scratch=(ext,),
        flops=4 * 10**9,
    )

    def shifted(value, distance):
        pairs = [(s, s + distance) for s in range(slabs - distance)]
        return lax.ppermute(value, "seq", pairs)

    before = None
    distance = 1
    local = reader = None
    while 2 * distance < slabs:
        got = shifted(slab_low, distance)
        maps = (heads, dim, 2 * dim)
        operands = [pos_at, got] + ([] if before is None else [before]) + [slab]
        before, slab, slab_low = vmem_call(
            functools.partial(step_kernel, heads, dim, before is None, distance),
            (shape(maps, f32), shape(maps, f32), shape(maps, bf16)),
            operands,
            scalars=1,
            flops=10**8,
        )
        distance *= 2
    got = shifted(slab_low[:, :, dim:], distance)
    local, reader = vmem_call(
        functools.partial(read_kernel, heads, dim),
        (shape((tokens, channels), f32), shape((tokens, channels), f32)),
        [queries, keys, running, solved, prefix],
        flops=4 * 10**9,
    )
    hidden = vmem_call(
        functools.partial(hidden_kernel, heads, dim),
        shape((tokens, channels), bf16),
        [local, reader, gates, before, got],
        flops=10**8,
    )
    pieces = gather_chunks([hidden], masks)
    return vmem_call(
        functools.partial(output_kernel, masks),
        shape((tokens, width), bf16),
        [p[0] for p in pieces] + columns,
        flops=10**9,
    )


def solution(mesh):
    return jax.shard_map(
        on_device,
        mesh=mesh,
        in_specs=(
            P("seq", "head"),
            P(None, "head"),
            P(None, "head"),
            P(None, "head"),
            P(None, "head"),
            P(None, "head"),
            P(None, "head"),
            P(None, None, "head"),
            P("head"),
            P("head"),
            P("head"),
            P(),
            P("head", None),
        ),
        out_specs=P("seq", "head"),
        check_vma=False,
    )
```

time: 184 us -> 96.6 us (0.53)
  matrix products: 49.9 us -> 0 us
  waiting for transfers between devices: 59.6 us -> 15.9 us
  starting transfers between devices: 3.64 us -> 40.5 us
  Pallas kernels: 0 us -> 28.1 us
  blocking collectives: 22.6 us -> 0 us
  other arithmetic: 15.9 us -> 0.69 us
  between operations: 13.9 us -> 0.37 us
  local copies, waits for them, and re-layouts: 17.1 us -> 10.2 us
    all_gather x3 -> x0, waiting for transfers between devices: 58.5 us -> none  [the longest x1 35 us: on_device(): every_map = lax.all_gather(stacked, 'seq', axis=0, tiled=True)]
    dot_general x45 -> x0, matrix products: 49.6 us -> none  [the longest x6 8.02 us: on_device(): jnp.dot(shard_piece, weight, preferred_element_type=jnp.float32)]
    ppermute x1 -> x19, starting transfers between devices: 3.56 us -> 40.5 us  [the longest x3 16.6 us: shifted(): return lax.ppermute(value, 'seq', pairs)]
    pallas_call x0 -> x7, Pallas kernels: none -> 28.1 us  [vmem_call(): pl.pallas_call(kernel, out_shape=out_shape, in_specs=specs, out_specs=out...]
    all_to_all x1 -> x0, blocking collectives: 22.6 us -> none  [on_device(): lax.all_to_all(out_weight, 'head', split_axis=1, concat_axis=0, tiled=True)]
    ppermute x1 -> x19, waiting for transfers between devices: 0.4 us -> 15.9 us  [the longest x12 12.4 us: xor_permute(): return lax.ppermute(value, 'head', [(i, i ^ mask) for i in range(count)])]
    mul x4 -> x0, other arithmetic: 5.17 us -> none  [the longest x2 3.83 us: unit_rows(): values * values]
    reduce_sum x2 -> x0, other arithmetic: 2.99 us -> none  [unit_rows(): jnp.sum(values * values, axis=-1, keepdims=True) + 1.0]
  transfers between devices with their start and end apart: 4 -> 19, of which waited for: 3 -> 5; matrix products, arithmetic and copies ran while one was open for 12% -> 5% of each run, Pallas kernels for 0% -> 9%
where the time goes in v1:
time: 96.6 us; the launch traced here: 95.7 us
  starting transfers between devices  40.5 us (42%)
  Pallas kernels  28.1 us (29%)
  waiting for transfers between devices  15.9 us (16%)
  local copies, waits for them, and re-layouts  10.2 us (11%)
    pallas_call x7, Pallas kernels, vmem_call(): pl.pallas_call(kernel, out_shape=out_shape, in_specs=specs, out_specs=out...  28.1 us
    ppermute x3, starting transfers between devices, shifted(): return lax.ppermute(value, 'seq', pairs)  16.6 us
    ppermute x4, starting transfers between devices, on_device(): halos.append(lax.ppermute(tail, ('seq', 'head'), pairs))  14.9 us
    ppermute x12, waiting for transfers between devices, xor_permute(): return lax.ppermute(value, 'head', [(i, i ^ mask) for i in range(count)])  12.4 us
    ppermute x12, starting transfers between devices, xor_permute(): return lax.ppermute(value, 'head', [(i, i ^ mask) for i in range(count)])  8.99 us
    unnamed x61, local copies, waits for them, and re-layouts  4.41 us
    ppermute x3, waiting for transfers between devices, shifted(): return lax.ppermute(value, 'seq', pairs)  2.81 us
  transfers between devices with their start and end apart: 19, of which 5 were waited for; matrix products, arithmetic and copies ran while one was open for 5% of the time, Pallas kernels for 9%

profile of v1, /device:TPU:0, one launch (start us, length us, event | category | flops | bytes accessed | tf_op | source)
XLA Modules:
  0.0 95.7 jit_solution(7491932514518762687)
XLA Ops:
  0.0 1.1 %fusion.2 = (bf16[256,512]{1,0:T(8,128)(2,1)S(1)}, bf16[256,512]{1,0:T(8,128)(2,1)S(1)}) fusion(bf16[512,512]{1,0:T(8,128)(2,1)} %param.13), kind=kLoop, calls=%fused_computation.10 | loop fusion | bytes 1048576 | tf_op jit(solution)/shard_map/slice | solution.py:360
  1.1 3.0 %collective-permute-start.2 = (bf16[256,512]{1,0:T(8,128)(2,1)S(1)}, bf16[256,512]{1,0:T(8,128)(2,1)S(1)}, u32[]{:S(2)}, u32[]{:S(2)}) collective-permute-start(bf16[256,512]{1,0:T(8,128)(2,1)S(1)} %get-tuple-element.33.refs_1_), channel_id=1, source_target_pairs={{0,2},{1,3},{2,0},{3,1},{4,6},{5,7},{6,4},{7,5},{8,10},{9,11},{10,... | collective-permute-start | bytes 786440 | tf_op jit(solution)/shard_map/ppermute | solution.py:298
  4.9 4.0 %collective-permute-start.6 = (bf16[8,512]{1,0:T(8,128)(2,1)S(1)}, bf16[8,512]{1,0:T(8,128)(2,1)S(1)}, u32[]{:S(2)}, u32[]{:S(2)}) collective-permute-start(bf16[8,512]{1,0:T(8,128)(2,1)S(1)} %slice.14), channel_id=1, source_target_pairs={{0,4},{1,5},{2,6},{3,7},{4,8},{5,9},{6,10},{7,11},{8,12},{9,13},{1... | collective-permute-start | bytes 24584 | tf_op jit(solution)/shard_map/ppermute | solution.py:369
  8.9 2.0 %collective-permute-start.7 = (bf16[8,512]{1,0:T(8,128)(2,1)S(1)}, bf16[8,512]{1,0:T(8,128)(2,1)S(1)}, u32[]{:S(2)}, u32[]{:S(2)}) collective-permute-start(bf16[8,512]{1,0:T(8,128)(2,1)S(1)} %slice.14), channel_id=1, source_target_pairs={{0,5},{1,4},{2,7},{3,6},{4,9},{5,8},{6,11},{7,10},{8,13},{9,12},{1... | collective-permute-start | bytes 24584 | tf_op jit(solution)/shard_map/ppermute | solution.py:369
  10.9 1.6 %collective-permute-start = (bf16[256,512]{1,0:T(8,128)(2,1)S(1)}, bf16[256,512]{1,0:T(8,128)(2,1)S(1)}, u32[]{:S(2)}, u32[]{:S(2)}) collective-permute-start(bf16[256,512]{1,0:T(8,128)(2,1)S(1)} %get-tuple-element.33.refs_1_), channel_id=1, source_target_pairs={{0,1},{1,0},{2,3},{3,2},{4,5},{5,4},{6,7},{7,6},{8,9},{9,8},{10,11... | collective-permute-start | bytes 786440 | tf_op jit(solution)/shard_map/ppermute | solution.py:298
  12.6 5.6 %collective-permute-start.8 = (bf16[8,512]{1,0:T(8,128)(2,1)S(1)}, bf16[8,512]{1,0:T(8,128)(2,1)S(1)}, u32[]{:S(2)}, u32[]{:S(2)}) collective-permute-start(bf16[8,512]{1,0:T(8,128)(2,1)S(1)} %slice.14), channel_id=1, source_target_pairs={{0,6},{1,7},{2,4},{3,5},{4,10},{5,11},{6,8},{7,9},{8,14},{9,15},{1... | collective-permute-start | bytes 24584 | tf_op jit(solution)/shard_map/ppermute | solution.py:369
  19.6 3.3 %collective-permute-start.9 = (bf16[8,512]{1,0:T(8,128)(2,1)S(1)}, bf16[8,512]{1,0:T(8,128)(2,1)S(1)}, u32[]{:S(2)}, u32[]{:S(2)}) collective-permute-start(bf16[8,512]{1,0:T(8,128)(2,1)S(1)} %slice.14), channel_id=1, source_target_pairs={{0,7},{1,6},{2,5},{3,4},{4,11},{5,10},{6,9},{7,8},{8,15},{9,14},{1... | collective-permute-start | bytes 24584 | tf_op jit(solution)/shard_map/ppermute | solution.py:369
  24.6 0.9 pad.12.refs_15_
  26.5 9.5 %shard_map.127 = (f32[512,256]{1,0:T(8,128)}, f32[512,128]{1,0:T(8,128)}, f32[8,128,256]{2,1,0:T(8,128)}, f32[6,128,256]{2,1,0:T(8,128)}, f32[2,128,256]{2,1,0:T(8,128)}, /*index=5*/bf16[2,128,256]{2,1,0:T(8,128)(2,1)}) custom-call(s32[1]{0:T(128)} %bitcast.refs_0_, bf16[256,512]{1,0:T(8,128)(2,1)} %copy-done.3, bf16[256,512]{1,0:T(8,128)(2,1)} %copy-done.2, ...), custom_call_target="tpu_custom_call" | custom-call | flops 10000000000 | bytes 39062500 | tf_op jit(solution)/shard_map/pallas_call | solution.py:320
  36.0 4.4 %collective-permute-start.10 = (bf16[2,128,256]{2,1,0:T(8,128)(2,1)}, bf16[2,128,256]{2,1,0:T(8,128)(2,1)S(1)}, u32[]{:S(2)}, u32[]{:S(2)}) collective-permute-start(bf16[2,128,256]{2,1,0:T(8,128)(2,1)} %get-tuple-element.32), channel_id=1, source_target_pairs={{0,4},{4,8},{8,12},{12,16},{16,20},{20,24},{24,28},{1,5},{5,9},{9,... | collective-permute-start | bytes 393224 | tf_op jit(solution)/shard_map/ppermute | solution.py:418
  40.4 2.8 %collective-permute-done.10.got_ref = bf16[2,128,256]{2,1,0:T(8,128)(2,1)S(1)} collective-permute-done((bf16[2,128,256]{2,1,0:T(8,128)(2,1)}, bf16[2,128,256]{2,1,0:T(8,128)(2,1)S(1)}, u32[]{:S(2)}, u32[]{:S(2)}) %collective-permute-start.10) | collective-permute-done | bytes 131104 | tf_op jit(solution)/shard_map/ppermute | solution.py:418
  43.9 2.0 %shard_map.130 = (f32[2,128,256]{2,1,0:T(8,128)}, f32[2,128,256]{2,1,0:T(8,128)}, bf16[2,128,256]{2,1,0:T(8,128)(2,1)}) custom-call(s32[1]{0:T(128)} %bitcast.4.pos_ref, bf16[2,128,256]{2,1,0:T(8,128)(2,1)} %copy-done.4, f32[2,128,256]{2,1,0:T(8,128)} %get-tuple-element.49.refs_0_), custom_call_target="tpu_custom_call" | custom-call | flops 100000000 | bytes 390625 | tf_op jit(solution)/shard_map/pallas_call | solution.py:320
  45.8 7.7 %collective-permute-start.11 = (bf16[2,128,256]{2,1,0:T(8,128)(2,1)}, bf16[2,128,256]{2,1,0:T(8,128)(2,1)S(1)}, u32[]{:S(2)}, u32[]{:S(2)}) collective-permute-start(bf16[2,128,256]{2,1,0:T(8,128)(2,1)} %get-tuple-element.50), channel_id=1, source_target_pairs={{0,8},{4,12},{8,16},{12,20},{16,24},{20,28},{1,9},{5,13},{9,17},{1... | collective-permute-start | bytes 393224 | tf_op jit(solution)/shard_map/ppermute | solution.py:418
  54.1 4.7 %shard_map.128 = (f32[512,256]{1,0:T(8,128)}, f32[512,256]{1,0:T(8,128)}) custom-call(s32[1]{0:T(128)} %bitcast.refs_0_, bf16[256,512]{1,0:T(8,128)(2,1)} %copy-done.3, bf16[256,512]{1,0:T(8,128)(2,1)} %copy-done.2, bf16[256,512]{1,0:T(8,128)(2,1)} %copy-done.14, bf16[256,512]{1,0:T(8,128)(2,1)} %copy-done.15, bf16[256,512]{1,0:T(8,128)(2,1)} %copy-done.12, ...), custom_call_target="tpu_custom_call" | custom-call | flops 4000000000 | bytes 15625000 | tf_op jit(solution)/shard_map/pallas_call | solution.py:320
  59.5 2.2 %shard_map.131 = (f32[2,128,256]{2,1,0:T(8,128)}, f32[2,128,256]{2,1,0:T(8,128)}, bf16[2,128,256]{2,1,0:T(8,128)(2,1)}) custom-call(s32[1]{0:T(128)} %bitcast.4.pos_ref, bf16[2,128,256]{2,1,0:T(8,128)(2,1)} %copy-done.5, f32[2,128,256]{2,1,0:T(8,128)} %get-tuple-element.51.refs_0_, f32[2,128,256]{2,1,0:T(8,128)} %get-tuple-element.52.refs_1_), custom_call_target="tpu_custom_call" | custom-call | flops 100000000 | bytes 390625 | tf_op jit(solution)/shard_map/pallas_call | solution.py:320
  62.5 4.5 %collective-permute-start.12 = (bf16[2,128,128]{2,1,0:T(8,128)(2,1)S(1)}, bf16[2,128,128]{2,1,0:T(8,128)(2,1)S(1)}, u32[]{:S(2)}, u32[]{:S(2)}) collective-permute-start(bf16[2,128,128]{2,1,0:T(8,128)(2,1)S(1)} %slice.15), channel_id=1, source_target_pairs={{0,16},{4,20},{8,24},{12,28},{1,17},{5,21},{9,25},{13,29},{2,18},{... | collective-permute-start | bytes 196616 | tf_op jit(solution)/shard_map/ppermute | solution.py:418
  67.0 4.0 %shard_map.129 = (f32[512,256]{1,0:T(8,128)}, f32[512,256]{1,0:T(8,128)}) custom-call(f32[512,256]{1,0:T(8,128)} %get-tuple-element.41.q_ref, f32[512,256]{1,0:T(8,128)} %get-tuple-element.42.k_ref, f32[512,128]{1,0:T(8,128)} %get-tuple-element.43.run_ref, f32[8,128,256]{2,1,0:T(8,128)} %get-tuple-element.44.solved_ref, ...), custom_call_target="tpu_custom_call" | custom-call | flops 4000000000 | bytes 15625000 | tf_op jit(solution)/shard_map/pallas_call | solution.py:320
  71.6 2.8 %shard_map.132.refs_0_ = bf16[512,256]{1,0:T(8,128)(2,1)} custom-call(f32[512,256]{1,0:T(8,128)} %get-tuple-element.46.a_ref, f32[512,256]{1,0:T(8,128)} %get-tuple-element.47.r_ref, f32[512,256]{1,0:T(8,128)} %get-tuple-element.48.gate_ref, f32[2,128,256]{2,1,0:T(8,128)} %get-tuple-element.53.before_ref, bf16[2,128,128]{2,1,0:T(8,128)(2,1)} %copy-done.6), custom_call_target="tpu_custom_call" | custom-call | flops 100000000 | bytes 390625 | tf_op jit(solution)/shard_map/pallas_call | solution.py:320
  74.4 1.5 %collective-permute-start.14 = (bf16[512,256]{1,0:T(8,128)(2,1)}, bf16[512,256]{1,0:T(8,128)(2,1)S(1)}, u32[]{:S(2)}, u32[]{:S(2)}) collective-permute-start(bf16[512,256]{1,0:T(8,128)(2,1)} %shard_map.132.refs_0_), channel_id=1, source_target_pairs={{0,2},{1,3},{2,0},{3,1},{4,6},{5,7},{6,4},{7,5},{8,10},{9,11},{10,... | collective-permute-start | bytes 786440 | tf_op jit(solution)/shard_map/ppermute | solution.py:298
  77.2 1.3 %collective-permute-start.18 = (bf16[256,512]{1,0:T(8,128)(2,1)S(1)}, bf16[256,512]{1,0:T(8,128)(2,1)S(1)}, u32[]{:S(2)}, u32[]{:S(2)}) collective-permute-start(bf16[256,512]{1,0:T(8,128)(2,1)S(1)} %get-tuple-element.58), channel_id=1, source_target_pairs={{0,3},{1,2},{2,1},{3,0},{4,7},{5,6},{6,5},{7,4},{8,11},{9,10},{10,... | collective-permute-start | bytes 786440 | tf_op jit(solution)/shard_map/ppermute | solution.py:298
  78.8 3.4 %collective-permute-done.14.refs_2_ = bf16[512,256]{1,0:T(8,128)(2,1)S(1)} collective-permute-done((bf16[512,256]{1,0:T(8,128)(2,1)}, bf16[512,256]{1,0:T(8,128)(2,1)S(1)}, u32[]{:S(2)}, u32[]{:S(2)}) %collective-permute-start.14) | collective-permute-done | bytes 262176 | tf_op jit(solution)/shard_map/ppermute | solution.py:298
  82.2 5.5 %collective-permute-done.17.refs_6_ = bf16[256,512]{1,0:T(8,128)(2,1)S(1)} collective-permute-done((bf16[256,512]{1,0:T(8,128)(2,1)S(1)}, bf16[256,512]{1,0:T(8,128)(2,1)S(1)}, u32[]{:S(2)}, u32[]{:S(2)}) %collective-permute-start.17) | collective-permute-done | bytes 262176 | tf_op jit(solution)/shard_map/ppermute | solution.py:298
  87.8 3.4 %collective-permute-done.18.refs_7_ = bf16[256,512]{1,0:T(8,128)(2,1)S(1)} collective-permute-done((bf16[256,512]{1,0:T(8,128)(2,1)S(1)}, bf16[256,512]{1,0:T(8,128)(2,1)S(1)}, u32[]{:S(2)}, u32[]{:S(2)}) %collective-permute-start.18) | collective-permute-done | bytes 262176 | tf_op jit(solution)/shard_map/ppermute | solution.py:298
  92.7 3.0 %shard_map.133 = bf16[512,512]{1,0:T(8,128)(2,1)} custom-call(bf16[512,256]{1,0:T(8,128)(2,1)} %shard_map.132.refs_0_, bf16[512,256]{1,0:T(8,128)(2,1)} %copy-done.22, bf16[512,256]{1,0:T(8,128)(2,1)} %copy-done.17, bf16[512,256]{1,0:T(8,128)(2,1)} %copy-done.23, bf16[256,512]{1,0:T(8,128)(2,1)} %get-tuple-element.55.refs_4_, bf16[256,512]{1,0:T(8,128)(2,1)} %copy-done.19, ...), custom_call_target="tpu_custom_call" | custom-call | flops 1000000000 | bytes 3906250 | tf_op jit(solution)/shard_map/pallas_call | solution.py:320
  (93 shorter events, 11.2 us)
Async XLA Ops:
  1.1 23.5 %copy-start.2 = (bf16[256,512]{1,0:T(8,128)(2,1)}, bf16[256,512]{1,0:T(8,128)(2,1)S(1)}, u32[]{:S(2)}) copy-start(bf16[256,512]{1,0:T(8,128)(2,1)S(1)} %get-tuple-element.34.refs_2_) | copy-start | bytes 786436
  1.1 23.5 %copy-start.3 = (bf16[256,512]{1,0:T(8,128)(2,1)}, bf16[256,512]{1,0:T(8,128)(2,1)S(1)}, u32[]{:S(2)}) copy-start(bf16[256,512]{1,0:T(8,128)(2,1)S(1)} %get-tuple-element.33.refs_1_) | copy-start | bytes 786436
  1.1 17.1 %collective-permute-start.2 = (bf16[256,512]{1,0:T(8,128)(2,1)S(1)}, bf16[256,512]{1,0:T(8,128)(2,1)S(1)}, u32[]{:S(2)}, u32[]{:S(2)}) collective-permute-start(bf16[256,512]{1,0:T(8,128)(2,1)S(1)} %get-tuple-element.33.refs_1_), channel_id=1, source_target_pairs={{0,2},{1,3},{2,0},{3,1},{4,6},{5,7},{6,4},{7,5},{8,10},{9,11},{10,... | collective-permute-start | bytes 786440 | tf_op jit(solution)/shard_map/ppermute | solution.py:298
  4.1 14.7 %copy-start.8 = (bf16[2048,2]{0,1:T(2,128)(2,1)S(1)}, bf16[2048,2]{0,1:T(2,128)(2,1)}, u32[]{:S(2)}) copy-start(bf16[2048,2]{0,1:T(2,128)(2,1)} %param.19) | copy-start | bytes 24580
  4.1 14.7 %copy-start.9 = (bf16[2048,2]{0,1:T(2,128)(2,1)S(1)}, bf16[2048,2]{0,1:T(2,128)(2,1)}, u32[]{:S(2)}) copy-start(bf16[2048,2]{0,1:T(2,128)(2,1)} %param.18) | copy-start | bytes 24580
  4.1 14.2 %collective-permute-start.3 = (bf16[256,512]{1,0:T(8,128)(2,1)S(1)}, bf16[256,512]{1,0:T(8,128)(2,1)S(1)}, u32[]{:S(2)}, u32[]{:S(2)}) collective-permute-start(bf16[256,512]{1,0:T(8,128)(2,1)S(1)} %get-tuple-element.34.refs_2_), channel_id=1, source_target_pairs={{0,2},{1,3},{2,0},{3,1},{4,6},{5,7},{6,4},{7,5},{8,10},{9,11},{10,... | collective-permute-start | bytes 786440 | tf_op jit(solution)/shard_map/ppermute | solution.py:298
  4.9 14.0 %copy-start.28 = (f32[2]{0:T(128)S(1)}, f32[2]{0:T(128)}, u32[]{:S(2)}) copy-start(f32[2]{0:T(128)} %param.21) | copy-start | bytes 28
  4.9 7.6 %collective-permute-start.6 = (bf16[8,512]{1,0:T(8,128)(2,1)S(1)}, bf16[8,512]{1,0:T(8,128)(2,1)S(1)}, u32[]{:S(2)}, u32[]{:S(2)}) collective-permute-start(bf16[8,512]{1,0:T(8,128)(2,1)S(1)} %slice.14), channel_id=1, source_target_pairs={{0,4},{1,5},{2,6},{3,7},{4,8},{5,9},{6,10},{7,11},{8,12},{9,13},{1... | collective-permute-start | bytes 24584 | tf_op jit(solution)/shard_map/ppermute | solution.py:369
  8.9 3.7 %collective-permute-start.7 = (bf16[8,512]{1,0:T(8,128)(2,1)S(1)}, bf16[8,512]{1,0:T(8,128)(2,1)S(1)}, u32[]{:S(2)}, u32[]{:S(2)}) collective-permute-start(bf16[8,512]{1,0:T(8,128)(2,1)S(1)} %slice.14), channel_id=1, source_target_pairs={{0,5},{1,4},{2,7},{3,6},{4,9},{5,8},{6,11},{7,10},{8,13},{9,12},{1... | collective-permute-start | bytes 24584 | tf_op jit(solution)/shard_map/ppermute | solution.py:369
  10.9 14.6 %collective-permute-start = (bf16[256,512]{1,0:T(8,128)(2,1)S(1)}, bf16[256,512]{1,0:T(8,128)(2,1)S(1)}, u32[]{:S(2)}, u32[]{:S(2)}) collective-permute-start(bf16[256,512]{1,0:T(8,128)(2,1)S(1)} %get-tuple-element.33.refs_1_), channel_id=1, source_target_pairs={{0,1},{1,0},{2,3},{3,2},{4,5},{5,4},{6,7},{7,6},{8,9},{9,8},{10,11... | collective-permute-start | bytes 786440 | tf_op jit(solution)/shard_map/ppermute | solution.py:298
  12.5 13.0 %collective-permute-start.1 = (bf16[256,512]{1,0:T(8,128)(2,1)S(1)}, bf16[256,512]{1,0:T(8,128)(2,1)S(1)}, u32[]{:S(2)}, u32[]{:S(2)}) collective-permute-start(bf16[256,512]{1,0:T(8,128)(2,1)S(1)} %get-tuple-element.34.refs_2_), channel_id=1, source_target_pairs={{0,1},{1,0},{2,3},{3,2},{4,5},{5,4},{6,7},{7,6},{8,9},{9,8},{10,11... | collective-permute-start | bytes 786440 | tf_op jit(solution)/shard_map/ppermute | solution.py:298
  12.6 7.0 %collective-permute-start.8 = (bf16[8,512]{1,0:T(8,128)(2,1)S(1)}, bf16[8,512]{1,0:T(8,128)(2,1)S(1)}, u32[]{:S(2)}, u32[]{:S(2)}) collective-permute-start(bf16[8,512]{1,0:T(8,128)(2,1)S(1)} %slice.14), channel_id=1, source_target_pairs={{0,6},{1,7},{2,4},{3,5},{4,10},{5,11},{6,8},{7,9},{8,14},{9,15},{1... | collective-permute-start | bytes 24584 | tf_op jit(solution)/shard_map/ppermute | solution.py:369
  18.3 7.3 %collective-permute-start.4 = (bf16[256,512]{1,0:T(8,128)(2,1)S(1)}, bf16[256,512]{1,0:T(8,128)(2,1)S(1)}, u32[]{:S(2)}, u32[]{:S(2)}) collective-permute-start(bf16[256,512]{1,0:T(8,128)(2,1)S(1)} %collective-permute-done.2.refs_5_), channel_id=1, source_target_pairs={{0,1},{1,0},{2,3},{3,2},{4,5},{5,4},{6,7},{7,6},{8,9},{9,8},{10,11... | collective-permute-start | bytes 786440 | tf_op jit(solution)/shard_map/ppermute | solution.py:298
  18.4 7.2 %collective-permute-start.5 = (bf16[256,512]{1,0:T(8,128)(2,1)S(1)}, bf16[256,512]{1,0:T(8,128)(2,1)S(1)}, u32[]{:S(2)}, u32[]{:S(2)}) collective-permute-start(bf16[256,512]{1,0:T(8,128)(2,1)S(1)} %collective-permute-done.3.refs_6_), channel_id=1, source_target_pairs={{0,1},{1,0},{2,3},{3,2},{4,5},{5,4},{6,7},{7,6},{8,9},{9,8},{10,11... | collective-permute-start | bytes 786440 | tf_op jit(solution)/shard_map/ppermute | solution.py:298
  19.6 5.9 %collective-permute-start.9 = (bf16[8,512]{1,0:T(8,128)(2,1)S(1)}, bf16[8,512]{1,0:T(8,128)(2,1)S(1)}, u32[]{:S(2)}, u32[]{:S(2)}) collective-permute-start(bf16[8,512]{1,0:T(8,128)(2,1)S(1)} %slice.14), channel_id=1, source_target_pairs={{0,7},{1,6},{2,5},{3,4},{4,11},{5,10},{6,9},{7,8},{8,15},{9,14},{1... | collective-permute-start | bytes 24584 | tf_op jit(solution)/shard_map/ppermute | solution.py:369
  36.0 7.2 %collective-permute-start.10 = (bf16[2,128,256]{2,1,0:T(8,128)(2,1)}, bf16[2,128,256]{2,1,0:T(8,128)(2,1)S(1)}, u32[]{:S(2)}, u32[]{:S(2)}) collective-permute-start(bf16[2,128,256]{2,1,0:T(8,128)(2,1)} %get-tuple-element.32), channel_id=1, source_target_pairs={{0,4},{4,8},{8,12},{12,16},{16,20},{20,24},{24,28},{1,5},{5,9},{9,... | collective-permute-start | bytes 393224 | tf_op jit(solution)/shard_map/ppermute | solution.py:418
  45.8 13.0 %collective-permute-start.11 = (bf16[2,128,256]{2,1,0:T(8,128)(2,1)}, bf16[2,128,256]{2,1,0:T(8,128)(2,1)S(1)}, u32[]{:S(2)}, u32[]{:S(2)}) collective-permute-start(bf16[2,128,256]{2,1,0:T(8,128)(2,1)} %get-tuple-element.50), channel_id=1, source_target_pairs={{0,8},{4,12},{8,16},{12,20},{16,24},{20,28},{1,9},{5,13},{9,17},{1... | collective-permute-start | bytes 393224 | tf_op jit(solution)/shard_map/ppermute | solution.py:418
  62.5 8.4 %collective-permute-start.12 = (bf16[2,128,128]{2,1,0:T(8,128)(2,1)S(1)}, bf16[2,128,128]{2,1,0:T(8,128)(2,1)S(1)}, u32[]{:S(2)}, u32[]{:S(2)}) collective-permute-start(bf16[2,128,128]{2,1,0:T(8,128)(2,1)S(1)} %slice.15), channel_id=1, source_target_pairs={{0,16},{4,20},{8,24},{12,28},{1,17},{5,21},{9,25},{13,29},{2,18},{... | collective-permute-start | bytes 196616 | tf_op jit(solution)/shard_map/ppermute | solution.py:418
  74.4 7.8 %collective-permute-start.14 = (bf16[512,256]{1,0:T(8,128)(2,1)}, bf16[512,256]{1,0:T(8,128)(2,1)S(1)}, u32[]{:S(2)}, u32[]{:S(2)}) collective-permute-start(bf16[512,256]{1,0:T(8,128)(2,1)} %shard_map.132.refs_0_), channel_id=1, source_target_pairs={{0,2},{1,3},{2,0},{3,1},{4,6},{5,7},{6,4},{7,5},{8,10},{9,11},{10,... | collective-permute-start | bytes 786440 | tf_op jit(solution)/shard_map/ppermute | solution.py:298
  76.7 5.6 %collective-permute-start.16 = (bf16[256,512]{1,0:T(8,128)(2,1)S(1)}, bf16[256,512]{1,0:T(8,128)(2,1)S(1)}, u32[]{:S(2)}, u32[]{:S(2)}) collective-permute-start(bf16[256,512]{1,0:T(8,128)(2,1)S(1)} %get-tuple-element.56), channel_id=1, source_target_pairs={{0,1},{1,0},{2,3},{3,2},{4,5},{5,4},{6,7},{7,6},{8,9},{9,8},{10,11... | collective-permute-start | bytes 786440 | tf_op jit(solution)/shard_map/ppermute | solution.py:298
  76.7 11.1 %collective-permute-start.17 = (bf16[256,512]{1,0:T(8,128)(2,1)S(1)}, bf16[256,512]{1,0:T(8,128)(2,1)S(1)}, u32[]{:S(2)}, u32[]{:S(2)}) collective-permute-start(bf16[256,512]{1,0:T(8,128)(2,1)S(1)} %get-tuple-element.57), channel_id=1, source_target_pairs={{0,2},{1,3},{2,0},{3,1},{4,6},{5,7},{6,4},{7,5},{8,10},{9,11},{10,... | collective-permute-start | bytes 786440 | tf_op jit(solution)/shard_map/ppermute | solution.py:298
  77.2 14.0 %collective-permute-start.18 = (bf16[256,512]{1,0:T(8,128)(2,1)S(1)}, bf16[256,512]{1,0:T(8,128)(2,1)S(1)}, u32[]{:S(2)}, u32[]{:S(2)}) collective-permute-start(bf16[256,512]{1,0:T(8,128)(2,1)S(1)} %get-tuple-element.58), channel_id=1, source_target_pairs={{0,3},{1,2},{2,1},{3,0},{4,7},{5,6},{6,5},{7,4},{8,11},{9,10},{10,... | collective-permute-start | bytes 786440 | tf_op jit(solution)/shard_map/ppermute | solution.py:298
  78.5 12.7 %collective-permute-start.13 = (bf16[512,256]{1,0:T(8,128)(2,1)S(1)}, bf16[512,256]{1,0:T(8,128)(2,1)S(1)}, u32[]{:S(2)}, u32[]{:S(2)}) collective-permute-start(bf16[512,256]{1,0:T(8,128)(2,1)S(1)} %copy-done.1), channel_id=1, source_target_pairs={{0,1},{1,0},{2,3},{3,2},{4,5},{5,4},{6,7},{7,6},{8,9},{9,8},{10,11... | collective-permute-start | bytes 786440 | tf_op jit(solution)/shard_map/ppermute | solution.py:298
  82.2 9.0 %collective-permute-start.15 = (bf16[512,256]{1,0:T(8,128)(2,1)S(1)}, bf16[512,256]{1,0:T(8,128)(2,1)S(1)}, u32[]{:S(2)}, u32[]{:S(2)}) collective-permute-start(bf16[512,256]{1,0:T(8,128)(2,1)S(1)} %collective-permute-done.14.refs_2_), channel_id=1, source_target_pairs={{0,1},{1,0},{2,3},{3,2},{4,5},{5,4},{6,7},{7,6},{8,9},{9,8},{10,11... | collective-permute-start | bytes 786440 | tf_op jit(solution)/shard_map/ppermute | solution.py:298
  (25 other events, 98.4 us)

commit v2 on v1

v2 whole, which is shorter than its diff:
```python
import functools

import jax
import jax.numpy as jnp
from jax import lax
from jax.experimental import pallas as pl
from jax.experimental.pallas import tpu as pltpu
from jax.sharding import PartitionSpec as P

BLOCK = 128
HALO = 16
norm_floor = 0.0001
f32 = jnp.float32
bf16 = jnp.bfloat16


def split(a):
    hi = a.astype(bf16)
    return hi, (a - hi.astype(f32)).astype(bf16)


def dot(a, b):
    return lax.dot_general(a, b, (((1,), (0,)), ((), ())), preferred_element_type=f32)


def dot_nt(a, b):
    return lax.dot_general(a, b, (((1,), (1,)), ((), ())), preferred_element_type=f32)


def mm_square(a, b):
    n = b[0].shape[1]
    right = jnp.concatenate([b[0], b[1]], axis=1)
    out = dot(jnp.concatenate([a[0], a[1]], axis=1), jnp.concatenate([right, right], axis=0))
    return out[:, :n] + out[:, n:]


def mm_wide(a, b):
    left = jnp.concatenate([a[0], a[1]], axis=1)
    return dot(left, jnp.concatenate([b[0], b[0]], axis=0)) + dot(a[0], b[1])


def mm_nt(a, b):
    left = jnp.concatenate([a[0], a[1]], axis=1)
    return dot_nt(left, jnp.concatenate([b[0], b[0]], axis=1)) + dot_nt(a[0], b[1])


def iotas(n):
    return (
        lax.broadcasted_iota(jnp.int32, (n, n), 0),
        lax.broadcasted_iota(jnp.int32, (n, n), 1),
    )


def project(pieces, weight_ref, index, features):
    parts = []
    for chunk in range(len(pieces[0])):
        total = None
        for mask in range(len(pieces)):
            start = pl.multiple_of((index ^ mask) * features, features)
            part = dot(pieces[mask][chunk][...], weight_ref[pl.ds(start, features), :])
            total = part if total is None else total + part
        parts.append(total)
    return parts


def project_rows(pieces, weight_ref, index, features):
    parts = []
    for chunk in range(len(pieces[0])):
        total = None
        for mask in range(len(pieces)):
            start = pl.multiple_of((index ^ mask) * features, features)
            x = pieces[mask][chunk]
            x = x[pl.ds(HALO, x.shape[0] - HALO), :] if chunk == 0 else x[...]
            part = dot_nt(weight_ref[:, pl.ds(start, features)], x)
            total = part if total is None else total + part
        parts.append(total)
    return jnp.concatenate(parts, axis=1)


def conv_rows(ext_ref, raw, conv_ref, channel, taps, tokens):
    at = 0
    for part in raw:
        ext_ref[pl.ds(at, part.shape[0]), :] = part
        at += part.shape[0]
    summed = None
    for s in range(taps):
        part = conv_ref[channel, pl.ds(s, 1), :] * ext_ref[pl.ds(HALO - s, tokens), :]
        summed = part if summed is None else summed + part
    return jax.nn.silu(summed)


def unit_heads(values, heads, dim):
    parts = []
    for h in range(heads):
        v = values[:, h * dim : (h + 1) * dim]
        parts.append(v * lax.rsqrt(jnp.sum(v * v, axis=-1, keepdims=True) + 1.0))
    return jnp.concatenate(parts, axis=1)


def decay_of(running, running_t, unit):
    row, col = iotas(BLOCK)
    spread = running_t[:, unit : unit + 1] - running[unit : unit + 1, :]
    return jnp.where(row >= col, jnp.exp(jnp.minimum(spread, 0.0)), 0.0)


def take_pieces(refs, masks, chunks):
    return [[refs[m * chunks + c] for c in range(chunks)] for m in range(masks)]


def key_kernel(masks, chunks, heads, dim, taps, *refs):
    index = refs[0][0]
    decay_log, beta_bias, decay_bias = refs[1:4]
    refs = refs[4:]
    pieces = take_pieces(refs, masks, chunks)
    refs = refs[masks * chunks :]
    key_w, value_w, beta_w, decay_w, conv_ref = refs[:5]
    k_out, run_out, solved_out, prefix_out, slab_out, slab_low_out, ext = refs[5:]
    tokens = k_out.shape[0]
    features = pieces[0][0].shape[1]
    blocks = tokens // BLOCK
    units = [(b, h) for b in range(blocks) for h in range(heads)]
    row, col = iotas(BLOCK)
    eye = jnp.where(row == col, 1.0, 0.0).astype(f32)

    beta_raw = project_rows(pieces, beta_w, index, features)
    decay_raw = project_rows(pieces, decay_w, index, features)
    beta_rows, log_rows = [], []
    for h in range(heads):
        beta_rows.append(jax.nn.sigmoid(beta_raw[h : h + 1] + beta_bias[h]))
        z = decay_raw[h : h + 1] + decay_bias[h]
        soft = jnp.maximum(z, 0.0) + jnp.log(1.0 + jnp.exp(-jnp.abs(z)))
        log_rows.append(-jnp.exp(jnp.full_like(z, decay_log[h])) * soft)

    def by_unit(rows):
        return jnp.concatenate(
            [rows[h][:, b * BLOCK : (b + 1) * BLOCK] for b, h in units], axis=0
        )

    running = lax.dot_general(
        by_unit(log_rows),
        jnp.where(row <= col, 1.0, 0.0).astype(f32),
        (((1,), (0,)), ((), ())),
        preferred_element_type=f32,
        precision=lax.Precision.HIGHEST,
    )
    run_out[...] = running
    running_t = jnp.transpose(running)
    beta_t = jnp.transpose(by_unit(beta_rows))
    keys = unit_heads(
        conv_rows(ext, project(pieces, key_w, index, features), conv_ref, 1, taps, tokens),
        heads,
        dim,
    )
    k_out[...] = keys
    values = conv_rows(
        ext, project(pieces, value_w, index, features), conv_ref, 2, taps, tokens
    )
    k_of = {}
    lower = {}
    inverse = {}
    for b, h in units:
        k = keys[b * BLOCK : (b + 1) * BLOCK, h * dim : (h + 1) * dim]
        k_of[b, h] = k
        pair = split(k)
        unit = b * heads + h
        gram = mm_nt(pair, pair)
        system = jnp.where(
            row > col,
            beta_t[:, unit : unit + 1] * decay_of(running, running_t, unit) * gram,
            0.0,
        )
        lower[b, h] = system
        link = (row // 2 == col // 2) & (row > col)
        inverse[b, h] = eye - jnp.where(link, system, 0.0)
    width = 2
    while width < BLOCK:
        link = (row // (2 * width) == col // (2 * width)) & (row // width > col // width)
        middle = {}
        pairs = {}
        for u in units:
            pairs[u] = split(inverse[u])
            middle[u] = mm_square(split(jnp.where(link, lower[u], 0.0)), pairs[u])
        for u in units:
            inverse[u] = inverse[u] - mm_square(pairs[u], split(middle[u]))
        width *= 2
    maps = {}
    solved_pair = {}
    for b, h in units:
        k = k_of[b, h]
        unit = b * heads + h
        bcol = beta_t[:, unit : unit + 1]
        rcol = running_t[:, unit : unit + 1]
        v = values[b * BLOCK : (b + 1) * BLOCK, h * dim : (h + 1) * dim]
        right = jnp.concatenate([(bcol * jnp.exp(rcol)) * k, bcol * v], axis=1)
        solved = mm_wide(split(inverse[b, h]), split(right))
        solved_out[b * heads + h] = solved
        solved_pair[b, h] = split(solved)
    for b, h in units:
        rcol = running_t[:, b * heads + h : b * heads + h + 1]
        last = rcol[BLOCK - 1 : BLOCK, :]
        weighted = jnp.transpose(jnp.exp(last - rcol) * k_of[b, h])
        moved = mm_wide(split(weighted), solved_pair[b, h])
        transit = jnp.exp(last) * eye - moved[:, :dim]
        maps[b, h] = jnp.concatenate([transit, moved[:, dim:]], axis=1)

    def compose(later, earlier):
        out = mm_wide(split(later[:, :dim]), split(earlier))
        return jnp.concatenate([out[:, :dim], out[:, dim:] + later[:, dim:]], axis=1)

    for h in range(heads):
        spans = {(b, 1): maps[b, h] for b in range(blocks)}

        def span(start, count):
            if (start, count) not in spans:
                half = 1
                while half * 2 < count:
                    half *= 2
                spans[start, count] = compose(
                    span(start + half, count - half), span(start, half)
                )
            return spans[start, count]

        for b in range(1, blocks):
            prefix_out[h * (blocks - 1) + b - 1] = span(0, b)
        slab = span(0, blocks)
        slab_out[h] = slab
        slab_low_out[h] = slab.astype(bf16)


def query_kernel(masks, chunks, heads, dim, taps, *refs):
    index = refs[0][0]
    refs = refs[1:]
    pieces = take_pieces(refs, masks, chunks)
    query_w, gate_w, conv_ref, gain_ref = refs[masks * chunks : masks * chunks + 4]
    q_out, gate_out, ext = refs[masks * chunks + 4 :]
    tokens = q_out.shape[0]
    features = pieces[0][0].shape[1]
    raw = project(pieces, query_w, index, features)
    q_out[...] = unit_heads(conv_rows(ext, raw, conv_ref, 0, taps, tokens), heads, dim)
    gain = jnp.concatenate([gain_ref[...]] * heads, axis=1)
    at = 0
    for chunk, part in enumerate(project(pieces, gate_w, index, features)):
        part = part[HALO:] if chunk == 0 else part
        gate_out[pl.ds(at, part.shape[0]), :] = jax.nn.silu(part) * gain
        at += part.shape[0]


def read_kernel(heads, dim, q_ref, k_ref, run_ref, solved_ref, prefix_ref, a_out, r_out):
    tokens = q_ref.shape[0]
    blocks = tokens // BLOCK
    units = [(b, h) for b in range(blocks) for h in range(heads)]
    running = run_ref[...]
    running_t = jnp.transpose(running)
    mixing = {}
    for b, h in units:
        q = split(q_ref[pl.ds(b * BLOCK, BLOCK), pl.ds(h * dim, dim)])
        k = split(k_ref[pl.ds(b * BLOCK, BLOCK), pl.ds(h * dim, dim)])
        mixing[b, h] = decay_of(running, running_t, b * heads + h) * mm_nt(q, k)
    for b, h in units:
        rows, cols = pl.ds(b * BLOCK, BLOCK), pl.ds(h * dim, dim)
        out = mm_wide(split(mixing[b, h]), split(solved_ref[b * heads + h]))
        growth = jnp.exp(running_t[:, b * heads + h : b * heads + h + 1])
        reader = growth * q_ref[rows, cols] - out[:, :dim]
        local = out[:, dim:]
        if b > 0:
            moved = mm_wide(split(reader), split(prefix_ref[h * (blocks - 1) + b - 1]))
            reader = moved[:, :dim]
            local = local + moved[:, dim:]
        a_out[rows, cols] = local
        r_out[rows, cols] = reader


def step_kernel(heads, dim, first, distance, pos_ref, got_ref, *refs):
    if first:
        own_ref, before_out, own_out, low_out = refs
    else:
        before_ref, own_ref, before_out, own_out, low_out = refs
    valid = pos_ref[0] >= distance
    row = lax.broadcasted_iota(jnp.int32, (dim, 2 * dim), 0)
    col = lax.broadcasted_iota(jnp.int32, (dim, 2 * dim), 1)
    unchanged = jnp.where(row == col, 1.0, 0.0).astype(f32)
    for h in range(heads):
        got = jnp.where(valid, got_ref[h].astype(f32), unchanged)
        low = got.astype(bf16)
        low = jnp.concatenate([low, low], axis=0)

        def after(later):
            hi, lo = split(later[:, :dim])
            out = dot(jnp.concatenate([hi, lo], axis=1), low)
            return jnp.concatenate([out[:, :dim], out[:, dim:] + later[:, dim:]], axis=1)

        own = after(own_ref[h])
        own_out[h] = own
        low_out[h] = own.astype(bf16)
        before_out[h] = got if first else after(before_ref[h])


def hidden_kernel(heads, dim, a_ref, r_ref, gate_ref, before_ref, got_ref, out_ref):
    for h in range(heads):
        cols = pl.ds(h * dim, dim)
        before = before_ref[h]
        got = got_ref[h]
        hi, lo = split(before[:, :dim])
        state = before[:, dim:] + dot(
            jnp.concatenate([hi, lo], axis=1), jnp.concatenate([got, got], axis=0)
        )
        out = a_ref[:, cols] + mm_square(split(r_ref[:, cols]), split(state))
        scaled = out * lax.rsqrt(jnp.mean(out * out, axis=-1, keepdims=True) + norm_floor)
        out_ref[:, cols] = (scaled * gate_ref[:, cols]).astype(bf16)


def output_kernel(masks, *refs):
    out_ref = refs[2 * masks]
    total = None
    for m in range(masks):
        part = dot(refs[m][...], refs[masks + m][...])
        total = part if total is None else total + part
    out_ref[...] = total.astype(bf16)


def xor_permute(value, mask):
    count = lax.axis_size("head")
    return lax.ppermute(value, "head", [(i, i ^ mask) for i in range(count)])


def gather_chunks(parts, masks):
    order = []
    bit = masks // 2
    while bit >= 1:
        order.append(bit)
        bit //= 2
    pieces = {0: list(parts)}
    for bit in order:
        for mask in sorted(pieces):
            got = list(pieces[mask])
            for c in reversed(range(len(got))):
                got[c] = xor_permute(got[c], bit)
            pieces[mask | bit] = got
    return [pieces[m] for m in range(masks)]


def vmem_call(kernel, out_shape, operands, scalars=0, scratch=(), limit=16):
    specs = [
        pl.BlockSpec(memory_space=pltpu.SMEM if i < scalars else pltpu.VMEM)
        for i in range(len(operands))
    ]
    outs = jax.tree.map(lambda _: pl.BlockSpec(memory_space=pltpu.VMEM), out_shape)
    return pl.pallas_call(
        kernel,
        out_shape=out_shape,
        in_specs=specs,
        out_specs=outs,
        scratch_shapes=list(scratch),
        compiler_params=pltpu.CompilerParams(vmem_limit_bytes=limit * 2**20),
    )(*operands)


def on_device(
    layer_in,
    query_weight,
    key_weight,
    value_weight,
    gate_weight,
    beta_weight,
    decay_weight,
    conv_weight,
    decay_log,
    beta_bias,
    decay_bias,
    norm_gain,
    out_weight,
):
    tokens, _ = layer_in.shape
    heads = beta_weight.shape[1]
    channels = query_weight.shape[1]
    dim = channels // heads
    taps = conv_weight.shape[0]
    masks = lax.axis_size("head")
    slabs = lax.axis_size("seq")
    blocks = tokens // BLOCK
    head = lax.axis_index("head")
    head_at = head.reshape(1).astype(jnp.int32)
    pos_at = lax.axis_index("seq").reshape(1).astype(jnp.int32)

    def shifted(value, distance):
        pairs = [(s, s + distance) for s in range(slabs - distance)]
        return lax.ppermute(value, "seq", pairs)

    chunks = 2
    step = tokens // chunks
    halo = shifted(layer_in[tokens - HALO :], 1)
    first = jnp.concatenate([halo, layer_in[:step]], axis=0)
    x_pieces = gather_chunks([first, layer_in[step:]], masks)
    x_flat = [c for piece in x_pieces for c in piece]
    conv = conv_weight.transpose(1, 0, 2)
    gain = norm_gain[None]

    shape = jax.ShapeDtypeStruct
    ext = pltpu.VMEM((tokens + HALO, channels), f32)
    maps = (heads, dim, 2 * dim)
    rows = (tokens, channels)
    keys, running, solved, prefix, slab, slab_low = vmem_call(
        functools.partial(key_kernel, masks, chunks, heads, dim, taps),
        (
            shape(rows, f32),
            shape((blocks * heads, BLOCK), f32),
            shape((blocks * heads, BLOCK, 2 * dim), f32),
            shape(((blocks - 1) * heads, dim, 2 * dim), f32),
            shape(maps, f32),
            shape(maps, bf16),
        ),
        [head_at, decay_log, beta_bias, decay_bias, *x_flat]
        + [key_weight, value_weight, beta_weight.T, decay_weight.T, conv],
        scalars=4,
        scratch=(ext,),
        limit=24,
    )

    width = out_weight.shape[1] // masks
    sends = [
        lax.dynamic_slice(out_weight, (0, (head ^ m) * width), (channels, width))
        for m in range(masks)
    ]
    columns = [sends[0]]
    held, _ = lax.optimization_barrier((sends, x_pieces[masks // 2]))
    for m in range(1, masks):
        columns.append(xor_permute(held[m], m))

    x_late, _ = lax.optimization_barrier((x_flat, slab_low))
    queries, gates = vmem_call(
        functools.partial(query_kernel, masks, chunks, heads, dim, taps),
        (shape(rows, f32), shape(rows, f32)),
        [head_at, *x_late, query_weight, gate_weight, conv, gain],
        scalars=1,
        scratch=(ext,),
        limit=16,
    )

    before = None
    distance = 1
    while 2 * distance < slabs:
        got = shifted(slab_low, distance)
        operands = [pos_at, got] + ([] if before is None else [before]) + [slab]
        before, slab, slab_low = vmem_call(
            functools.partial(step_kernel, heads, dim, before is None, distance),
            (shape(maps, f32), shape(maps, f32), shape(maps, bf16)),
            operands,
            scalars=1,
            limit=8,
        )
        distance *= 2
    got = shifted(slab_low[:, :, dim:], distance)
    local, reader = vmem_call(
        functools.partial(read_kernel, heads, dim),
        (shape(rows, f32), shape(rows, f32)),
        [queries, keys, running, solved, prefix],
        limit=16,
    )
    hidden = vmem_call(
        functools.partial(hidden_kernel, heads, dim),
        shape(rows, bf16),
        [local, reader, gates, before, got],
        limit=8,
    )
    pieces = gather_chunks([hidden], masks)
    return vmem_call(
        functools.partial(output_kernel, masks),
        shape((tokens, width), bf16),
        [p[0] for p in pieces] + columns,
        limit=8,
    )


def solution(mesh):
    return jax.shard_map(
        on_device,
        mesh=mesh,
        in_specs=(
            P("seq", "head"),
            P(None, "head"),
            P(None, "head"),
            P(None, "head"),
            P(None, "head"),
            P(None, "head"),
            P(None, "head"),
            P(None, None, "head"),
            P("head"),
            P("head"),
            P("head"),
            P(),
            P("head", None),
        ),
        out_specs=P("seq", "head"),
        check_vma=False,
    )
```

time: 96.6 us -> 81.3 us (0.84)
  waiting for transfers between devices: 15.9 us -> 30.7 us
  Pallas kernels: 28.1 us -> 14.3 us
  starting transfers between devices: 40.5 us -> 27.5 us
  local copies, waits for them, and re-layouts: 10.2 us -> 7.87 us
    ppermute x4 -> x0, starting transfers between devices: 14.9 us -> none  [on_device(): halos.append(lax.ppermute(tail, ('seq', 'head'), pairs))]
    pallas_call x7, Pallas kernels: 28.1 us -> 14.3 us  [vmem_call(): pl.pallas_call(kernel, out_shape=out_shape, in_specs=specs, out_specs=out...]
    ppermute x12, waiting for transfers between devices: 12.4 us -> 25.1 us  [xor_permute(): return lax.ppermute(value, 'head', [(i, i ^ mask) for i in range(count)])]
    ppermute x3 -> x4, starting transfers between devices: 16.6 us -> 21 us  [shifted(): return lax.ppermute(value, 'seq', pairs)]
    ppermute x3 -> x4, waiting for transfers between devices: 2.81 us -> 5.56 us  [shifted(): return lax.ppermute(value, 'seq', pairs)]
    ppermute x12, starting transfers between devices: 8.99 us -> 6.44 us  [xor_permute(): return lax.ppermute(value, 'head', [(i, i ^ mask) for i in range(count)])]
    unnamed x61 -> x36, local copies, waits for them, and re-layouts: 4.41 us -> 5.89 us
  transfers between devices with their start and end apart: 19 -> 16, of which waited for: 5 -> 9; matrix products, arithmetic and copies ran while one was open for 5% -> 1% of each run, Pallas kernels for 9% -> 3%
where the time goes in v2:
time: 81.3 us; the launch traced here: 80.6 us
  waiting for transfers between devices  30.7 us (38%)
  starting transfers between devices  27.5 us (34%)
  Pallas kernels  14.3 us (18%)
  local copies, waits for them, and re-layouts  7.87 us (10%)
    ppermute x12, waiting for transfers between devices, xor_permute(): return lax.ppermute(value, 'head', [(i, i ^ mask) for i in range(count)])  25.1 us
    ppermute x4, starting transfers between devices, shifted(): return lax.ppermute(value, 'seq', pairs)  21 us
    pallas_call x7, Pallas kernels, vmem_call(): pl.pallas_call(kernel, out_shape=out_shape, in_specs=specs, out_specs=out...  14.3 us
    ppermute x12, starting transfers between devices, xor_permute(): return lax.ppermute(value, 'head', [(i, i ^ mask) for i in range(count)])  6.44 us
    unnamed x36, local copies, waits for them, and re-layouts  5.89 us
    ppermute x4, waiting for transfers between devices, shifted(): return lax.ppermute(value, 'seq', pairs)  5.56 us
  transfers between devices with their start and end apart: 16, of which 9 were waited for; matrix products, arithmetic and copies ran while one was open for 1% of the time, Pallas kernels for 3%

profile of v2, /device:TPU:0, one launch (start us, length us, event | category | flops | bytes accessed | tf_op | source)
XLA Modules:
  0.0 80.6 jit_solution(9828862414525030850)
XLA Ops:
  0.8 4.9 %collective-permute-start = (bf16[16,512]{1,0:T(8,128)(2,1)S(1)}, bf16[16,512]{1,0:T(8,128)(2,1)S(1)}, u32[]{:S(2)}, u32[]{:S(2)}) collective-permute-start(bf16[16,512]{1,0:T(8,128)(2,1)S(1)} %slice.12), channel_id=1, source_target_pairs={{0,4},{4,8},{8,12},{12,16},{16,20},{20,24},{24,28},{1,5},{5,9},{9,... | collective-permute-start | bytes 49160 | tf_op jit(solution)/shard_map/ppermute | solution.py:387
  5.7 1.1 %fusion = (bf16[256,512]{1,0:T(8,128)(2,1)S(1)}, bf16[256,512]{1,0:T(8,128)(2,1)S(1)}) fusion(bf16[512,512]{1,0:T(8,128)(2,1)} %param.13), kind=kLoop, calls=%fused_computation.5 | loop fusion | bytes 1048576 | tf_op jit(solution)/shard_map/slice | solution.py:393
  7.2 1.6 %collective-permute-start.3 = (bf16[272,512]{1,0:T(8,128)(2,1)S(1)}, bf16[272,512]{1,0:T(8,128)(2,1)S(1)}, u32[]{:S(2)}, u32[]{:S(2)}) collective-permute-start(bf16[272,512]{1,0:T(8,128)(2,1)S(1)} %pad_maximum_fusion.refs_4_.refs_1_), channel_id=1, source_target_pairs={{0,2},{1,3},{2,0},{3,1},{4,6},{5,7},{6,4},{7,5},{8,10},{9,11},{10,... | collective-permute-start | bytes 835592 | tf_op jit(solution)/shard_map/ppermute | solution.py:323
  9.3 7.5 %collective-permute-done.3.refs_8_.refs_5_ = bf16[272,512]{1,0:T(8,128)(2,1)S(1)} collective-permute-done((bf16[272,512]{1,0:T(8,128)(2,1)S(1)}, bf16[272,512]{1,0:T(8,128)(2,1)S(1)}, u32[]{:S(2)}, u32[]{:S(2)}) %collective-permute-start.3) | collective-permute-done | bytes 278560 | tf_op jit(solution)/shard_map/ppermute | solution.py:323
  17.3 3.4 %collective-permute-done.4.refs_9_.refs_6_ = bf16[256,512]{1,0:T(8,128)(2,1)S(1)} collective-permute-done((bf16[256,512]{1,0:T(8,128)(2,1)S(1)}, bf16[256,512]{1,0:T(8,128)(2,1)S(1)}, u32[]{:S(2)}, u32[]{:S(2)}) %collective-permute-start.4) | collective-permute-done | bytes 262176 | tf_op jit(solution)/shard_map/ppermute | solution.py:323
  20.7 1.5 %collective-permute-done.6.refs_11_.refs_8_ = bf16[256,512]{1,0:T(8,128)(2,1)S(1)} collective-permute-done((bf16[256,512]{1,0:T(8,128)(2,1)S(1)}, bf16[256,512]{1,0:T(8,128)(2,1)S(1)}, u32[]{:S(2)}, u32[]{:S(2)}) %collective-permute-start.6) | collective-permute-done | bytes 262176 | tf_op jit(solution)/shard_map/ppermute | solution.py:323
  22.9 1.2 %copy-done.1 = bf16[2048,256]{1,0:T(8,128)(2,1)S(1)} copy-done((bf16[2048,256]{1,0:T(8,128)(2,1)S(1)}, bf16[2048,256]{1,0:T(8,128)(2,1)}, u32[]{:S(2)}) %copy-start.1) | copy-done | bytes 1048600
  24.1 7.6 %shard_map.127 = (f32[512,256]{1,0:T(8,128)S(1)}, f32[8,128]{1,0:T(8,128)S(1)}, f32[8,128,256]{2,1,0:T(8,128)S(1)}, f32[6,128,256]{2,1,0:T(8,128)S(1)}, f32[2,12...) custom-call(s32[1]{0:T(128)} %bitcast.refs_0_, f32[2]{0:T(128)S(1)} %copy-done.13, f32[2]{0:T(128)S(1)} %copy-done.14, ...), custom_call_target="tpu_custom_call" | custom-call | tf_op jit(solution)/shard_map/pallas_call | solution.py:348
  31.7 1.0 %copy-done.2 = f32[8,128,256]{2,1,0:T(8,128)} copy-done((f32[8,128,256]{2,1,0:T(8,128)}, f32[8,128,256]{2,1,0:T(8,128)S(1)}, u32[]{:S(2)}) %copy-start.2) | copy-done | bytes 1048600
  34.4 4.4 %collective-permute-start.7 = (bf16[2,128,256]{2,1,0:T(8,128)(2,1)}, bf16[2,128,256]{2,1,0:T(8,128)(2,1)}, u32[]{:S(2)}, u32[]{:S(2)}) collective-permute-start(bf16[2,128,256]{2,1,0:T(8,128)(2,1)} %get-tuple-element.31), channel_id=1, source_target_pairs={{0,4},{4,8},{8,12},{12,16},{16,20},{20,24},{24,28},{1,5},{5,9},{9,... | collective-permute-start | bytes 393224 | tf_op jit(solution)/shard_map/ppermute | solution.py:387
  38.8 2.7 %collective-permute-done.7.got_ref = bf16[2,128,256]{2,1,0:T(8,128)(2,1)} collective-permute-done((bf16[2,128,256]{2,1,0:T(8,128)(2,1)}, bf16[2,128,256]{2,1,0:T(8,128)(2,1)}, u32[]{:S(2)}, u32[]{:S(2)}) %collective-permute-start.7) | collective-permute-done | bytes 131104 | tf_op jit(solution)/shard_map/ppermute | solution.py:387
  41.5 1.1 %shard_map.130 = (f32[2,128,256]{2,1,0:T(8,128)S(1)}, f32[2,128,256]{2,1,0:T(8,128)S(1)}, bf16[2,128,256]{2,1,0:T(8,128)(2,1)S(1)}) custom-call(s32[1]{0:T(128)} %bitcast.5.pos_ref, bf16[2,128,256]{2,1,0:T(8,128)(2,1)} %collective-permute-done.7.got_ref, f32[2,128,256]{2,1,0:T(8,128)S(1)} %get-tuple-element.48.refs_0_), custom_call_target="tpu_custom_call" | custom-call | tf_op jit(solution)/shard_map/pallas_call | solution.py:348
  42.6 6.2 %collective-permute-start.8 = (bf16[2,128,256]{2,1,0:T(8,128)(2,1)S(1)}, bf16[2,128,256]{2,1,0:T(8,128)(2,1)S(1)}, u32[]{:S(2)}, u32[]{:S(2)}) collective-permute-start(bf16[2,128,256]{2,1,0:T(8,128)(2,1)S(1)} %get-tuple-element.49), channel_id=1, source_target_pairs={{0,8},{4,12},{8,16},{12,20},{16,24},{20,28},{1,9},{5,13},{9,17},{1... | collective-permute-start | bytes 393224 | tf_op jit(solution)/shard_map/ppermute | solution.py:387
  48.9 2.5 %collective-permute-done.8.got_ref = bf16[2,128,256]{2,1,0:T(8,128)(2,1)S(1)} collective-permute-done((bf16[2,128,256]{2,1,0:T(8,128)(2,1)S(1)}, bf16[2,128,256]{2,1,0:T(8,128)(2,1)S(1)}, u32[]{:S(2)}, u32[]{:S(2)}) %collective-permute-start.8) | collective-permute-done | bytes 131104 | tf_op jit(solution)/shard_map/ppermute | solution.py:387
  52.3 5.5 %collective-permute-start.9 = (bf16[2,128,128]{2,1,0:T(8,128)(2,1)S(1)}, bf16[2,128,128]{2,1,0:T(8,128)(2,1)S(1)}, u32[]{:S(2)}, u32[]{:S(2)}) collective-permute-start(bf16[2,128,128]{2,1,0:T(8,128)(2,1)S(1)} %slice.15), channel_id=1, source_target_pairs={{0,16},{4,20},{8,24},{12,28},{1,17},{5,21},{9,25},{13,29},{2,18},{... | collective-permute-start | bytes 196616 | tf_op jit(solution)/shard_map/ppermute | solution.py:387
  57.8 1.2 %copy-done.5 = bf16[2048,256]{1,0:T(8,128)(2,1)S(1)} copy-done((bf16[2048,256]{1,0:T(8,128)(2,1)S(1)}, bf16[2048,256]{1,0:T(8,128)(2,1)}, u32[]{:S(2)}) %copy-start.5) | copy-done | bytes 1048600
  59.1 1.4 %shard_map.128 = (f32[512,256]{1,0:T(8,128)S(1)}, f32[512,256]{1,0:T(8,128)S(1)}) custom-call(s32[1]{0:T(128)} %bitcast.refs_0_, bf16[272,512]{1,0:T(8,128)(2,1)S(1)} %pad_maximum_fusion.refs_4_.refs_1_, bf16[256,512]{1,0:T(8,128)(2,1)S(1)} %get-tuple-element.33.refs_5_.refs_2_, bf16[272,512]{1,0:T(8,128)(2,1)S(1)} %collective-permute-done.1.refs_6_.refs_3_, ...), custom_call_target="tpu_custom_call" | custom-call | tf_op jit(solution)/shard_map/pallas_call | solution.py:348
  60.6 1.2 %shard_map.129 = (f32[512,256]{1,0:T(8,128)S(1)}, f32[512,256]{1,0:T(8,128)S(1)}) custom-call(f32[512,256]{1,0:T(8,128)S(1)} %get-tuple-element.40.q_ref, f32[512,256]{1,0:T(8,128)S(1)} %copy-done.9, f32[8,128]{1,0:T(8,128)S(1)} %get-tuple-element.42.run_ref, f32[8,128,256]{2,1,0:T(8,128)S(1)} %copy-done.3, f32[6,128,256]{2,1,0:T(8,128)S(1)} %copy-done.7), custom_call_target="tpu_custom_call" | custom-call | tf_op jit(solution)/shard_map/pallas_call | solution.py:348
  62.4 1.6 %collective-permute-start.11 = (bf16[512,256]{1,0:T(8,128)(2,1)S(1)}, bf16[512,256]{1,0:T(8,128)(2,1)S(1)}, u32[]{:S(2)}, u32[]{:S(2)}) collective-permute-start(bf16[512,256]{1,0:T(8,128)(2,1)S(1)} %shard_map.132.refs_0_), channel_id=1, source_target_pairs={{0,2},{1,3},{2,0},{3,1},{4,6},{5,7},{6,4},{7,5},{8,10},{9,11},{10,... | collective-permute-start | bytes 786440 | tf_op jit(solution)/shard_map/ppermute | solution.py:323
  64.8 1.2 %collective-permute-start.15 = (bf16[256,512]{1,0:T(8,128)(2,1)S(1)}, bf16[256,512]{1,0:T(8,128)(2,1)S(1)}, u32[]{:S(2)}, u32[]{:S(2)}) collective-permute-start(bf16[256,512]{1,0:T(8,128)(2,1)S(1)} %get-tuple-element.56), channel_id=1, source_target_pairs={{0,3},{1,2},{2,1},{3,0},{4,7},{5,6},{6,5},{7,4},{8,11},{9,10},{10,... | collective-permute-start | bytes 786440 | tf_op jit(solution)/shard_map/ppermute | solution.py:323
  66.4 4.1 %collective-permute-done.11.refs_2_ = bf16[512,256]{1,0:T(8,128)(2,1)S(1)} collective-permute-done((bf16[512,256]{1,0:T(8,128)(2,1)S(1)}, bf16[512,256]{1,0:T(8,128)(2,1)S(1)}, u32[]{:S(2)}, u32[]{:S(2)}) %collective-permute-start.11) | collective-permute-done | bytes 262176 | tf_op jit(solution)/shard_map/ppermute | solution.py:323
  70.5 5.6 %collective-permute-done.14.refs_6_ = bf16[256,512]{1,0:T(8,128)(2,1)S(1)} collective-permute-done((bf16[256,512]{1,0:T(8,128)(2,1)S(1)}, bf16[256,512]{1,0:T(8,128)(2,1)S(1)}, u32[]{:S(2)}, u32[]{:S(2)}) %collective-permute-start.14) | collective-permute-done | bytes 262176 | tf_op jit(solution)/shard_map/ppermute | solution.py:323
  76.1 3.0 %collective-permute-done.15.refs_7_ = bf16[256,512]{1,0:T(8,128)(2,1)S(1)} collective-permute-done((bf16[256,512]{1,0:T(8,128)(2,1)S(1)}, bf16[256,512]{1,0:T(8,128)(2,1)S(1)}, u32[]{:S(2)}, u32[]{:S(2)}) %collective-permute-start.15) | collective-permute-done | bytes 262176 | tf_op jit(solution)/shard_map/ppermute | solution.py:323
  79.1 1.5 %shard_map.133 = bf16[512,512]{1,0:T(8,128)(2,1)} custom-call(bf16[512,256]{1,0:T(8,128)(2,1)S(1)} %shard_map.132.refs_0_, bf16[512,256]{1,0:T(8,128)(2,1)S(1)} %collective-permute-done.10.refs_1_, bf16[512,256]{1,0:T(8,128)(2,1)S(1)} %collective-permute-done.11.refs_2_, bf16[512,256]{1,0:T(8,128)(2,1)S(1)} %collective-permute-done.12.refs_3_, ...), custom_call_target="tpu_custom_call" | custom-call | tf_op jit(solution)/shard_map/pallas_call | solution.py:348
  (56 shorter events, 7.4 us)
Async XLA Ops:
  0.0 22.2 %copy-start = (bf16[2048,256]{1,0:T(8,128)(2,1)S(1)}, bf16[2048,256]{1,0:T(8,128)(2,1)}, u32[]{:S(2)}) copy-start(bf16[2048,256]{1,0:T(8,128)(2,1)} %refs_12_.1) | copy-start | bytes 3145732
  0.8 6.3 %collective-permute-start = (bf16[16,512]{1,0:T(8,128)(2,1)S(1)}, bf16[16,512]{1,0:T(8,128)(2,1)S(1)}, u32[]{:S(2)}, u32[]{:S(2)}) collective-permute-start(bf16[16,512]{1,0:T(8,128)(2,1)S(1)} %slice.12), channel_id=1, source_target_pairs={{0,4},{4,8},{8,12},{12,16},{16,20},{20,24},{24,28},{1,5},{5,9},{9,... | collective-permute-start | bytes 49160 | tf_op jit(solution)/shard_map/ppermute | solution.py:387
  7.1 15.1 %copy-start.11 = (bf16[2048,2]{0,1:T(2,128)(2,1)S(1)}, bf16[2048,2]{0,1:T(2,128)(2,1)}, u32[]{:S(2)}) copy-start(bf16[2048,2]{0,1:T(2,128)(2,1)} %param.18) | copy-start | bytes 24580
  7.1 15.1 %copy-start.12 = (bf16[2048,2]{0,1:T(2,128)(2,1)S(1)}, bf16[2048,2]{0,1:T(2,128)(2,1)}, u32[]{:S(2)}) copy-start(bf16[2048,2]{0,1:T(2,128)(2,1)} %param.19) | copy-start | bytes 24580
  7.2 15.1 %copy-start.10 = (f32[4,3,256]{2,0,1:T(4,128)S(1)}, f32[4,3,256]{2,0,1:T(4,128)}, u32[]{:S(2)}) copy-start(f32[4,3,256]{2,0,1:T(4,128)} %param.20) | copy-start | bytes 36868
  7.2 9.6 %collective-permute-start.3 = (bf16[272,512]{1,0:T(8,128)(2,1)S(1)}, bf16[272,512]{1,0:T(8,128)(2,1)S(1)}, u32[]{:S(2)}, u32[]{:S(2)}) collective-permute-start(bf16[272,512]{1,0:T(8,128)(2,1)S(1)} %pad_maximum_fusion.refs_4_.refs_1_), channel_id=1, source_target_pairs={{0,2},{1,3},{2,0},{3,1},{4,6},{5,7},{6,4},{7,5},{8,10},{9,11},{10,... | collective-permute-start | bytes 835592 | tf_op jit(solution)/shard_map/ppermute | solution.py:323
  8.7 11.9 %collective-permute-start.4 = (bf16[256,512]{1,0:T(8,128)(2,1)S(1)}, bf16[256,512]{1,0:T(8,128)(2,1)S(1)}, u32[]{:S(2)}, u32[]{:S(2)}) collective-permute-start(bf16[256,512]{1,0:T(8,128)(2,1)S(1)} %get-tuple-element.33.refs_5_.refs_2_), channel_id=1, source_target_pairs={{0,2},{1,3},{2,0},{3,1},{4,6},{5,7},{6,4},{7,5},{8,10},{9,11},{10,... | collective-permute-start | bytes 786440 | tf_op jit(solution)/shard_map/ppermute | solution.py:323
  9.3 11.4 %collective-permute-start.1 = (bf16[272,512]{1,0:T(8,128)(2,1)S(1)}, bf16[272,512]{1,0:T(8,128)(2,1)S(1)}, u32[]{:S(2)}, u32[]{:S(2)}) collective-permute-start(bf16[272,512]{1,0:T(8,128)(2,1)S(1)} %pad_maximum_fusion.refs_4_.refs_1_), channel_id=1, source_target_pairs={{0,1},{1,0},{2,3},{3,2},{4,5},{5,4},{6,7},{7,6},{8,9},{9,8},{10,11... | collective-permute-start | bytes 835592 | tf_op jit(solution)/shard_map/ppermute | solution.py:323
  16.8 5.4 %collective-permute-start.5 = (bf16[272,512]{1,0:T(8,128)(2,1)S(1)}, bf16[272,512]{1,0:T(8,128)(2,1)S(1)}, u32[]{:S(2)}, u32[]{:S(2)}) collective-permute-start(bf16[272,512]{1,0:T(8,128)(2,1)S(1)} %collective-permute-done.3.refs_8_.refs_5_), channel_id=1, source_target_pairs={{0,1},{1,0},{2,3},{3,2},{4,5},{5,4},{6,7},{7,6},{8,9},{9,8},{10,11... | collective-permute-start | bytes 835592 | tf_op jit(solution)/shard_map/ppermute | solution.py:323
  16.8 3.9 %collective-permute-start.2 = (bf16[256,512]{1,0:T(8,128)(2,1)S(1)}, bf16[256,512]{1,0:T(8,128)(2,1)S(1)}, u32[]{:S(2)}, u32[]{:S(2)}) collective-permute-start(bf16[256,512]{1,0:T(8,128)(2,1)S(1)} %get-tuple-element.33.refs_5_.refs_2_), channel_id=1, source_target_pairs={{0,1},{1,0},{2,3},{3,2},{4,5},{5,4},{6,7},{7,6},{8,9},{9,8},{10,11... | collective-permute-start | bytes 786440 | tf_op jit(solution)/shard_map/ppermute | solution.py:323
  20.7 1.5 %collective-permute-start.6 = (bf16[256,512]{1,0:T(8,128)(2,1)S(1)}, bf16[256,512]{1,0:T(8,128)(2,1)S(1)}, u32[]{:S(2)}, u32[]{:S(2)}) collective-permute-start(bf16[256,512]{1,0:T(8,128)(2,1)S(1)} %collective-permute-done.4.refs_9_.refs_6_), channel_id=1, source_target_pairs={{0,1},{1,0},{2,3},{3,2},{4,5},{5,4},{6,7},{7,6},{8,9},{9,8},{10,11... | collective-permute-start | bytes 786440 | tf_op jit(solution)/shard_map/ppermute | solution.py:323
  34.4 23.5 %copy-start.4 = (bf16[2048,256]{1,0:T(8,128)(2,1)S(1)}, bf16[2048,256]{1,0:T(8,128)(2,1)}, u32[]{:S(2)}) copy-start(bf16[2048,256]{1,0:T(8,128)(2,1)} %refs_9_.1) | copy-start | bytes 3145732
  34.4 7.1 %collective-permute-start.7 = (bf16[2,128,256]{2,1,0:T(8,128)(2,1)}, bf16[2,128,256]{2,1,0:T(8,128)(2,1)}, u32[]{:S(2)}, u32[]{:S(2)}) collective-permute-start(bf16[2,128,256]{2,1,0:T(8,128)(2,1)} %get-tuple-element.31), channel_id=1, source_target_pairs={{0,4},{4,8},{8,12},{12,16},{16,20},{20,24},{24,28},{1,5},{5,9},{9,... | collective-permute-start | bytes 393224 | tf_op jit(solution)/shard_map/ppermute | solution.py:387
  42.6 8.8 %collective-permute-start.8 = (bf16[2,128,256]{2,1,0:T(8,128)(2,1)S(1)}, bf16[2,128,256]{2,1,0:T(8,128)(2,1)S(1)}, u32[]{:S(2)}, u32[]{:S(2)}) collective-permute-start(bf16[2,128,256]{2,1,0:T(8,128)(2,1)S(1)} %get-tuple-element.49), channel_id=1, source_target_pairs={{0,8},{4,12},{8,16},{12,20},{16,24},{20,28},{1,9},{5,13},{9,17},{1... | collective-permute-start | bytes 393224 | tf_op jit(solution)/shard_map/ppermute | solution.py:387
  52.3 5.5 %copy-start.16 = (f32[128]{0:T(128)S(1)}, f32[128]{0:T(128)}, u32[]{:S(2)}) copy-start(f32[128]{0:T(128)} %param.24) | copy-start | bytes 1540
  52.3 9.5 %collective-permute-start.9 = (bf16[2,128,128]{2,1,0:T(8,128)(2,1)S(1)}, bf16[2,128,128]{2,1,0:T(8,128)(2,1)S(1)}, u32[]{:S(2)}, u32[]{:S(2)}) collective-permute-start(bf16[2,128,128]{2,1,0:T(8,128)(2,1)S(1)} %slice.15), channel_id=1, source_target_pairs={{0,16},{4,20},{8,24},{12,28},{1,17},{5,21},{9,25},{13,29},{2,18},{... | collective-permute-start | bytes 196616 | tf_op jit(solution)/shard_map/ppermute | solution.py:387
  59.1 1.6 %copy-start.9 = (f32[512,256]{1,0:T(8,128)S(1)}, f32[512,256]{1,0:T(8,128)}, u32[]{:S(2)}) copy-start(f32[512,256]{1,0:T(8,128)} %copy-done.8) | copy-start | bytes 1572868
  61.8 2.2 %copy-start.17 = (bf16[256,2048]{1,0:T(8,128)(2,1)S(1)}, bf16[256,2048]{1,0:T(8,128)(2,1)}, u32[]{:S(2)}) copy-start(bf16[256,2048]{1,0:T(8,128)(2,1)} %param.25) | copy-start | bytes 3145732
  62.4 8.0 %collective-permute-start.11 = (bf16[512,256]{1,0:T(8,128)(2,1)S(1)}, bf16[512,256]{1,0:T(8,128)(2,1)S(1)}, u32[]{:S(2)}, u32[]{:S(2)}) collective-permute-start(bf16[512,256]{1,0:T(8,128)(2,1)S(1)} %shard_map.132.refs_0_), channel_id=1, source_target_pairs={{0,2},{1,3},{2,0},{3,1},{4,6},{5,7},{6,4},{7,5},{8,10},{9,11},{10,... | collective-permute-start | bytes 786440 | tf_op jit(solution)/shard_map/ppermute | solution.py:323
  64.1 6.4 %collective-permute-start.13 = (bf16[256,512]{1,0:T(8,128)(2,1)S(1)}, bf16[256,512]{1,0:T(8,128)(2,1)S(1)}, u32[]{:S(2)}, u32[]{:S(2)}) collective-permute-start(bf16[256,512]{1,0:T(8,128)(2,1)S(1)} %get-tuple-element.54), channel_id=1, source_target_pairs={{0,1},{1,0},{2,3},{3,2},{4,5},{5,4},{6,7},{7,6},{8,9},{9,8},{10,11... | collective-permute-start | bytes 786440 | tf_op jit(solution)/shard_map/ppermute | solution.py:323
  64.2 11.9 %collective-permute-start.14 = (bf16[256,512]{1,0:T(8,128)(2,1)S(1)}, bf16[256,512]{1,0:T(8,128)(2,1)S(1)}, u32[]{:S(2)}, u32[]{:S(2)}) collective-permute-start(bf16[256,512]{1,0:T(8,128)(2,1)S(1)} %get-tuple-element.55), channel_id=1, source_target_pairs={{0,2},{1,3},{2,0},{3,1},{4,6},{5,7},{6,4},{7,5},{8,10},{9,11},{10,... | collective-permute-start | bytes 786440 | tf_op jit(solution)/shard_map/ppermute | solution.py:323
  64.8 14.3 %collective-permute-start.15 = (bf16[256,512]{1,0:T(8,128)(2,1)S(1)}, bf16[256,512]{1,0:T(8,128)(2,1)S(1)}, u32[]{:S(2)}, u32[]{:S(2)}) collective-permute-start(bf16[256,512]{1,0:T(8,128)(2,1)S(1)} %get-tuple-element.56), channel_id=1, source_target_pairs={{0,3},{1,2},{2,1},{3,0},{4,7},{5,6},{6,5},{7,4},{8,11},{9,10},{10,... | collective-permute-start | bytes 786440 | tf_op jit(solution)/shard_map/ppermute | solution.py:323
  66.0 13.1 %collective-permute-start.10 = (bf16[512,256]{1,0:T(8,128)(2,1)S(1)}, bf16[512,256]{1,0:T(8,128)(2,1)S(1)}, u32[]{:S(2)}, u32[]{:S(2)}) collective-permute-start(bf16[512,256]{1,0:T(8,128)(2,1)S(1)} %shard_map.132.refs_0_), channel_id=1, source_target_pairs={{0,1},{1,0},{2,3},{3,2},{4,5},{5,4},{6,7},{7,6},{8,9},{9,8},{10,11... | collective-permute-start | bytes 786440 | tf_op jit(solution)/shard_map/ppermute | solution.py:323
  70.5 8.7 %collective-permute-start.12 = (bf16[512,256]{1,0:T(8,128)(2,1)S(1)}, bf16[512,256]{1,0:T(8,128)(2,1)S(1)}, u32[]{:S(2)}, u32[]{:S(2)}) collective-permute-start(bf16[512,256]{1,0:T(8,128)(2,1)S(1)} %collective-permute-done.11.refs_2_), channel_id=1, source_target_pairs={{0,1},{1,0},{2,3},{3,2},{4,5},{5,4},{6,7},{7,6},{8,9},{9,8},{10,11... | collective-permute-start | bytes 786440 | tf_op jit(solution)/shard_map/ppermute | solution.py:323
  (10 other events, 10.0 us)

commit v3 on v2

--- a/solution.py
+++ b/solution.py
@@ -114,8 +114,15 @@
     pieces = take_pieces(refs, masks, chunks)
     refs = refs[masks * chunks :]
     key_w, value_w, beta_w, decay_w, conv_ref = refs[:5]
-    k_out, run_out, solved_out, prefix_out, slab_out, slab_low_out, ext = refs[5:]
+    k_hbm, run_out, solved_hbm, prefix_hbm, slab_hbm, slab_low_out = refs[5:11]
+    ext, k_out, solved_out, prefix_out, slab_out, sems = refs[11:]
     tokens = k_out.shape[0]
+    leaving = [
+        pltpu.make_async_copy(k_out, k_hbm, sems.at[0]),
+        pltpu.make_async_copy(solved_out, solved_hbm, sems.at[1]),
+        pltpu.make_async_copy(prefix_out, prefix_hbm, sems.at[2]),
+        pltpu.make_async_copy(slab_out, slab_hbm, sems.at[3]),
+    ]
     features = pieces[0][0].shape[1]
     blocks = tokens // BLOCK
     units = [(b, h) for b in range(blocks) for h in range(heads)]
@@ -152,6 +159,7 @@
         dim,
     )
     k_out[...] = keys
+    leaving[0].start()
     values = conv_rows(
         ext, project(pieces, value_w, index, features), conv_ref, 2, taps, tokens
     )
@@ -195,6 +203,7 @@
         solved = mm_wide(split(inverse[b, h]), split(right))
         solved_out[b * heads + h] = solved
         solved_pair[b, h] = split(solved)
+    leaving[1].start()
     for b, h in units:
         rcol = running_t[:, b * heads + h : b * heads + h + 1]
         last = rcol[BLOCK - 1 : BLOCK, :]
@@ -207,10 +216,11 @@
         out = mm_wide(split(later[:, :dim]), split(earlier))
         return jnp.concatenate([out[:, :dim], out[:, dim:] + later[:, dim:]], axis=1)
 
+    slabs = []
     for h in range(heads):
         spans = {(b, 1): maps[b, h] for b in range(blocks)}
 
-        def span(start, count):
+        def span(start, count, h=h, spans=spans):
             if (start, count) not in spans:
                 half = 1
                 while half * 2 < count:
@@ -222,9 +232,15 @@
 
         for b in range(1, blocks):
             prefix_out[h * (blocks - 1) + b - 1] = span(0, b)
+        slabs.append(span)
+    leaving[2].start()
+    for h, span in enumerate(slabs):
         slab = span(0, blocks)
         slab_out[h] = slab
         slab_low_out[h] = slab.astype(bf16)
+    leaving[3].start()
+    for copy in leaving:
+        copy.wait()
 
 
 def query_kernel(masks, chunks, heads, dim, taps, *refs):
@@ -309,13 +325,13 @@
         out_ref[:, cols] = (scaled * gate_ref[:, cols]).astype(bf16)
 
 
-def output_kernel(masks, *refs):
-    out_ref = refs[2 * masks]
-    total = None
-    for m in range(masks):
-        part = dot(refs[m][...], refs[masks + m][...])
+def output_kernel(count, has_sum, *refs):
+    out_ref = refs[-1]
+    total = refs[2 * count][...] if has_sum else None
+    for m in range(count):
+        part = dot(refs[m][...], refs[count + m][...])
         total = part if total is None else total + part
-    out_ref[...] = total.astype(bf16)
+    out_ref[...] = total.astype(out_ref.dtype)
 
 
 def xor_permute(value, mask):
@@ -339,12 +355,20 @@
     return [pieces[m] for m in range(masks)]
 
 
-def vmem_call(kernel, out_shape, operands, scalars=0, scratch=(), limit=16):
+def vmem_call(kernel, out_shape, operands, scalars=0, scratch=(), limit=16, hbm=()):
     specs = [
         pl.BlockSpec(memory_space=pltpu.SMEM if i < scalars else pltpu.VMEM)
         for i in range(len(operands))
     ]
-    outs = jax.tree.map(lambda _: pl.BlockSpec(memory_space=pltpu.VMEM), out_shape)
+    outs = pl.BlockSpec(memory_space=pltpu.VMEM)
+    if isinstance(out_shape, tuple):
+        outs = tuple(
+            pl.BlockSpec(memory_space=pltpu.HBM if i in hbm else pltpu.VMEM)
+            for i in range(len(out_shape))
+        )
+        out_shape = tuple(
+            pltpu.HBM(o.shape, o.dtype) if i in hbm else o for i, o in enumerate(out_shape)
+        )
     return pl.pallas_call(
         kernel,
         out_shape=out_shape,
@@ -412,8 +436,16 @@
         [head_at, decay_log, beta_bias, decay_bias, *x_flat]
         + [key_weight, value_weight, beta_weight.T, decay_weight.T, conv],
         scalars=4,
-        scratch=(ext,),
+        scratch=(
+            ext,
+            pltpu.VMEM(rows, f32),
+            pltpu.VMEM((blocks * heads, BLOCK, 2 * dim), f32),
+            pltpu.VMEM(((blocks - 1) * heads, dim, 2 * dim), f32),
+            pltpu.VMEM(maps, f32),
+            pltpu.SemaphoreType.DMA((4,)),
+        ),
         limit=24,
+        hbm=(0, 2, 3, 4),
     )
 
     width = out_weight.shape[1] // masks
@@ -463,12 +495,18 @@
         limit=8,
     )
     pieces = gather_chunks([hidden], masks)
-    return vmem_call(
-        functools.partial(output_kernel, masks),
-        shape((tokens, width), bf16),
-        [p[0] for p in pieces] + columns,
-        limit=8,
-    )
+    total = None
+    stages = [list(range(masks // 2))] + [[m] for m in range(masks // 2, masks)]
+    for i, stage in enumerate(stages):
+        last = i == len(stages) - 1
+        operands = [pieces[m][0] for m in stage] + [columns[m] for m in stage]
+        total = vmem_call(
+            functools.partial(output_kernel, len(stage), i > 0),
+            shape((tokens, width), bf16 if last else f32),
+            operands + ([total] if i > 0 else []),
+            limit=8,
+        )
+    return total
 
 
 def solution(mesh):

time: 81.3 us -> 78.2 us (0.962)
  local copies, waits for them, and re-layouts: 7.87 us -> 6.18 us
  starting transfers between devices: 27.5 us -> 26.6 us
    unnamed x36 -> x32, local copies, waits for them, and re-layouts: 5.89 us -> 4.2 us
    pallas_call x7 -> x9, Pallas kernels: 14.3 us -> 13.9 us  [vmem_call(): pl.pallas_call(kernel, out_shape=out_shape, in_specs=specs, out_specs=out...]
  transfers between devices with their start and end apart: 16 -> 16, of which waited for: 9 -> 9; matrix products, arithmetic and copies ran while one was open for 1% -> 2% of each run, Pallas kernels for 3% -> 4%
where the time goes in v3:
time: 78.2 us; the launch traced here: 77.5 us
  waiting for transfers between devices  30.6 us (39%)
  starting transfers between devices  26.6 us (34%)
  Pallas kernels  13.9 us (18%)
  local copies, waits for them, and re-layouts  6.18 us (8%)
    ppermute x12, waiting for transfers between devices, xor_permute(): return lax.ppermute(value, 'head', [(i, i ^ mask) for i in range(count)])  24.7 us
    ppermute x4, starting transfers between devices, shifted(): return lax.ppermute(value, 'seq', pairs)  20.4 us
    pallas_call x9, Pallas kernels, vmem_call(): pl.pallas_call(kernel, out_shape=out_shape, in_specs=specs, out_specs=out...  13.9 us
    ppermute x12, starting transfers between devices, xor_permute(): return lax.ppermute(value, 'head', [(i, i ^ mask) for i in range(count)])  6.16 us
    ppermute x4, waiting for transfers between devices, shifted(): return lax.ppermute(value, 'seq', pairs)  5.88 us
    unnamed x32, local copies, waits for them, and re-layouts  4.2 us
  transfers between devices with their start and end apart: 16, of which 9 were waited for; matrix products, arithmetic and copies ran while one was open for 2% of the time, Pallas kernels for 4%

profile of v3, /device:TPU:0, one launch (start us, length us, event | category | flops | bytes accessed | tf_op | source)
XLA Modules:
  0.0 77.5 jit_solution(11005380281942413669)
XLA Ops:
  0.8 4.9 %collective-permute-start = (bf16[16,512]{1,0:T(8,128)(2,1)S(1)}, bf16[16,512]{1,0:T(8,128)(2,1)S(1)}, u32[]{:S(2)}, u32[]{:S(2)}) collective-permute-start(bf16[16,512]{1,0:T(8,128)(2,1)S(1)} %slice.12), channel_id=1, source_target_pairs={{0,4},{4,8},{8,12},{12,16},{16,20},{20,24},{24,28},{1,5},{5,9},{9,... | collective-permute-start | bytes 49160 | tf_op jit(solution)/shard_map/ppermute | solution.py:411
  5.7 1.1 %fusion = (bf16[256,512]{1,0:T(8,128)(2,1)S(1)}, bf16[256,512]{1,0:T(8,128)(2,1)S(1)}) fusion(bf16[512,512]{1,0:T(8,128)(2,1)} %param.13), kind=kLoop, calls=%fused_computation.5 | loop fusion | bytes 1048576 | tf_op jit(solution)/shard_map/slice | solution.py:417
  7.2 1.6 %collective-permute-start.3 = (bf16[272,512]{1,0:T(8,128)(2,1)S(1)}, bf16[272,512]{1,0:T(8,128)(2,1)S(1)}, u32[]{:S(2)}, u32[]{:S(2)}) collective-permute-start(bf16[272,512]{1,0:T(8,128)(2,1)S(1)} %pad_maximum_fusion.refs_4_.refs_1_), channel_id=1, source_target_pairs={{0,2},{1,3},{2,0},{3,1},{4,6},{5,7},{6,4},{7,5},{8,10},{9,11},{10,... | collective-permute-start | bytes 835592 | tf_op jit(solution)/shard_map/ppermute | solution.py:339
  9.3 7.5 %collective-permute-done.3.refs_8_.refs_5_ = bf16[272,512]{1,0:T(8,128)(2,1)S(1)} collective-permute-done((bf16[272,512]{1,0:T(8,128)(2,1)S(1)}, bf16[272,512]{1,0:T(8,128)(2,1)S(1)}, u32[]{:S(2)}, u32[]{:S(2)}) %collective-permute-start.3) | collective-permute-done | bytes 278560 | tf_op jit(solution)/shard_map/ppermute | solution.py:339
  17.3 3.4 %collective-permute-done.4.refs_9_.refs_6_ = bf16[256,512]{1,0:T(8,128)(2,1)S(1)} collective-permute-done((bf16[256,512]{1,0:T(8,128)(2,1)S(1)}, bf16[256,512]{1,0:T(8,128)(2,1)S(1)}, u32[]{:S(2)}, u32[]{:S(2)}) %collective-permute-start.4) | collective-permute-done | bytes 262176 | tf_op jit(solution)/shard_map/ppermute | solution.py:339
  20.7 1.5 %collective-permute-done.6.refs_11_.refs_8_ = bf16[256,512]{1,0:T(8,128)(2,1)S(1)} collective-permute-done((bf16[256,512]{1,0:T(8,128)(2,1)S(1)}, bf16[256,512]{1,0:T(8,128)(2,1)S(1)}, u32[]{:S(2)}, u32[]{:S(2)}) %collective-permute-start.6) | collective-permute-done | bytes 262176 | tf_op jit(solution)/shard_map/ppermute | solution.py:339
  22.9 1.2 %copy-done.1 = bf16[2048,256]{1,0:T(8,128)(2,1)S(1)} copy-done((bf16[2048,256]{1,0:T(8,128)(2,1)S(1)}, bf16[2048,256]{1,0:T(8,128)(2,1)}, u32[]{:S(2)}) %copy-start.1) | copy-done | bytes 1048600
  24.1 7.8 %shard_map.127 = (f32[512,256]{1,0:T(8,128)}, f32[8,128]{1,0:T(8,128)S(1)}, f32[8,128,256]{2,1,0:T(8,128)}, f32[6,128,256]{2,1,0:T(8,128)}, f32[2,128,256]{2,1,0:T(8,128)}, /*index=5*/bf16[2,128,256]{2,1,0:T(8,128)(2,1)S(1)}) custom-call(s32[1]{0:T(128)} %bitcast.refs_0_, f32[2]{0:T(128)S(1)} %copy-done.11, f32[2]{0:T(128)S(1)} %copy-done.12, ...), custom_call_target="tpu_custom_call" | custom-call | tf_op jit(solution)/shard_map/pallas_call | solution.py:372
  31.9 3.8 %collective-permute-start.7 = (bf16[2,128,256]{2,1,0:T(8,128)(2,1)S(1)}, bf16[2,128,256]{2,1,0:T(8,128)(2,1)S(1)}, u32[]{:S(2)}, u32[]{:S(2)}) collective-permute-start(bf16[2,128,256]{2,1,0:T(8,128)(2,1)S(1)} %get-tuple-element.31), channel_id=1, source_target_pairs={{0,4},{4,8},{8,12},{12,16},{16,20},{20,24},{24,28},{1,5},{5,9},{9,... | collective-permute-start | bytes 393224 | tf_op jit(solution)/shard_map/ppermute | solution.py:411
  35.7 3.0 %collective-permute-done.7.got_ref = bf16[2,128,256]{2,1,0:T(8,128)(2,1)S(1)} collective-permute-done((bf16[2,128,256]{2,1,0:T(8,128)(2,1)S(1)}, bf16[2,128,256]{2,1,0:T(8,128)(2,1)S(1)}, u32[]{:S(2)}, u32[]{:S(2)}) %collective-permute-start.7) | collective-permute-done | bytes 131104 | tf_op jit(solution)/shard_map/ppermute | solution.py:411
  38.7 0.9 %copy-done.7 = f32[2,128,256]{2,1,0:T(8,128)S(1)} copy-done((f32[2,128,256]{2,1,0:T(8,128)S(1)}, f32[2,128,256]{2,1,0:T(8,128)}, u32[]{:S(2)}) %copy-start.7) | copy-done | bytes 262168
  39.9 6.3 %collective-permute-start.8 = (bf16[2,128,256]{2,1,0:T(8,128)(2,1)S(1)}, bf16[2,128,256]{2,1,0:T(8,128)(2,1)S(1)}, u32[]{:S(2)}, u32[]{:S(2)}) collective-permute-start(bf16[2,128,256]{2,1,0:T(8,128)(2,1)S(1)} %get-tuple-element.49), channel_id=1, source_target_pairs={{0,8},{4,12},{8,16},{12,20},{16,24},{20,28},{1,9},{5,13},{9,17},{1... | collective-permute-start | bytes 393224 | tf_op jit(solution)/shard_map/ppermute | solution.py:411
  46.1 2.5 %collective-permute-done.8.got_ref = bf16[2,128,256]{2,1,0:T(8,128)(2,1)S(1)} collective-permute-done((bf16[2,128,256]{2,1,0:T(8,128)(2,1)S(1)}, bf16[2,128,256]{2,1,0:T(8,128)(2,1)S(1)}, u32[]{:S(2)}, u32[]{:S(2)}) %collective-permute-start.8) | collective-permute-done | bytes 131104 | tf_op jit(solution)/shard_map/ppermute | solution.py:411
  48.6 1.0 %shard_map.131 = (f32[2,128,256]{2,1,0:T(8,128)S(1)}, f32[2,128,256]{2,1,0:T(8,128)}, bf16[2,128,256]{2,1,0:T(8,128)(2,1)S(1)}) custom-call(s32[1]{0:T(128)} %bitcast.5.pos_ref, bf16[2,128,256]{2,1,0:T(8,128)(2,1)S(1)} %collective-permute-done.8.got_ref, f32[2,128,256]{2,1,0:T(8,128)S(1)} %get-tuple-element.50.refs_0_, ...), custom_call_target="tpu_custom_call" | custom-call | tf_op jit(solution)/shard_map/pallas_call | solution.py:372
  49.6 5.5 %collective-permute-start.9 = (bf16[2,128,128]{2,1,0:T(8,128)(2,1)S(1)}, bf16[2,128,128]{2,1,0:T(8,128)(2,1)S(1)}, u32[]{:S(2)}, u32[]{:S(2)}) collective-permute-start(bf16[2,128,128]{2,1,0:T(8,128)(2,1)S(1)} %slice.15), channel_id=1, source_target_pairs={{0,16},{4,20},{8,24},{12,28},{1,17},{5,21},{9,25},{13,29},{2,18},{... | collective-permute-start | bytes 196616 | tf_op jit(solution)/shard_map/ppermute | solution.py:411
  55.1 1.2 %copy-done.4 = bf16[2048,256]{1,0:T(8,128)(2,1)S(1)} copy-done((bf16[2048,256]{1,0:T(8,128)(2,1)S(1)}, bf16[2048,256]{1,0:T(8,128)(2,1)}, u32[]{:S(2)}) %copy-start.4) | copy-done | bytes 1048600
  56.3 1.4 %shard_map.128 = (f32[512,256]{1,0:T(8,128)S(1)}, f32[512,256]{1,0:T(8,128)S(1)}) custom-call(s32[1]{0:T(128)} %bitcast.refs_0_, bf16[272,512]{1,0:T(8,128)(2,1)S(1)} %pad_maximum_fusion.refs_4_.refs_1_, bf16[256,512]{1,0:T(8,128)(2,1)S(1)} %get-tuple-element.33.refs_5_.refs_2_, bf16[272,512]{1,0:T(8,128)(2,1)S(1)} %collective-permute-done.1.refs_6_.refs_3_, ...), custom_call_target="tpu_custom_call" | custom-call | tf_op jit(solution)/shard_map/pallas_call | solution.py:372
  57.9 1.2 %shard_map.129 = (f32[512,256]{1,0:T(8,128)S(1)}, f32[512,256]{1,0:T(8,128)S(1)}) custom-call(f32[512,256]{1,0:T(8,128)S(1)} %get-tuple-element.40.q_ref, f32[512,256]{1,0:T(8,128)S(1)} %copy-done.6, f32[8,128]{1,0:T(8,128)S(1)} %get-tuple-element.42.run_ref, f32[8,128,256]{2,1,0:T(8,128)S(1)} %copy-done.2, f32[6,128,256]{2,1,0:T(8,128)S(1)} %copy-done.5), custom_call_target="tpu_custom_call" | custom-call | tf_op jit(solution)/shard_map/pallas_call | solution.py:372
  59.7 1.6 %collective-permute-start.10 = (bf16[512,256]{1,0:T(8,128)(2,1)S(1)}, bf16[512,256]{1,0:T(8,128)(2,1)S(1)}, u32[]{:S(2)}, u32[]{:S(2)}) collective-permute-start(bf16[512,256]{1,0:T(8,128)(2,1)S(1)} %shard_map.132.refs_0_), channel_id=1, source_target_pairs={{0,2},{1,3},{2,0},{3,1},{4,6},{5,7},{6,4},{7,5},{8,10},{9,11},{10,... | collective-permute-start | bytes 786440 | tf_op jit(solution)/shard_map/ppermute | solution.py:339
  62.5 0.9 %collective-permute-start.12 = (bf16[256,512]{1,0:T(8,128)(2,1)S(1)}, bf16[256,512]{1,0:T(8,128)(2,1)S(1)}, u32[]{:S(2)}, u32[]{:S(2)}) collective-permute-start(bf16[256,512]{1,0:T(8,128)(2,1)S(1)} %get-tuple-element.54), channel_id=1, source_target_pairs={{0,3},{1,2},{2,1},{3,0},{4,7},{5,6},{6,5},{7,4},{8,11},{9,10},{10,... | collective-permute-start | bytes 786440 | tf_op jit(solution)/shard_map/ppermute | solution.py:339
  63.4 4.3 %collective-permute-done.10.refs_0_ = bf16[512,256]{1,0:T(8,128)(2,1)S(1)} collective-permute-done((bf16[512,256]{1,0:T(8,128)(2,1)S(1)}, bf16[512,256]{1,0:T(8,128)(2,1)S(1)}, u32[]{:S(2)}, u32[]{:S(2)}) %collective-permute-start.10) | collective-permute-done | bytes 262176 | tf_op jit(solution)/shard_map/ppermute | solution.py:339
  68.1 5.2 %collective-permute-done.13.refs_1_ = bf16[256,512]{1,0:T(8,128)(2,1)S(1)} collective-permute-done((bf16[256,512]{1,0:T(8,128)(2,1)S(1)}, bf16[256,512]{1,0:T(8,128)(2,1)S(1)}, u32[]{:S(2)}, u32[]{:S(2)}) %collective-permute-start.13) | collective-permute-done | bytes 262176 | tf_op jit(solution)/shard_map/ppermute | solution.py:339
  73.6 2.8 %collective-permute-done.12.refs_1_ = bf16[256,512]{1,0:T(8,128)(2,1)S(1)} collective-permute-done((bf16[256,512]{1,0:T(8,128)(2,1)S(1)}, bf16[256,512]{1,0:T(8,128)(2,1)S(1)}, u32[]{:S(2)}, u32[]{:S(2)}) %collective-permute-start.12) | collective-permute-done | bytes 262176 | tf_op jit(solution)/shard_map/ppermute | solution.py:339
  76.4 1.1 %shard_map.135 = bf16[512,512]{1,0:T(8,128)(2,1)} custom-call(bf16[512,256]{1,0:T(8,128)(2,1)S(1)} %collective-permute-done.11.refs_0_, bf16[256,512]{1,0:T(8,128)(2,1)S(1)} %collective-permute-done.12.refs_1_, f32[512,512]{1,0:T(8,128)S(1)} %shard_map.134.refs_2_), custom_call_target="tpu_custom_call" | custom-call | tf_op jit(solution)/shard_map/pallas_call | solution.py:372
  (54 shorter events, 5.8 us)
Async XLA Ops:
  0.0 22.2 %copy-start = (bf16[2048,256]{1,0:T(8,128)(2,1)S(1)}, bf16[2048,256]{1,0:T(8,128)(2,1)}, u32[]{:S(2)}) copy-start(bf16[2048,256]{1,0:T(8,128)(2,1)} %refs_12_.1) | copy-start | bytes 3145732
  0.8 6.3 %collective-permute-start = (bf16[16,512]{1,0:T(8,128)(2,1)S(1)}, bf16[16,512]{1,0:T(8,128)(2,1)S(1)}, u32[]{:S(2)}, u32[]{:S(2)}) collective-permute-start(bf16[16,512]{1,0:T(8,128)(2,1)S(1)} %slice.12), channel_id=1, source_target_pairs={{0,4},{4,8},{8,12},{12,16},{16,20},{20,24},{24,28},{1,5},{5,9},{9,... | collective-permute-start | bytes 49160 | tf_op jit(solution)/shard_map/ppermute | solution.py:411
  7.1 15.1 %copy-start.9 = (bf16[2048,2]{0,1:T(2,128)(2,1)S(1)}, bf16[2048,2]{0,1:T(2,128)(2,1)}, u32[]{:S(2)}) copy-start(bf16[2048,2]{0,1:T(2,128)(2,1)} %param.18) | copy-start | bytes 24580
  7.1 15.1 %copy-start.10 = (bf16[2048,2]{0,1:T(2,128)(2,1)S(1)}, bf16[2048,2]{0,1:T(2,128)(2,1)}, u32[]{:S(2)}) copy-start(bf16[2048,2]{0,1:T(2,128)(2,1)} %param.19) | copy-start | bytes 24580
  7.2 15.1 %copy-start.8 = (f32[4,3,256]{2,0,1:T(4,128)S(1)}, f32[4,3,256]{2,0,1:T(4,128)}, u32[]{:S(2)}) copy-start(f32[4,3,256]{2,0,1:T(4,128)} %param.20) | copy-start | bytes 36868
  7.2 9.6 %collective-permute-start.3 = (bf16[272,512]{1,0:T(8,128)(2,1)S(1)}, bf16[272,512]{1,0:T(8,128)(2,1)S(1)}, u32[]{:S(2)}, u32[]{:S(2)}) collective-permute-start(bf16[272,512]{1,0:T(8,128)(2,1)S(1)} %pad_maximum_fusion.refs_4_.refs_1_), channel_id=1, source_target_pairs={{0,2},{1,3},{2,0},{3,1},{4,6},{5,7},{6,4},{7,5},{8,10},{9,11},{10,... | collective-permute-start | bytes 835592 | tf_op jit(solution)/shard_map/ppermute | solution.py:339
  8.7 11.9 %collective-permute-start.4 = (bf16[256,512]{1,0:T(8,128)(2,1)S(1)}, bf16[256,512]{1,0:T(8,128)(2,1)S(1)}, u32[]{:S(2)}, u32[]{:S(2)}) collective-permute-start(bf16[256,512]{1,0:T(8,128)(2,1)S(1)} %get-tuple-element.33.refs_5_.refs_2_), channel_id=1, source_target_pairs={{0,2},{1,3},{2,0},{3,1},{4,6},{5,7},{6,4},{7,5},{8,10},{9,11},{10,... | collective-permute-start | bytes 786440 | tf_op jit(solution)/shard_map/ppermute | solution.py:339
  9.3 11.4 %collective-permute-start.1 = (bf16[272,512]{1,0:T(8,128)(2,1)S(1)}, bf16[272,512]{1,0:T(8,128)(2,1)S(1)}, u32[]{:S(2)}, u32[]{:S(2)}) collective-permute-start(bf16[272,512]{1,0:T(8,128)(2,1)S(1)} %pad_maximum_fusion.refs_4_.refs_1_), channel_id=1, source_target_pairs={{0,1},{1,0},{2,3},{3,2},{4,5},{5,4},{6,7},{7,6},{8,9},{9,8},{10,11... | collective-permute-start | bytes 835592 | tf_op jit(solution)/shard_map/ppermute | solution.py:339
  16.8 5.4 %collective-permute-start.5 = (bf16[272,512]{1,0:T(8,128)(2,1)S(1)}, bf16[272,512]{1,0:T(8,128)(2,1)S(1)}, u32[]{:S(2)}, u32[]{:S(2)}) collective-permute-start(bf16[272,512]{1,0:T(8,128)(2,1)S(1)} %collective-permute-done.3.refs_8_.refs_5_), channel_id=1, source_target_pairs={{0,1},{1,0},{2,3},{3,2},{4,5},{5,4},{6,7},{7,6},{8,9},{9,8},{10,11... | collective-permute-start | bytes 835592 | tf_op jit(solution)/shard_map/ppermute | solution.py:339
  16.8 3.9 %collective-permute-start.2 = (bf16[256,512]{1,0:T(8,128)(2,1)S(1)}, bf16[256,512]{1,0:T(8,128)(2,1)S(1)}, u32[]{:S(2)}, u32[]{:S(2)}) collective-permute-start(bf16[256,512]{1,0:T(8,128)(2,1)S(1)} %get-tuple-element.33.refs_5_.refs_2_), channel_id=1, source_target_pairs={{0,1},{1,0},{2,3},{3,2},{4,5},{5,4},{6,7},{7,6},{8,9},{9,8},{10,11... | collective-permute-start | bytes 786440 | tf_op jit(solution)/shard_map/ppermute | solution.py:339
  20.7 1.5 %collective-permute-start.6 = (bf16[256,512]{1,0:T(8,128)(2,1)S(1)}, bf16[256,512]{1,0:T(8,128)(2,1)S(1)}, u32[]{:S(2)}, u32[]{:S(2)}) collective-permute-start(bf16[256,512]{1,0:T(8,128)(2,1)S(1)} %collective-permute-done.4.refs_9_.refs_6_), channel_id=1, source_target_pairs={{0,1},{1,0},{2,3},{3,2},{4,5},{5,4},{6,7},{7,6},{8,9},{9,8},{10,11... | collective-permute-start | bytes 786440 | tf_op jit(solution)/shard_map/ppermute | solution.py:339
  31.9 23.2 %copy-start.3 = (bf16[2048,256]{1,0:T(8,128)(2,1)S(1)}, bf16[2048,256]{1,0:T(8,128)(2,1)}, u32[]{:S(2)}) copy-start(bf16[2048,256]{1,0:T(8,128)(2,1)} %refs_9_.1) | copy-start | bytes 3145732
  31.9 6.8 %collective-permute-start.7 = (bf16[2,128,256]{2,1,0:T(8,128)(2,1)S(1)}, bf16[2,128,256]{2,1,0:T(8,128)(2,1)S(1)}, u32[]{:S(2)}, u32[]{:S(2)}) collective-permute-start(bf16[2,128,256]{2,1,0:T(8,128)(2,1)S(1)} %get-tuple-element.31), channel_id=1, source_target_pairs={{0,4},{4,8},{8,12},{12,16},{16,20},{20,24},{24,28},{1,5},{5,9},{9,... | collective-permute-start | bytes 393224 | tf_op jit(solution)/shard_map/ppermute | solution.py:411
  39.9 8.8 %collective-permute-start.8 = (bf16[2,128,256]{2,1,0:T(8,128)(2,1)S(1)}, bf16[2,128,256]{2,1,0:T(8,128)(2,1)S(1)}, u32[]{:S(2)}, u32[]{:S(2)}) collective-permute-start(bf16[2,128,256]{2,1,0:T(8,128)(2,1)S(1)} %get-tuple-element.49), channel_id=1, source_target_pairs={{0,8},{4,12},{8,16},{12,20},{16,24},{20,28},{1,9},{5,13},{9,17},{1... | collective-permute-start | bytes 393224 | tf_op jit(solution)/shard_map/ppermute | solution.py:411
  49.6 5.5 %copy-start.14 = (f32[128]{0:T(128)S(1)}, f32[128]{0:T(128)}, u32[]{:S(2)}) copy-start(f32[128]{0:T(128)} %param.24) | copy-start | bytes 1540
  49.6 9.5 %collective-permute-start.9 = (bf16[2,128,128]{2,1,0:T(8,128)(2,1)S(1)}, bf16[2,128,128]{2,1,0:T(8,128)(2,1)S(1)}, u32[]{:S(2)}, u32[]{:S(2)}) collective-permute-start(bf16[2,128,128]{2,1,0:T(8,128)(2,1)S(1)} %slice.15), channel_id=1, source_target_pairs={{0,16},{4,20},{8,24},{12,28},{1,17},{5,21},{9,25},{13,29},{2,18},{... | collective-permute-start | bytes 196616 | tf_op jit(solution)/shard_map/ppermute | solution.py:411
  56.3 1.6 %copy-start.6 = (f32[512,256]{1,0:T(8,128)S(1)}, f32[512,256]{1,0:T(8,128)}, u32[]{:S(2)}) copy-start(f32[512,256]{1,0:T(8,128)} %get-tuple-element.41.k_ref) | copy-start | bytes 1572868
  59.1 2.2 %copy-start.15 = (bf16[256,2048]{1,0:T(8,128)(2,1)S(1)}, bf16[256,2048]{1,0:T(8,128)(2,1)}, u32[]{:S(2)}) copy-start(bf16[256,2048]{1,0:T(8,128)(2,1)} %param.25) | copy-start | bytes 3145732
  59.7 8.0 %collective-permute-start.10 = (bf16[512,256]{1,0:T(8,128)(2,1)S(1)}, bf16[512,256]{1,0:T(8,128)(2,1)S(1)}, u32[]{:S(2)}, u32[]{:S(2)}) collective-permute-start(bf16[512,256]{1,0:T(8,128)(2,1)S(1)} %shard_map.132.refs_0_), channel_id=1, source_target_pairs={{0,2},{1,3},{2,0},{3,1},{4,6},{5,7},{6,4},{7,5},{8,10},{9,11},{10,... | collective-permute-start | bytes 786440 | tf_op jit(solution)/shard_map/ppermute | solution.py:339
  61.4 6.3 %collective-permute-start.15 = (bf16[256,512]{1,0:T(8,128)(2,1)S(1)}, bf16[256,512]{1,0:T(8,128)(2,1)S(1)}, u32[]{:S(2)}, u32[]{:S(2)}) collective-permute-start(bf16[256,512]{1,0:T(8,128)(2,1)S(1)} %get-tuple-element.56), channel_id=1, source_target_pairs={{0,1},{1,0},{2,3},{3,2},{4,5},{5,4},{6,7},{7,6},{8,9},{9,8},{10,11... | collective-permute-start | bytes 786440 | tf_op jit(solution)/shard_map/ppermute | solution.py:339
  61.5 6.2 %collective-permute-start.14 = (bf16[512,256]{1,0:T(8,128)(2,1)S(1)}, bf16[512,256]{1,0:T(8,128)(2,1)S(1)}, u32[]{:S(2)}, u32[]{:S(2)}) collective-permute-start(bf16[512,256]{1,0:T(8,128)(2,1)S(1)} %shard_map.132.refs_0_), channel_id=1, source_target_pairs={{0,1},{1,0},{2,3},{3,2},{4,5},{5,4},{6,7},{7,6},{8,9},{9,8},{10,11... | collective-permute-start | bytes 786440 | tf_op jit(solution)/shard_map/ppermute | solution.py:339
  62.0 11.3 %collective-permute-start.13 = (bf16[256,512]{1,0:T(8,128)(2,1)S(1)}, bf16[256,512]{1,0:T(8,128)(2,1)S(1)}, u32[]{:S(2)}, u32[]{:S(2)}) collective-permute-start(bf16[256,512]{1,0:T(8,128)(2,1)S(1)} %get-tuple-element.55), channel_id=1, source_target_pairs={{0,2},{1,3},{2,0},{3,1},{4,6},{5,7},{6,4},{7,5},{8,10},{9,11},{10,... | collective-permute-start | bytes 786440 | tf_op jit(solution)/shard_map/ppermute | solution.py:339
  62.5 13.9 %collective-permute-start.12 = (bf16[256,512]{1,0:T(8,128)(2,1)S(1)}, bf16[256,512]{1,0:T(8,128)(2,1)S(1)}, u32[]{:S(2)}, u32[]{:S(2)}) collective-permute-start(bf16[256,512]{1,0:T(8,128)(2,1)S(1)} %get-tuple-element.54), channel_id=1, source_target_pairs={{0,3},{1,2},{2,1},{3,0},{4,7},{5,6},{6,5},{7,4},{8,11},{9,10},{10,... | collective-permute-start | bytes 786440 | tf_op jit(solution)/shard_map/ppermute | solution.py:339
  67.7 8.7 %collective-permute-start.11 = (bf16[512,256]{1,0:T(8,128)(2,1)S(1)}, bf16[512,256]{1,0:T(8,128)(2,1)S(1)}, u32[]{:S(2)}, u32[]{:S(2)}) collective-permute-start(bf16[512,256]{1,0:T(8,128)(2,1)S(1)} %collective-permute-done.10.refs_0_), channel_id=1, source_target_pairs={{0,1},{1,0},{2,3},{3,2},{4,5},{5,4},{6,7},{7,6},{8,9},{9,8},{10,11... | collective-permute-start | bytes 786440 | tf_op jit(solution)/shard_map/ppermute | solution.py:339
  (8 other events, 8.3 us)

commit v4 on v3

--- a/solution.py
+++ b/solution.py
@@ -212,10 +212,6 @@
         transit = jnp.exp(last) * eye - moved[:, :dim]
         maps[b, h] = jnp.concatenate([transit, moved[:, dim:]], axis=1)
 
-    def compose(later, earlier):
-        out = mm_wide(split(later[:, :dim]), split(earlier))
-        return jnp.concatenate([out[:, :dim], out[:, dim:] + later[:, dim:]], axis=1)
-
     slabs = []
     for h in range(heads):
         spans = {(b, 1): maps[b, h] for b in range(blocks)}
@@ -226,7 +222,7 @@
                 while half * 2 < count:
                     half *= 2
                 spans[start, count] = compose(
-                    span(start + half, count - half), span(start, half)
+                    span(start + half, count - half), span(start, half), dim
                 )
             return spans[start, count]
 
@@ -286,48 +282,60 @@
         r_out[rows, cols] = reader
 
 
+def compose(later, earlier, dim):
+    out = mm_wide(split(later[:, :dim]), split(earlier))
+    return jnp.concatenate([out[:, :dim], out[:, dim:] + later[:, dim:]], axis=1)
+
+
+def own_kernel(in_ref, out_ref):
+    out_ref[...] = in_ref[...]
+
+
 def step_kernel(heads, dim, first, distance, pos_ref, got_ref, *refs):
     if first:
         own_ref, before_out, own_out, low_out = refs
     else:
         before_ref, own_ref, before_out, own_out, low_out = refs
-    valid = pos_ref[0] >= distance
+    partner_earlier = (pos_ref[0] & distance) != 0
     row = lax.broadcasted_iota(jnp.int32, (dim, 2 * dim), 0)
     col = lax.broadcasted_iota(jnp.int32, (dim, 2 * dim), 1)
     unchanged = jnp.where(row == col, 1.0, 0.0).astype(f32)
     for h in range(heads):
-        got = jnp.where(valid, got_ref[h].astype(f32), unchanged)
-        low = got.astype(bf16)
-        low = jnp.concatenate([low, low], axis=0)
-
-        def after(later):
-            hi, lo = split(later[:, :dim])
-            out = dot(jnp.concatenate([hi, lo], axis=1), low)
-            return jnp.concatenate([out[:, :dim], out[:, dim:] + later[:, dim:]], axis=1)
-
-        own = after(own_ref[h])
+        got = got_ref[h].astype(f32)
+        mine = own_ref[h]
+        own = compose(
+            jnp.where(partner_earlier, mine, got), jnp.where(partner_earlier, got, mine), dim
+        )
         own_out[h] = own
-        low_out[h] = own.astype(bf16)
-        before_out[h] = got if first else after(before_ref[h])
-
-
-def hidden_kernel(heads, dim, a_ref, r_ref, gate_ref, before_ref, got_ref, out_ref):
+        low_out[h] = own[:, dim - low_out.shape[2] + dim :].astype(bf16)
+        if first:
+            before_out[h] = jnp.where(partner_earlier, got, unchanged)
+        else:
+            before = before_ref[h]
+            before_out[h] = jnp.where(partner_earlier, compose(before, got, dim), before)
+
+
+def hidden_kernel(heads, dim, distance, pos_ref, a_ref, r_ref, gate_ref, before_ref, got_ref, *outs):
+    partner_earlier = (pos_ref[0] & distance) != 0
+    rows = a_ref.shape[0] // len(outs)
     for h in range(heads):
         cols = pl.ds(h * dim, dim)
         before = before_ref[h]
-        got = got_ref[h]
+        got = jnp.where(partner_earlier, got_ref[h].astype(f32), 0.0).astype(bf16)
         hi, lo = split(before[:, :dim])
         state = before[:, dim:] + dot(
             jnp.concatenate([hi, lo], axis=1), jnp.concatenate([got, got], axis=0)
         )
         out = a_ref[:, cols] + mm_square(split(r_ref[:, cols]), split(state))
         scaled = out * lax.rsqrt(jnp.mean(out * out, axis=-1, keepdims=True) + norm_floor)
-        out_ref[:, cols] = (scaled * gate_ref[:, cols]).astype(bf16)
-
-
-def output_kernel(count, has_sum, *refs):
+        result = (scaled * gate_ref[:, cols]).astype(bf16)
+        for c, out_ref in enumerate(outs):
+            out_ref[:, cols] = result[c * rows : (c + 1) * rows]
+
+
+def output_kernel(count, *refs):
     out_ref = refs[-1]
-    total = refs[2 * count][...] if has_sum else None
+    total = None
     for m in range(count):
         part = dot(refs[m][...], refs[count + m][...])
         total = part if total is None else total + part
@@ -468,45 +476,62 @@
         limit=16,
     )
 
+    def exchanged(value, distance):
+        pairs = [(s, s ^ distance) for s in range(slabs)]
+        return lax.ppermute(value, "seq", pairs)
+
     before = None
     distance = 1
     while 2 * distance < slabs:
-        got = shifted(slab_low, distance)
+        got = exchanged(slab_low, distance)
+        if before is None:
+            slab = vmem_call(own_kernel, shape(maps, f32), [slab], limit=8)
         operands = [pos_at, got] + ([] if before is None else [before]) + [slab]
+        sent = dim if 4 * distance >= slabs else 2 * dim
         before, slab, slab_low = vmem_call(
             functools.partial(step_kernel, heads, dim, before is None, distance),
-            (shape(maps, f32), shape(maps, f32), shape(maps, bf16)),
+            (shape(maps, f32), shape(maps, f32), shape((heads, dim, sent), bf16)),
             operands,
             scalars=1,
             limit=8,
         )
         distance *= 2
-    got = shifted(slab_low[:, :, dim:], distance)
+    got = exchanged(slab_low, distance)
     local, reader = vmem_call(
         functools.partial(read_kernel, heads, dim),
         (shape(rows, f32), shape(rows, f32)),
         [queries, keys, running, solved, prefix],
         limit=16,
     )
+    half = (tokens // 2, channels)
     hidden = vmem_call(
-        functools.partial(hidden_kernel, heads, dim),
-        shape(rows, bf16),
-        [local, reader, gates, before, got],
+        functools.partial(hidden_kernel, heads, dim, distance),
+        (shape(half, bf16), shape(half, bf16)),
+        [pos_at, local, reader, gates, before, got],
+        scalars=1,
         limit=8,
     )
-    pieces = gather_chunks([hidden], masks)
-    total = None
-    stages = [list(range(masks // 2))] + [[m] for m in range(masks // 2, masks)]
-    for i, stage in enumerate(stages):
-        last = i == len(stages) - 1
-        operands = [pieces[m][0] for m in stage] + [columns[m] for m in stage]
-        total = vmem_call(
-            functools.partial(output_kernel, len(stage), i > 0),
-            shape((tokens, width), bf16 if last else f32),
-            operands + ([total] if i > 0 else []),
-            limit=8,
-        )
-    return total
+    pieces = gather_chunks(hidden, masks)
+    result = None
+    whole = pl.BlockSpec(memory_space=pltpu.VMEM)
+    for c in reversed(range(2)):
+        operands = [p[c] for p in pieces] + columns
+        specs = [whole] * len(operands)
+        aliases = {}
+        if result is not None:
+            aliases = {len(operands): 0}
+            operands.append(result)
+            specs.append(pl.BlockSpec(memory_space=pl.ANY))
+        result = pl.pallas_call(
+            functools.partial(output_kernel, masks),
+            grid=(1,),
+            out_shape=shape((tokens, width), bf16),
+            in_specs=specs,
+            out_specs=pl.BlockSpec((tokens // 2, width), lambda i, c=c: (c, 0)),
+            input_output_aliases=aliases,
+            compiler_params=pltpu.CompilerParams(vmem_limit_bytes=8 * 2**20),
+        )(*operands)
+    return result
 
 
 def solution(mesh):

time: 78.2 us -> 64.7 us (0.83)
  waiting for transfers between devices: 30.6 us -> 23 us
  starting transfers between devices: 26.6 us -> 20.4 us
    ppermute x4 -> x1, starting transfers between devices: 20.4 us -> 4.89 us  [shifted(): return lax.ppermute(value, 'seq', pairs)]
    ppermute x0 -> x3, starting transfers between devices: none -> 7.61 us  [exchanged(): return lax.ppermute(value, 'seq', pairs)]
    ppermute x4 -> x1, waiting for transfers between devices: 5.88 us -> 0.35 us  [shifted(): return lax.ppermute(value, 'seq', pairs)]
    ppermute x12 -> x15, waiting for transfers between devices: 24.7 us -> 19.8 us  [xor_permute(): return lax.ppermute(value, 'head', [(i, i ^ mask) for i in range(count)])]
    ppermute x0 -> x3, waiting for transfers between devices: none -> 2.85 us  [exchanged(): return lax.ppermute(value, 'seq', pairs)]
    pallas_call x0 -> x2, Pallas kernels: none -> 2.28 us  [on_device(): pl.pallas_call(functools.partial(output_kernel, masks), grid=(1,), out_sh...]
    ppermute x12 -> x15, starting transfers between devices: 6.16 us -> 7.91 us  [xor_permute(): return lax.ppermute(value, 'head', [(i, i ^ mask) for i in range(count)])]
    pallas_call x9 -> x7, Pallas kernels: 13.9 us -> 12.3 us  [vmem_call(): pl.pallas_call(kernel, out_shape=out_shape, in_specs=specs, out_specs=out...]
  transfers between devices with their start and end apart: 16 -> 19, of which waited for: 9 -> 8; matrix products, arithmetic and copies ran while one was open for 2% -> 4% of each run, Pallas kernels for 4% -> 8%
where the time goes in v4:
time: 64.7 us; the launch traced here: 64.4 us
  waiting for transfers between devices  23 us (36%)
  starting transfers between devices  20.4 us (32%)
  Pallas kernels  14.6 us (23%)
  local copies, waits for them, and re-layouts  6.09 us (9%)
    ppermute x15, waiting for transfers between devices, xor_permute(): return lax.ppermute(value, 'head', [(i, i ^ mask) for i in range(count)])  19.8 us
    pallas_call x7, Pallas kernels, vmem_call(): pl.pallas_call(kernel, out_shape=out_shape, in_specs=specs, out_specs=out...  12.3 us
    ppermute x15, starting transfers between devices, xor_permute(): return lax.ppermute(value, 'head', [(i, i ^ mask) for i in range(count)])  7.91 us
    ppermute x3, starting transfers between devices, exchanged(): return lax.ppermute(value, 'seq', pairs)  7.61 us
    ppermute x1, starting transfers between devices, shifted(): return lax.ppermute(value, 'seq', pairs)  4.89 us
    unnamed x30, local copies, waits for them, and re-layouts  2.94 us
    ppermute x3, waiting for transfers between devices, exchanged(): return lax.ppermute(value, 'seq', pairs)  2.85 us
    pallas_call x2, Pallas kernels, on_device(): pl.pallas_call(functools.partial(output_kernel, masks), grid=(1,), out_sh...  2.28 us
  transfers between devices with their start and end apart: 19, of which 8 were waited for; matrix products, arithmetic and copies ran while one was open for 4% of the time, Pallas kernels for 8%

profile of v4, /device:TPU:0, one launch (start us, length us, event | category | flops | bytes accessed | tf_op | source)
XLA Modules:
  0.0 64.4 jit_solution(9229720342028707172)
XLA Ops:
  0.8 4.9 %collective-permute-start = (bf16[16,512]{1,0:T(8,128)(2,1)S(1)}, bf16[16,512]{1,0:T(8,128)(2,1)S(1)}, u32[]{:S(2)}, u32[]{:S(2)}) collective-permute-start(bf16[16,512]{1,0:T(8,128)(2,1)S(1)} %slice.9), channel_id=1, source_target_pairs={{0,4},{4,8},{8,12},{12,16},{16,20},{20,24},{24,28},{1,5},{5,9},{9,... | collective-permute-start | bytes 49160 | tf_op jit(solution)/shard_map/ppermute | solution.py:419
  5.7 1.1 %fusion = (bf16[256,512]{1,0:T(8,128)(2,1)S(1)}, bf16[256,512]{1,0:T(8,128)(2,1)S(1)}) fusion(bf16[512,512]{1,0:T(8,128)(2,1)} %param.13), kind=kLoop, calls=%fused_computation.5 | loop fusion | bytes 1048576 | tf_op jit(solution)/shard_map/slice | solution.py:425
  7.2 1.6 %collective-permute-start.3 = (bf16[272,512]{1,0:T(8,128)(2,1)S(1)}, bf16[272,512]{1,0:T(8,128)(2,1)S(1)}, u32[]{:S(2)}, u32[]{:S(2)}) collective-permute-start(bf16[272,512]{1,0:T(8,128)(2,1)S(1)} %pad_maximum_fusion.refs_4_.refs_1_), channel_id=1, source_target_pairs={{0,2},{1,3},{2,0},{3,1},{4,6},{5,7},{6,4},{7,5},{8,10},{9,11},{10,... | collective-permute-start | bytes 835592 | tf_op jit(solution)/shard_map/ppermute | solution.py:347
  9.3 7.5 %collective-permute-done.3.refs_8_.refs_5_ = bf16[272,512]{1,0:T(8,128)(2,1)S(1)} collective-permute-done((bf16[272,512]{1,0:T(8,128)(2,1)S(1)}, bf16[272,512]{1,0:T(8,128)(2,1)S(1)}, u32[]{:S(2)}, u32[]{:S(2)}) %collective-permute-start.3) | collective-permute-done | bytes 278560 | tf_op jit(solution)/shard_map/ppermute | solution.py:347
  17.3 3.4 %collective-permute-done.4.refs_9_.refs_6_ = bf16[256,512]{1,0:T(8,128)(2,1)S(1)} collective-permute-done((bf16[256,512]{1,0:T(8,128)(2,1)S(1)}, bf16[256,512]{1,0:T(8,128)(2,1)S(1)}, u32[]{:S(2)}, u32[]{:S(2)}) %collective-permute-start.4) | collective-permute-done | bytes 262176 | tf_op jit(solution)/shard_map/ppermute | solution.py:347
  20.7 1.5 %collective-permute-done.6.refs_11_.refs_8_ = bf16[256,512]{1,0:T(8,128)(2,1)S(1)} collective-permute-done((bf16[256,512]{1,0:T(8,128)(2,1)S(1)}, bf16[256,512]{1,0:T(8,128)(2,1)S(1)}, u32[]{:S(2)}, u32[]{:S(2)}) %collective-permute-start.6) | collective-permute-done | bytes 262176 | tf_op jit(solution)/shard_map/ppermute | solution.py:347
  22.9 1.2 %copy-done.1 = bf16[2048,256]{1,0:T(8,128)(2,1)S(1)} copy-done((bf16[2048,256]{1,0:T(8,128)(2,1)S(1)}, bf16[2048,256]{1,0:T(8,128)(2,1)}, u32[]{:S(2)}) %copy-start.1) | copy-done | bytes 1048600
  24.1 7.8 %shard_map.127 = (f32[512,256]{1,0:T(8,128)}, f32[8,128]{1,0:T(8,128)S(1)}, f32[8,128,256]{2,1,0:T(8,128)}, f32[6,128,256]{2,1,0:T(8,128)}, f32[2,128,256]{2,1,0:T(8,128)}, /*index=5*/bf16[2,128,256]{2,1,0:T(8,128)(2,1)S(1)}) custom-call(s32[1]{0:T(128)} %bitcast.1.refs_0_, f32[2]{0:T(128)S(1)} %copy-done.11, f32[2]{0:T(128)S(1)} %copy-done.12, ...), custom_call_target="tpu_custom_call" | custom-call | tf_op jit(solution)/shard_map/pallas_call | solution.py:380
  31.9 1.8 %collective-permute-start.7 = (bf16[2,128,256]{2,1,0:T(8,128)(2,1)S(1)}, bf16[2,128,256]{2,1,0:T(8,128)(2,1)S(1)}, u32[]{:S(2)}, u32[]{:S(2)}) collective-permute-start(bf16[2,128,256]{2,1,0:T(8,128)(2,1)S(1)} %get-tuple-element.33), channel_id=1, source_target_pairs={{0,4},{4,0},{8,12},{12,8},{16,20},{20,16},{24,28},{28,24},{1,5},{5... | collective-permute-start | bytes 393224 | tf_op jit(solution)/shard_map/ppermute | solution.py:481
  33.7 0.9 %copy-done.7 = f32[2,128,256]{2,1,0:T(8,128)S(1)} copy-done((f32[2,128,256]{2,1,0:T(8,128)S(1)}, f32[2,128,256]{2,1,0:T(8,128)}, u32[]{:S(2)}) %copy-start.7) | copy-done | bytes 262168
  34.7 2.8 %collective-permute-done.7.got_ref = bf16[2,128,256]{2,1,0:T(8,128)(2,1)S(1)} collective-permute-done((bf16[2,128,256]{2,1,0:T(8,128)(2,1)S(1)}, bf16[2,128,256]{2,1,0:T(8,128)(2,1)S(1)}, u32[]{:S(2)}, u32[]{:S(2)}) %collective-permute-start.7) | collective-permute-done | bytes 131104 | tf_op jit(solution)/shard_map/ppermute | solution.py:481
  37.8 2.8 %collective-permute-start.8 = (bf16[2,128,256]{2,1,0:T(8,128)(2,1)S(1)}, bf16[2,128,256]{2,1,0:T(8,128)(2,1)S(1)}, u32[]{:S(2)}, u32[]{:S(2)}) collective-permute-start(bf16[2,128,256]{2,1,0:T(8,128)(2,1)S(1)} %get-tuple-element.51), channel_id=1, source_target_pairs={{0,8},{4,12},{8,0},{12,4},{16,24},{20,28},{24,16},{28,20},{1,9},{5... | collective-permute-start | bytes 393224 | tf_op jit(solution)/shard_map/ppermute | solution.py:481
  40.6 1.3 %constant_dynamic-slice_fusion = (bf16[256,512]{1,0:T(8,128)(2,1)S(1)}, bf16[256,512]{1,0:T(8,128)(2,1)S(1)}, bf16[256,512]{1,0:T(8,128)(2,1)S(1)}, bf16[256,512]{1,0:T(8,128)(2,1)S(1)}) fusion(bf16[256,2048]{1,0:T(8,128)(2,1)} %param.25, s32[]{:T(128)S(6)} %select_n.15, s32[]{:T(128)S(6)} %select_n.13, s32[]{:T(128)S(6)} %select_n.12, s32[]{:T(128)S(6)} %select_n.14), kind=kLoop, calls=%fused_computation.1 | loop fusion | bytes 2097168 | tf_op jit(solution)/shard_map/dynamic_slice | solution.py:461
  41.9 1.6 %collective-permute-start.14 = (bf16[256,512]{1,0:T(8,128)(2,1)S(1)}, bf16[256,512]{1,0:T(8,128)(2,1)S(1)}, u32[]{:S(2)}, u32[]{:S(2)}) collective-permute-start(bf16[256,512]{1,0:T(8,128)(2,1)S(1)} %get-tuple-element.58), channel_id=1, source_target_pairs={{0,2},{1,3},{2,0},{3,1},{4,6},{5,7},{6,4},{7,5},{8,10},{9,11},{10,... | collective-permute-start | bytes 786440 | tf_op jit(solution)/shard_map/ppermute | solution.py:347
  43.5 1.0 %shard_map.132 = (f32[2,128,256]{2,1,0:T(8,128)S(1)}, f32[2,128,256]{2,1,0:T(8,128)}, bf16[2,128,128]{2,1,0:T(8,128)(2,1)S(1)}) custom-call(s32[1]{0:T(128)} %bitcast.pos_ref, bf16[2,128,256]{2,1,0:T(8,128)(2,1)S(1)} %collective-permute-done.8.got_ref, f32[2,128,256]{2,1,0:T(8,128)S(1)} %get-tuple-element.52.refs_0_, ...), custom_call_target="tpu_custom_call" | custom-call | tf_op jit(solution)/shard_map/pallas_call | solution.py:380
  44.5 3.0 %collective-permute-start.9 = (bf16[2,128,128]{2,1,0:T(8,128)(2,1)S(1)}, bf16[2,128,128]{2,1,0:T(8,128)(2,1)S(1)}, u32[]{:S(2)}, u32[]{:S(2)}) collective-permute-start(bf16[2,128,128]{2,1,0:T(8,128)(2,1)S(1)} %get-tuple-element.55), channel_id=1, source_target_pairs={{0,16},{4,20},{8,24},{12,28},{16,0},{20,4},{24,8},{28,12},{1,17},{... | collective-permute-start | bytes 196616 | tf_op jit(solution)/shard_map/ppermute | solution.py:481
  47.6 1.5 %shard_map.128 = (f32[512,256]{1,0:T(8,128)S(1)}, f32[512,256]{1,0:T(8,128)S(1)}) custom-call(s32[1]{0:T(128)} %bitcast.1.refs_0_, bf16[272,512]{1,0:T(8,128)(2,1)S(1)} %pad_maximum_fusion.refs_4_.refs_1_, bf16[256,512]{1,0:T(8,128)(2,1)S(1)} %get-tuple-element.35.refs_5_.refs_2_, bf16[272,512]{1,0:T(8,128)(2,1)S(1)} %collective-permute-done.1.refs_6_.refs_3_, ...), custom_call_target="tpu_custom_call" | custom-call | tf_op jit(solution)/shard_map/pallas_call | solution.py:380
  49.2 1.2 %shard_map.129 = (f32[512,256]{1,0:T(8,128)S(1)}, f32[512,256]{1,0:T(8,128)S(1)}) custom-call(f32[512,256]{1,0:T(8,128)S(1)} %get-tuple-element.42.q_ref, f32[512,256]{1,0:T(8,128)S(1)} %copy-done.6, f32[8,128]{1,0:T(8,128)S(1)} %get-tuple-element.44.run_ref, f32[8,128,256]{2,1,0:T(8,128)S(1)} %copy-done.2, f32[6,128,256]{2,1,0:T(8,128)S(1)} %copy-done.5), custom_call_target="tpu_custom_call" | custom-call | tf_op jit(solution)/shard_map/pallas_call | solution.py:380
  51.0 1.6 %collective-permute-start.17 = (bf16[256,256]{1,0:T(8,128)(2,1)S(1)}, bf16[256,256]{1,0:T(8,128)(2,1)S(1)}, u32[]{:S(2)}, u32[]{:S(2)}) collective-permute-start(bf16[256,256]{1,0:T(8,128)(2,1)S(1)} %get-tuple-element.60.refs_0_), channel_id=1, source_target_pairs={{0,2},{1,3},{2,0},{3,1},{4,6},{5,7},{6,4},{7,5},{8,10},{9,11},{10,... | collective-permute-start | bytes 393224 | tf_op jit(solution)/shard_map/ppermute | solution.py:347
  53.1 1.0 %collective-permute-start.16 = (bf16[256,256]{1,0:T(8,128)(2,1)S(1)}, bf16[256,256]{1,0:T(8,128)(2,1)S(1)}, u32[]{:S(2)}, u32[]{:S(2)}) collective-permute-start(bf16[256,256]{1,0:T(8,128)(2,1)S(1)} %get-tuple-element.60.refs_0_), channel_id=1, source_target_pairs={{0,1},{1,0},{2,3},{3,2},{4,5},{5,4},{6,7},{7,6},{8,9},{9,8},{10,11... | collective-permute-start | bytes 393224 | tf_op jit(solution)/shard_map/ppermute | solution.py:347
  54.1 5.0 %collective-permute-done.17.refs_2_ = bf16[256,256]{1,0:T(8,128)(2,1)S(1)} collective-permute-done((bf16[256,256]{1,0:T(8,128)(2,1)S(1)}, bf16[256,256]{1,0:T(8,128)(2,1)S(1)}, u32[]{:S(2)}, u32[]{:S(2)}) %collective-permute-start.17) | collective-permute-done | bytes 131104 | tf_op jit(solution)/shard_map/ppermute | solution.py:347
  59.7 2.2 %collective-permute-done.11.refs_2_ = bf16[256,256]{1,0:T(8,128)(2,1)S(1)} collective-permute-done((bf16[256,256]{1,0:T(8,128)(2,1)S(1)}, bf16[256,256]{1,0:T(8,128)(2,1)S(1)}, u32[]{:S(2)}, u32[]{:S(2)}) %collective-permute-start.11) | collective-permute-done | bytes 131104 | tf_op jit(solution)/shard_map/ppermute | solution.py:347
  61.9 1.1 %shard_map.134.refs_8_ = bf16[512,512]{1,0:T(8,128)(2,1)} custom-call(bf16[256,256]{1,0:T(8,128)(2,1)S(1)} %get-tuple-element.60.refs_0_, bf16[256,256]{1,0:T(8,128)(2,1)S(1)} %collective-permute-done.16.refs_1_, bf16[256,256]{1,0:T(8,128)(2,1)S(1)} %collective-permute-done.17.refs_2_, bf16[256,256]{1,0:T(8,128)(2,1)S(1)} %collective-permute-done.18.refs_3_, ...), custom_call_target="tpu_custom_call" | custom-call | tf_op jit(solution)/shard_map/pallas_call | solution.py:525
  63.2 1.1 %shard_map.135 = bf16[512,512]{1,0:T(8,128)(2,1)} custom-call(bf16[256,256]{1,0:T(8,128)(2,1)S(1)} %get-tuple-element.56.refs_0_, bf16[256,256]{1,0:T(8,128)(2,1)S(1)} %collective-permute-done.10.refs_1_, bf16[256,256]{1,0:T(8,128)(2,1)S(1)} %collective-permute-done.11.refs_2_, ...), custom_call_target="tpu_custom_call", output_to_operand_aliasing={{}: (8, {})} | custom-call | tf_op jit(solution)/shard_map/pallas_call | solution.py:525
  (57 shorter events, 5.2 us)
Async XLA Ops:
  0.0 22.2 %copy-start = (bf16[2048,256]{1,0:T(8,128)(2,1)S(1)}, bf16[2048,256]{1,0:T(8,128)(2,1)}, u32[]{:S(2)}) copy-start(bf16[2048,256]{1,0:T(8,128)(2,1)} %refs_12_.1) | copy-start | bytes 3145732
  0.8 6.3 %collective-permute-start = (bf16[16,512]{1,0:T(8,128)(2,1)S(1)}, bf16[16,512]{1,0:T(8,128)(2,1)S(1)}, u32[]{:S(2)}, u32[]{:S(2)}) collective-permute-start(bf16[16,512]{1,0:T(8,128)(2,1)S(1)} %slice.9), channel_id=1, source_target_pairs={{0,4},{4,8},{8,12},{12,16},{16,20},{20,24},{24,28},{1,5},{5,9},{9,... | collective-permute-start | bytes 49160 | tf_op jit(solution)/shard_map/ppermute | solution.py:419
  7.1 15.1 %copy-start.9 = (bf16[2048,2]{0,1:T(2,128)(2,1)S(1)}, bf16[2048,2]{0,1:T(2,128)(2,1)}, u32[]{:S(2)}) copy-start(bf16[2048,2]{0,1:T(2,128)(2,1)} %param.18) | copy-start | bytes 24580
  7.1 15.1 %copy-start.10 = (bf16[2048,2]{0,1:T(2,128)(2,1)S(1)}, bf16[2048,2]{0,1:T(2,128)(2,1)}, u32[]{:S(2)}) copy-start(bf16[2048,2]{0,1:T(2,128)(2,1)} %param.19) | copy-start | bytes 24580
  7.2 15.1 %copy-start.8 = (f32[4,3,256]{2,0,1:T(4,128)S(1)}, f32[4,3,256]{2,0,1:T(4,128)}, u32[]{:S(2)}) copy-start(f32[4,3,256]{2,0,1:T(4,128)} %param.20) | copy-start | bytes 36868
  7.2 9.6 %collective-permute-start.3 = (bf16[272,512]{1,0:T(8,128)(2,1)S(1)}, bf16[272,512]{1,0:T(8,128)(2,1)S(1)}, u32[]{:S(2)}, u32[]{:S(2)}) collective-permute-start(bf16[272,512]{1,0:T(8,128)(2,1)S(1)} %pad_maximum_fusion.refs_4_.refs_1_), channel_id=1, source_target_pairs={{0,2},{1,3},{2,0},{3,1},{4,6},{5,7},{6,4},{7,5},{8,10},{9,11},{10,... | collective-permute-start | bytes 835592 | tf_op jit(solution)/shard_map/ppermute | solution.py:347
  8.7 11.9 %collective-permute-start.4 = (bf16[256,512]{1,0:T(8,128)(2,1)S(1)}, bf16[256,512]{1,0:T(8,128)(2,1)S(1)}, u32[]{:S(2)}, u32[]{:S(2)}) collective-permute-start(bf16[256,512]{1,0:T(8,128)(2,1)S(1)} %get-tuple-element.35.refs_5_.refs_2_), channel_id=1, source_target_pairs={{0,2},{1,3},{2,0},{3,1},{4,6},{5,7},{6,4},{7,5},{8,10},{9,11},{10,... | collective-permute-start | bytes 786440 | tf_op jit(solution)/shard_map/ppermute | solution.py:347
  9.3 11.4 %collective-permute-start.1 = (bf16[272,512]{1,0:T(8,128)(2,1)S(1)}, bf16[272,512]{1,0:T(8,128)(2,1)S(1)}, u32[]{:S(2)}, u32[]{:S(2)}) collective-permute-start(bf16[272,512]{1,0:T(8,128)(2,1)S(1)} %pad_maximum_fusion.refs_4_.refs_1_), channel_id=1, source_target_pairs={{0,1},{1,0},{2,3},{3,2},{4,5},{5,4},{6,7},{7,6},{8,9},{9,8},{10,11... | collective-permute-start | bytes 835592 | tf_op jit(solution)/shard_map/ppermute | solution.py:347
  16.8 5.4 %collective-permute-start.5 = (bf16[272,512]{1,0:T(8,128)(2,1)S(1)}, bf16[272,512]{1,0:T(8,128)(2,1)S(1)}, u32[]{:S(2)}, u32[]{:S(2)}) collective-permute-start(bf16[272,512]{1,0:T(8,128)(2,1)S(1)} %collective-permute-done.3.refs_8_.refs_5_), channel_id=1, source_target_pairs={{0,1},{1,0},{2,3},{3,2},{4,5},{5,4},{6,7},{7,6},{8,9},{9,8},{10,11... | collective-permute-start | bytes 835592 | tf_op jit(solution)/shard_map/ppermute | solution.py:347
  16.8 3.9 %collective-permute-start.2 = (bf16[256,512]{1,0:T(8,128)(2,1)S(1)}, bf16[256,512]{1,0:T(8,128)(2,1)S(1)}, u32[]{:S(2)}, u32[]{:S(2)}) collective-permute-start(bf16[256,512]{1,0:T(8,128)(2,1)S(1)} %get-tuple-element.35.refs_5_.refs_2_), channel_id=1, source_target_pairs={{0,1},{1,0},{2,3},{3,2},{4,5},{5,4},{6,7},{7,6},{8,9},{9,8},{10,11... | collective-permute-start | bytes 786440 | tf_op jit(solution)/shard_map/ppermute | solution.py:347
  20.7 1.5 %collective-permute-start.6 = (bf16[256,512]{1,0:T(8,128)(2,1)S(1)}, bf16[256,512]{1,0:T(8,128)(2,1)S(1)}, u32[]{:S(2)}, u32[]{:S(2)}) collective-permute-start(bf16[256,512]{1,0:T(8,128)(2,1)S(1)} %collective-permute-done.4.refs_9_.refs_6_), channel_id=1, source_target_pairs={{0,1},{1,0},{2,3},{3,2},{4,5},{5,4},{6,7},{7,6},{8,9},{9,8},{10,11... | collective-permute-start | bytes 786440 | tf_op jit(solution)/shard_map/ppermute | solution.py:347
  31.9 5.6 %collective-permute-start.7 = (bf16[2,128,256]{2,1,0:T(8,128)(2,1)S(1)}, bf16[2,128,256]{2,1,0:T(8,128)(2,1)S(1)}, u32[]{:S(2)}, u32[]{:S(2)}) collective-permute-start(bf16[2,128,256]{2,1,0:T(8,128)(2,1)S(1)} %get-tuple-element.33), channel_id=1, source_target_pairs={{0,4},{4,0},{8,12},{12,8},{16,20},{20,16},{24,28},{28,24},{1,5},{5... | collective-permute-start | bytes 393224 | tf_op jit(solution)/shard_map/ppermute | solution.py:481
  37.8 9.8 %copy-start.3 = (bf16[2048,256]{1,0:T(8,128)(2,1)S(1)}, bf16[2048,256]{1,0:T(8,128)(2,1)}, u32[]{:S(2)}) copy-start(bf16[2048,256]{1,0:T(8,128)(2,1)} %refs_9_.1) | copy-start | bytes 3145732
  37.8 5.7 %collective-permute-start.8 = (bf16[2,128,256]{2,1,0:T(8,128)(2,1)S(1)}, bf16[2,128,256]{2,1,0:T(8,128)(2,1)S(1)}, u32[]{:S(2)}, u32[]{:S(2)}) collective-permute-start(bf16[2,128,256]{2,1,0:T(8,128)(2,1)S(1)} %get-tuple-element.51), channel_id=1, source_target_pairs={{0,8},{4,12},{8,0},{12,4},{16,24},{20,28},{24,16},{28,20},{1,9},{5... | collective-permute-start | bytes 393224 | tf_op jit(solution)/shard_map/ppermute | solution.py:481
  41.9 11.2 %collective-permute-start.13 = (bf16[256,512]{1,0:T(8,128)(2,1)S(1)}, bf16[256,512]{1,0:T(8,128)(2,1)S(1)}, u32[]{:S(2)}, u32[]{:S(2)}) collective-permute-start(bf16[256,512]{1,0:T(8,128)(2,1)S(1)} %get-tuple-element.57), channel_id=1, source_target_pairs={{0,1},{1,0},{2,3},{3,2},{4,5},{5,4},{6,7},{7,6},{8,9},{9,8},{10,11... | collective-permute-start | bytes 786440 | tf_op jit(solution)/shard_map/ppermute | solution.py:347
  41.9 17.2 %collective-permute-start.14 = (bf16[256,512]{1,0:T(8,128)(2,1)S(1)}, bf16[256,512]{1,0:T(8,128)(2,1)S(1)}, u32[]{:S(2)}, u32[]{:S(2)}) collective-permute-start(bf16[256,512]{1,0:T(8,128)(2,1)S(1)} %get-tuple-element.58), channel_id=1, source_target_pairs={{0,2},{1,3},{2,0},{3,1},{4,6},{5,7},{6,4},{7,5},{8,10},{9,11},{10,... | collective-permute-start | bytes 786440 | tf_op jit(solution)/shard_map/ppermute | solution.py:347
  44.5 5.8 %collective-permute-start.9 = (bf16[2,128,128]{2,1,0:T(8,128)(2,1)S(1)}, bf16[2,128,128]{2,1,0:T(8,128)(2,1)S(1)}, u32[]{:S(2)}, u32[]{:S(2)}) collective-permute-start(bf16[2,128,128]{2,1,0:T(8,128)(2,1)S(1)} %get-tuple-element.55), channel_id=1, source_target_pairs={{0,16},{4,20},{8,24},{12,28},{16,0},{20,4},{24,8},{28,12},{1,17},{... | collective-permute-start | bytes 196616 | tf_op jit(solution)/shard_map/ppermute | solution.py:481
  47.6 14.3 %collective-permute-start.15 = (bf16[256,512]{1,0:T(8,128)(2,1)S(1)}, bf16[256,512]{1,0:T(8,128)(2,1)S(1)}, u32[]{:S(2)}, u32[]{:S(2)}) collective-permute-start(bf16[256,512]{1,0:T(8,128)(2,1)S(1)} %get-tuple-element.59), channel_id=1, source_target_pairs={{0,3},{1,2},{2,1},{3,0},{4,7},{5,6},{6,5},{7,4},{8,11},{9,10},{10,... | collective-permute-start | bytes 786440 | tf_op jit(solution)/shard_map/ppermute | solution.py:347
  51.0 8.2 %collective-permute-start.17 = (bf16[256,256]{1,0:T(8,128)(2,1)S(1)}, bf16[256,256]{1,0:T(8,128)(2,1)S(1)}, u32[]{:S(2)}, u32[]{:S(2)}) collective-permute-start(bf16[256,256]{1,0:T(8,128)(2,1)S(1)} %get-tuple-element.60.refs_0_), channel_id=1, source_target_pairs={{0,2},{1,3},{2,0},{3,1},{4,6},{5,7},{6,4},{7,5},{8,10},{9,11},{10,... | collective-permute-start | bytes 393224 | tf_op jit(solution)/shard_map/ppermute | solution.py:347
  52.5 9.4 %collective-permute-start.11 = (bf16[256,256]{1,0:T(8,128)(2,1)S(1)}, bf16[256,256]{1,0:T(8,128)(2,1)S(1)}, u32[]{:S(2)}, u32[]{:S(2)}) collective-permute-start(bf16[256,256]{1,0:T(8,128)(2,1)S(1)} %get-tuple-element.56.refs_0_), channel_id=1, source_target_pairs={{0,2},{1,3},{2,0},{3,1},{4,6},{5,7},{6,4},{7,5},{8,10},{9,11},{10,... | collective-permute-start | bytes 393224 | tf_op jit(solution)/shard_map/ppermute | solution.py:347
  53.1 8.9 %collective-permute-start.16 = (bf16[256,256]{1,0:T(8,128)(2,1)S(1)}, bf16[256,256]{1,0:T(8,128)(2,1)S(1)}, u32[]{:S(2)}, u32[]{:S(2)}) collective-permute-start(bf16[256,256]{1,0:T(8,128)(2,1)S(1)} %get-tuple-element.60.refs_0_), channel_id=1, source_target_pairs={{0,1},{1,0},{2,3},{3,2},{4,5},{5,4},{6,7},{7,6},{8,9},{9,8},{10,11... | collective-permute-start | bytes 393224 | tf_op jit(solution)/shard_map/ppermute | solution.py:347
  59.1 2.8 %collective-permute-start.18 = (bf16[256,256]{1,0:T(8,128)(2,1)S(1)}, bf16[256,256]{1,0:T(8,128)(2,1)S(1)}, u32[]{:S(2)}, u32[]{:S(2)}) collective-permute-start(bf16[256,256]{1,0:T(8,128)(2,1)S(1)} %collective-permute-done.17.refs_2_), channel_id=1, source_target_pairs={{0,1},{1,0},{2,3},{3,2},{4,5},{5,4},{6,7},{7,6},{8,9},{9,8},{10,11... | collective-permute-start | bytes 393224 | tf_op jit(solution)/shard_map/ppermute | solution.py:347
  59.2 3.9 %collective-permute-start.10 = (bf16[256,256]{1,0:T(8,128)(2,1)S(1)}, bf16[256,256]{1,0:T(8,128)(2,1)S(1)}, u32[]{:S(2)}, u32[]{:S(2)}) collective-permute-start(bf16[256,256]{1,0:T(8,128)(2,1)S(1)} %get-tuple-element.56.refs_0_), channel_id=1, source_target_pairs={{0,1},{1,0},{2,3},{3,2},{4,5},{5,4},{6,7},{7,6},{8,9},{9,8},{10,11... | collective-permute-start | bytes 393224 | tf_op jit(solution)/shard_map/ppermute | solution.py:347
  61.9 1.3 %collective-permute-start.12 = (bf16[256,256]{1,0:T(8,128)(2,1)S(1)}, bf16[256,256]{1,0:T(8,128)(2,1)S(1)}, u32[]{:S(2)}, u32[]{:S(2)}) collective-permute-start(bf16[256,256]{1,0:T(8,128)(2,1)S(1)} %collective-permute-done.11.refs_2_), channel_id=1, source_target_pairs={{0,1},{1,0},{2,3},{3,2},{4,5},{5,4},{6,7},{7,6},{8,9},{9,8},{10,11... | collective-permute-start | bytes 393224 | tf_op jit(solution)/shard_map/ppermute | solution.py:347
  (10 other events, 21.6 us)
